TPU v7x, 32 devices: a whole 2x2x4 slice. The times are simulated.
32 devices in a mesh: ctx: 4 (over y, x), fsdp: 8 (over z, core).
Axes of the slice: x: 2, y: 2, z: 4, core: 2. Of those that a mesh axis runs over, the one named last changes fastest.
Arguments:
- queries: bfloat16 [512, 3072], P('ctx', 'fsdp'), may hold values from -200 to 200, as said below
- keys: bfloat16 [512, 3072], P('ctx', 'fsdp'), may hold values from -200 to 200, as said below
- values: bfloat16 [512, 3072], P('ctx', 'fsdp'), may hold values from -6 to 6
- query_tangent: bfloat16 [512, 3072], P('ctx', 'fsdp'), may hold values from -6 to 6
- key_tangent: bfloat16 [512, 3072], P('ctx', 'fsdp'), may hold values from -6 to 6
- value_tangent: bfloat16 [512, 3072], P('ctx', 'fsdp'), may hold values from -6 to 6
- query_gain: float32 [3072], P('fsdp'), may hold values from 0.5 to 1.5
- key_gain: float32 [3072], P('fsdp'), may hold values from 0.5 to 1.5
- time_index: int32 [1], replicated, may hold values from 0 to 999
- shard_order: int32 [4], P('ctx'), may hold values from 0 to 3, each once
Outputs:
- query_grad: bfloat16 [512, 3072], P('ctx', 'fsdp')
- key_grad: bfloat16 [512, 3072], P('ctx', 'fsdp')
- value_grad: bfloat16 [512, 3072], P('ctx', 'fsdp')
- query_gain_grad: float32 [3072], P('fsdp')
- key_gain_grad: float32 [3072], P('fsdp')
Inputs may be any that keep to these rules, and one draw needn't show every extreme that they name: `queries`: each sample's channels hold 24 heads of 128 channels in order. `keys`: laid out as the queries. `shard_order`: each block index appears once.
All inputs are finite; a program needn't handle non-finite values.
Results may differ from a plain program's by a relative error of at most 0.024.
Values may be sent and summed in bfloat16 or wider, within the bound.
No kernel may reach another device: no remote copies, remote signals or barrier semaphores. Data moves between devices by JAX's collectives and lax.ppermute only.
A program may use at most 64 MiB of HBM per device.

v0:
```python
import math

import jax
import jax.numpy as jnp
from jax import lax
from jax.sharding import PartitionSpec as P

HD = 128
HEAD_SPLIT = 8
STEPS = 1000
CHANNELS = 3072


eps_norm = 1e-06
loss_scale = 256.0
rope_base = 10000.0
floor_term = 0.1


def from_behind(block, axis, distance):
    devices = range(lax.axis_size(axis))
    route = [((i - distance) % len(devices), i) for i in devices]
    return lax.ppermute(block, axis, route)


def group_sum(pieces):
    slot_count = lax.axis_size("fsdp") // HEAD_SPLIT
    sample_id = lax.axis_index("fsdp") // HEAD_SPLIT
    onehot = (jnp.arange(slot_count, dtype=jnp.int32) == sample_id).astype(jnp.float32)
    placed = tuple((onehot[:, None] * piece[None, :] for piece in pieces))
    summed = lax.psum(placed, "fsdp")
    return tuple((jnp.sum(onehot[:, None] * whole, axis=0) for whole in summed))


def rotate(field, cos_table, sin_table, turn_sign):
    half_width = field.shape[-1] // 2
    first_half = field[..., :half_width]
    second_half = field[..., half_width:]
    return jnp.concatenate(
        [
            first_half * cos_table - turn_sign * second_half * sin_table,
            turn_sign * first_half * sin_table + second_half * cos_table,
        ],
        axis=-1,
    )


def attend(carry, query_n, query_nt, pieces, head_count):
    key_blk, value_blk, ktan_blk, vtan_blk = tuple(
        (piece.reshape(piece.shape[0], head_count, HD) for piece in pieces)
    )
    peak, totals, numer, numer_tan, tilt = carry
    inv_root = HD ** (-0.5)
    scores = (
        jnp.einsum("thd,khd->thk", query_n, key_blk, preferred_element_type=jnp.float32) * inv_root
    )
    slopes = (
        jnp.einsum("thd,khd->thk", query_nt, key_blk, preferred_element_type=jnp.float32)
        + jnp.einsum("thd,khd->thk", query_n, ktan_blk, preferred_element_type=jnp.float32)
    ) * inv_root
    new_peak = jnp.maximum(peak, jnp.max(scores, axis=-1))
    shrink = jnp.exp(peak - new_peak)
    weights = jnp.exp(scores - new_peak[..., None])
    tilted = weights * slopes
    weights_b = weights.astype(jnp.bfloat16)
    tilted_b = tilted.astype(jnp.bfloat16)
    totals = totals * shrink + jnp.sum(weights, axis=-1)
    numer = numer * shrink[..., None] + jnp.einsum(
        "thk,khd->thd", weights_b, value_blk, preferred_element_type=jnp.float32
    )
    numer_tan = (
        numer_tan * shrink[..., None]
        + jnp.einsum("thk,khd->thd", weights_b, vtan_blk, preferred_element_type=jnp.float32)
        + jnp.einsum("thk,khd->thd", tilted_b, value_blk, preferred_element_type=jnp.float32)
    )
    tilt = tilt * shrink + jnp.sum(tilted, axis=-1)
    return (new_peak, totals, numer, numer_tan, tilt)


def gradients(query_n, cotangent, logsum, drift, key_blk, value_blk):
    inv_root = HD ** (-0.5)
    scores = (
        jnp.einsum("thd,khd->thk", query_n, key_blk, preferred_element_type=jnp.float32) * inv_root
    )
    probs = jnp.exp(scores - logsum[..., None])
    probs_b = probs.astype(jnp.bfloat16)
    dvalue = jnp.einsum("thk,thd->khd", probs_b, cotangent, preferred_element_type=jnp.float32)
    dprobs = jnp.einsum("thd,khd->thk", cotangent, value_blk, preferred_element_type=jnp.float32)
    dscore = (probs * (dprobs - drift[..., None]) * inv_root).astype(jnp.bfloat16)
    dquery = jnp.einsum("thk,khd->thd", dscore, key_blk, preferred_element_type=jnp.float32)
    dkey = jnp.einsum("thk,thd->khd", dscore, query_n, preferred_element_type=jnp.float32)
    return (dquery, dkey, dvalue)


def per_device(
    queries,
    keys,
    values,
    query_tangent,
    key_tangent,
    value_tangent,
    query_gain,
    key_gain,
    time_index,
    shard_order,
):
    tok_rows = queries.shape[0]
    ch_dev = queries.shape[1]
    head_count = ch_dev // HD
    rank_in = lax.axis_index("fsdp") % HEAD_SPLIT
    sample_id = lax.axis_index("fsdp") // HEAD_SPLIT
    gains_all = (
        lax.all_gather(query_gain, "fsdp", axis=0, tiled=True),
        lax.all_gather(key_gain, "fsdp", axis=0, tiled=True),
    )
    query_gvec = lax.dynamic_slice_in_dim(gains_all[0], rank_in * ch_dev, ch_dev, 0)
    key_gvec = lax.dynamic_slice_in_dim(gains_all[1], rank_in * ch_dev, ch_dev, 0)
    places = (shard_order[0] * tok_rows + jnp.arange(tok_rows, dtype=jnp.int32)).astype(jnp.float32)
    freqs = rope_base ** (-jnp.arange(HD // 2, dtype=jnp.float32) / (HD // 2))
    angles = places[:, None] * freqs[None, :]
    cos_table = jnp.cos(angles)[:, None, :]
    sin_table = jnp.sin(angles)[:, None, :]
    query_x = queries.astype(jnp.float32)
    key_x = keys.astype(jnp.float32)
    query_dx = query_tangent.astype(jnp.float32)
    key_dx = key_tangent.astype(jnp.float32)
    stats = group_sum(
        (
            jnp.sum(query_x * query_x, axis=1),
            jnp.sum(key_x * key_x, axis=1),
            jnp.sum(query_x * query_dx, axis=1),
            jnp.sum(key_x * key_dx, axis=1),
        )
    )
    query_r = lax.rsqrt(stats[0] / CHANNELS + eps_norm)[:, None]
    key_r = lax.rsqrt(stats[1] / CHANNELS + eps_norm)[:, None]
    query_y = query_x * query_r * query_gvec
    key_y = key_x * key_r * key_gvec
    query_yt = (
        query_dx * query_r - query_x * query_r**3 * (stats[2] / CHANNELS)[:, None]
    ) * query_gvec
    key_yt = (key_dx * key_r - key_x * key_r**3 * (stats[3] / CHANNELS)[:, None]) * key_gvec

    def rotated(field):
        return rotate(field.reshape(tok_rows, head_count, HD), cos_table, sin_table, 1.0).astype(
            jnp.bfloat16
        )

    query_n = rotated(query_y)
    query_nt = rotated(query_yt)
    key_flat = rotated(key_y).reshape(tok_rows, ch_dev)
    ktan_flat = rotated(key_yt).reshape(tok_rows, ch_dev)
    zero_rows = jnp.zeros((tok_rows, head_count), jnp.float32)
    zero_field = jnp.zeros((tok_rows, head_count, HD), jnp.float32)
    init_state = (
        jnp.full((tok_rows, head_count), -1e30, jnp.float32),
        zero_rows,
        zero_field,
        zero_field,
        zero_rows,
    )
    gathered = (
        lax.all_gather(key_flat, "ctx", axis=0, tiled=True),
        lax.all_gather(values, "ctx", axis=0, tiled=True),
        lax.all_gather(ktan_flat, "ctx", axis=0, tiled=True),
        lax.all_gather(value_tangent, "ctx", axis=0, tiled=True),
    )
    seq_rows = gathered[0].shape[0]
    block_rows = math.gcd(seq_rows, 512)

    def scan_step(carry, block_id):
        pieces = tuple(
            (
                lax.dynamic_slice_in_dim(whole, block_id * block_rows, block_rows, 0)
                for whole in gathered
            )
        )
        return (attend(carry, query_n, query_nt, pieces, head_count), None)

    fold_state, unused = lax.scan(
        scan_step, init_state, jnp.arange(seq_rows // block_rows, dtype=jnp.int32)
    )
    peak, totals, numer, numer_tan, tilt = fold_state
    outputs = numer / totals[..., None]
    output_tan = numer_tan / totals[..., None] - (tilt / totals)[..., None] * outputs
    logsum = peak + jnp.log(totals)
    slot_count = time_index.shape[0]
    picked = jnp.sum(jnp.where(jnp.arange(slot_count, dtype=jnp.int32) == sample_id, time_index, 0))
    angle_t = 0.5 * math.pi * (picked.astype(jnp.float32) + 0.5) / STEPS
    raw_target = jnp.sin(angle_t) * jnp.cos(angle_t) * outputs + jnp.cos(angle_t) ** 2 * output_tan
    energy = group_sum((jnp.sum(raw_target * raw_target, axis=(1, 2)),))[0]
    level = jnp.sqrt(energy / CHANNELS)[:, None, None]
    cotangent = (loss_scale * raw_target / (level + floor_term)).astype(jnp.bfloat16)
    drift = jnp.sum(cotangent.astype(jnp.float32) * outputs, axis=-1)
    cycle_size = lax.axis_size("ctx")
    cycle_rank = lax.axis_index("ctx")

    def cycle_turn(step_id, carry):
        key_cur, value_cur, dkey_acc, dvalue_acc, dquery_acc = carry
        owner = (cycle_rank - step_id) % cycle_size
        key_use = lax.dynamic_slice_in_dim(gathered[0], owner * tok_rows, tok_rows, 0)
        value_use = lax.dynamic_slice_in_dim(gathered[1], owner * tok_rows, tok_rows, 0)
        dquery_add, dkey_add, dvalue_add = gradients(
            query_n,
            cotangent,
            logsum,
            drift,
            key_use.reshape(tok_rows, head_count, HD),
            value_use.reshape(tok_rows, head_count, HD),
        )
        dkey_acc, dvalue_acc = (
            from_behind(
                (dkey_acc + dkey_add.reshape(tok_rows, ch_dev)).astype(jnp.bfloat16), "ctx", 1
            ).astype(jnp.float32),
            from_behind(
                (dvalue_acc + dvalue_add.reshape(tok_rows, ch_dev)).astype(jnp.bfloat16), "ctx", 1
            ).astype(jnp.float32),
        )
        return (key_cur, value_cur, dkey_acc, dvalue_acc, dquery_acc + dquery_add)

    zero_flat = jnp.zeros((tok_rows, ch_dev), jnp.float32)
    cycle_state = lax.fori_loop(
        0, cycle_size, cycle_turn, (key_flat, values, zero_flat, zero_flat, zero_field)
    )
    dkey_hat = cycle_state[2].reshape(tok_rows, head_count, HD)
    value_grad = cycle_state[3].astype(jnp.bfloat16)
    dquery_hat = cycle_state[4]
    query_dy = rotate(dquery_hat, cos_table, sin_table, -1.0).reshape(tok_rows, ch_dev)
    key_dy = rotate(dkey_hat, cos_table, sin_table, -1.0).reshape(tok_rows, ch_dev)
    query_h = query_gvec * query_dy
    key_h = key_gvec * key_dy
    crosses = group_sum((jnp.sum(query_x * query_h, axis=1), jnp.sum(key_x * key_h, axis=1)))
    query_grad = (
        query_r * query_h - query_x * query_r**3 * (crosses[0] / CHANNELS)[:, None]
    ).astype(jnp.bfloat16)
    key_grad = (key_r * key_h - key_x * key_r**3 * (crosses[1] / CHANNELS)[:, None]).astype(
        jnp.bfloat16
    )
    query_part = jnp.sum(query_dy * query_x * query_r, axis=0)
    key_part = jnp.sum(key_dy * key_x * key_r, axis=0)
    empty_vec = jnp.zeros((CHANNELS,), jnp.float32)
    query_full = lax.dynamic_update_slice_in_dim(empty_vec, query_part, rank_in * ch_dev, 0)
    key_full = lax.dynamic_update_slice_in_dim(empty_vec, key_part, rank_in * ch_dev, 0)
    summed_ctx = lax.psum((query_full, key_full), "ctx")
    query_gain_grad, key_gain_grad = (
        lax.psum_scatter(summed_ctx[0], "fsdp", scatter_dimension=0, tiled=True),
        lax.psum_scatter(summed_ctx[1], "fsdp", scatter_dimension=0, tiled=True),
    )
    return (query_grad, key_grad, value_grad, query_gain_grad, key_gain_grad)


def solution(mesh):
    placed = (
        P("ctx", "fsdp"),
        P("ctx", "fsdp"),
        P("ctx", "fsdp"),
        P("ctx", "fsdp"),
        P("ctx", "fsdp"),
        P("ctx", "fsdp"),
        P("fsdp"),
        P("fsdp"),
        P(),
        P("ctx"),
    )
    return jax.shard_map(
        per_device,
        mesh=mesh,
        in_specs=placed,
        out_specs=(P("ctx", "fsdp"), P("ctx", "fsdp"), P("ctx", "fsdp"), P("fsdp"), P("fsdp")),
        check_vma=False,
    )
```

profile of v0, /device:TPU:0, one launch (start us, length us, event | category | flops | bytes accessed | tf_op | source)
XLA Modules:
  0.0 181.0 jit_solution(17366701281808251188)
XLA Ops:
  0.7 1.0 copy.77
  3.8 18.1 %all-reduce.3 = (f32[1,128]{1,0:T(1,128)S(1)}, f32[1,128]{1,0:T(1,128)S(1)}, f32[1,128]{1,0:T(1,128)S(1)}, f32[1,128]{1,0:T(1,128)S(1)}) all-reduce(f32[1,128]{1,0:T(1,128)S(1)} %get-tuple-element.484, f32[1,128]{1,0:T(1,128)S(1)} %get-tuple-element.486, ...), channel_id=1, replica_groups=mesh['ctx'=4,'fsdp'=8] {'fsdp'}, use_global_device_ids=true, to_apply=%region_3.4 | all-reduce | flops 512 | bytes 4096 | tf_op jit(solution)/shard_map/psum | solution.py:31
  22.7 12.7 %all-gather = f32[8,1,384]{2,1,0:T(1,128)S(1)} all-gather(f32[1,1,384]{2,1,0:T(1,128)S(1)} %reshape.362), channel_id=1, replica_groups=mesh['ctx'=4,'fsdp'=8] {'fsdp'}, dimensions={0}, use_global_device_ids=true | all-gather | bytes 13824 | tf_op jit(solution)/shard_map/all_gather | solution.py:113
  36.9 12.7 %all-gather.1 = f32[8,1,384]{2,1,0:T(1,128)S(1)} all-gather(f32[1,1,384]{2,1,0:T(1,128)S(1)} %reshape.364), channel_id=1, replica_groups=mesh['ctx'=4,'fsdp'=8] {'fsdp'}, dimensions={0}, use_global_device_ids=true | all-gather | bytes 13824 | tf_op jit(solution)/shard_map/all_gather | solution.py:114
  52.0 9.5 %all_gather.20 = bf16[512,384]{0,1:T(8,128)(2,1)S(1)} all-gather(bf16[128,384]{0,1:T(8,128)(2,1)S(1)} %bitcast.188), channel_id=1, replica_groups=mesh['ctx'=4,'fsdp'=8] {'ctx'}, dimensions={0}, use_global_device_ids=true | all-gather | bytes 491520 | tf_op jit(solution)/shard_map/all_gather | solution.py:163
  62.3 9.6 %all_gather.23 = bf16[512,384]{0,1:T(8,128)(2,1)S(1)} all-gather(bf16[128,384]{0,1:T(8,128)(2,1)S(1)} %bitcast.189), channel_id=1, replica_groups=mesh['ctx'=4,'fsdp'=8] {'ctx'}, dimensions={0}, use_global_device_ids=true | all-gather | bytes 491520 | tf_op jit(solution)/shard_map/all_gather | solution.py:165
  73.1 9.4 %all_gather.22 = bf16[512,384]{1,0:T(8,128)(2,1)S(1)} all-gather(bf16[128,384]{1,0:T(8,128)(2,1)S(1)} %copy-done.4), channel_id=1, replica_groups=mesh['ctx'=4,'fsdp'=8] {'ctx'}, dimensions={0}, use_global_device_ids=true | all-gather | bytes 491520 | tf_op jit(solution)/shard_map/all_gather | solution.py:166
  83.8 8.8 %all_gather.21 = bf16[512,384]{0,1:T(8,128)(2,1)S(1)} all-gather(bf16[128,384]{0,1:T(8,128)(2,1)S(1)} %copy.84), channel_id=1, replica_groups=mesh['ctx'=4,'fsdp'=8] {'ctx'}, dimensions={0}, use_global_device_ids=true | all-gather | bytes 491520 | tf_op jit(solution)/shard_map/all_gather | solution.py:164
  94.0 13.6 %psum.67 = f32[1,128]{1,0:T(1,128)S(1)} all-reduce(f32[1,128]{1,0:T(1,128)S(1)} %multiply_bitcast_fusion.4), channel_id=1, replica_groups=mesh['ctx'=4,'fsdp'=8] {'fsdp'}, use_global_device_ids=true, to_apply=%region_12.13 | all-reduce | flops 128 | bytes 1024 | tf_op jit(solution)/shard_map/psum | solution.py:31
  107.8 31.3 %while.13 = (s32[]{:T(128)}, f32[128,384]{0,1:T(8,128)S(1)}, f32[128,384]{0,1:T(8,128)S(1)}, f32[128,3,128]{0,2,1:T(8,128)S(1)}, s32[]{:T(128)}, /*index=5*/bf16...) while((s32[]{:T(128)}, f32[128,384]{0,1:T(8,128)S(1)}, ...), condition=%wide.region_15.16_spmd.clone, body=%wide.region_14.15_spmd.clone.sunk | while | flops 63750160 | bytes 5115304 | solution.py:222
  108.7 1.2 collective-permute-start
  110.1 1.5 collective-permute-start.1
  111.9 3.3 %collective-permute-done = bf16[128,384]{0,1:T(8,128)(2,1)S(1)} collective-permute-done((bf16[128,384]{0,1:T(8,128)(2,1)S(1)}, bf16[128,384]{0,1:T(8,128)(2,1)S(1)}, u32[]{:S(2)}, u32[]{:S(2)}) %collective-permute-start) | collective-permute-done | bytes 98336 | tf_op jit(solution)/shard_map/while/body/eval_jaxpr/ppermute | solution.py:23
  115.2 1.1 collective-permute-done.1
  117.8 2.4 %collective-permute-start.1 = (bf16[128,384]{0,1:T(8,128)(2,1)S(1)}, bf16[128,384]{0,1:T(8,128)(2,1)S(1)}, u32[]{:S(2)}, u32[]{:S(2)}) collective-permute-start(bf16[128,384]{0,1:T(8,128)(2,1)S(1)} %fusion.117), channel_id=1, source_target_pairs={{24,0},{0,8},{8,16},{16,24},{25,1},{1,9},{9,17},{17,25},{26,2},{2,... | collective-permute-start | bytes 294920 | tf_op jit(solution)/shard_map/while/body/eval_jaxpr/ppermute | solution.py:23
  120.4 2.7 %collective-permute-done = bf16[128,384]{0,1:T(8,128)(2,1)S(1)} collective-permute-done((bf16[128,384]{0,1:T(8,128)(2,1)S(1)}, bf16[128,384]{0,1:T(8,128)(2,1)S(1)}, u32[]{:S(2)}, u32[]{:S(2)}) %collective-permute-start) | collective-permute-done | bytes 98336 | tf_op jit(solution)/shard_map/while/body/eval_jaxpr/ppermute | solution.py:23
  123.1 1.0 collective-permute-done.1
  125.9 1.9 %collective-permute-start.1 = (bf16[128,384]{0,1:T(8,128)(2,1)S(1)}, bf16[128,384]{0,1:T(8,128)(2,1)S(1)}, u32[]{:S(2)}, u32[]{:S(2)}) collective-permute-start(bf16[128,384]{0,1:T(8,128)(2,1)S(1)} %fusion.117), channel_id=1, source_target_pairs={{24,0},{0,8},{8,16},{16,24},{25,1},{1,9},{9,17},{17,25},{26,2},{2,... | collective-permute-start | bytes 294920 | tf_op jit(solution)/shard_map/while/body/eval_jaxpr/ppermute | solution.py:23
  128.0 2.6 %collective-permute-done = bf16[128,384]{0,1:T(8,128)(2,1)S(1)} collective-permute-done((bf16[128,384]{0,1:T(8,128)(2,1)S(1)}, bf16[128,384]{0,1:T(8,128)(2,1)S(1)}, u32[]{:S(2)}, u32[]{:S(2)}) %collective-permute-start) | collective-permute-done | bytes 98336 | tf_op jit(solution)/shard_map/while/body/eval_jaxpr/ppermute | solution.py:23
  133.6 1.7 collective-permute-start.1
  135.5 2.6 %collective-permute-done = bf16[128,384]{0,1:T(8,128)(2,1)S(1)} collective-permute-done((bf16[128,384]{0,1:T(8,128)(2,1)S(1)}, bf16[128,384]{0,1:T(8,128)(2,1)S(1)}, u32[]{:S(2)}, u32[]{:S(2)}) %collective-permute-start) | collective-permute-done | bytes 98336 | tf_op jit(solution)/shard_map/while/body/eval_jaxpr/ppermute | solution.py:23
  138.0 1.1 collective-permute-done.1
  141.2 26.0 %all-reduce.2 = (f32[1,128]{1,0:T(1,128)S(1)}, f32[1,128]{1,0:T(1,128)S(1)}, f32[3072]{0:T(1024)S(1)}, f32[3072]{0:T(1024)S(1)}) all-reduce(f32[1,128]{1,0:T(1,128)S(1)} %multiply_bitcast_fusion.3, f32[1,128]{1,0:T(1,128)S(1)} %multiply_bitcast_fusion.1, ...), channel_id=1, replica_groups=mesh['ctx'=4,'fsdp'=8] {'fsdp'}, use_global_device_ids=true, to_apply=%region_17.18 | all-reduce | flops 6400 | bytes 51200 | tf_op jit(solution)/shard_map/psum | solution.py:31
  169.3 9.2 %all-reduce.4 = (f32[384]{0:T(512)}, f32[384]{0:T(512)}) all-reduce(f32[384]{0:T(512)S(1)} %dynamic-slice.1, f32[384]{0:T(512)S(1)} %dynamic-slice.3), channel_id=1, replica_groups=mesh['ctx'=4,'fsdp'=8] {'ctx'}, use_global_device_ids=true, to_apply=%region_21.22 | all-reduce | flops 768 | bytes 6144 | tf_op jit(solution)/shard_map/psum | solution.py:244
  (147 shorter events, 23.4 us)
Async XLA Ops:
  0.7 1.1 copy-start
  1.8 0.9 copy-start.1
  2.7 0.9 copy-start.2
  22.0 0.7 copy-start.5
  36.2 0.7 copy-start.6
  72.2 0.9 copy-start.4
  82.7 0.9 copy-start.3
  108.7 6.5 %collective-permute-start = (bf16[128,384]{0,1:T(8,128)(2,1)S(1)}, bf16[128,384]{0,1:T(8,128)(2,1)S(1)}, u32[]{:S(2)}, u32[]{:S(2)}) collective-permute-start(bf16[128,384]{0,1:T(8,128)(2,1)S(1)} %fusion.115), channel_id=1, source_target_pairs={{24,0},{0,8},{8,16},{16,24},{25,1},{1,9},{9,17},{17,25},{26,2},{2,... | collective-permute-start | bytes 294920 | tf_op jit(solution)/shard_map/while/body/eval_jaxpr/ppermute | solution.py:23
  110.1 6.2 %collective-permute-start.1 = (bf16[128,384]{0,1:T(8,128)(2,1)S(1)}, bf16[128,384]{0,1:T(8,128)(2,1)S(1)}, u32[]{:S(2)}, u32[]{:S(2)}) collective-permute-start(bf16[128,384]{0,1:T(8,128)(2,1)S(1)} %fusion.117), channel_id=1, source_target_pairs={{24,0},{0,8},{8,16},{16,24},{25,1},{1,9},{9,17},{17,25},{26,2},{2,... | collective-permute-start | bytes 294920 | tf_op jit(solution)/shard_map/while/body/eval_jaxpr/ppermute | solution.py:23
  117.2 5.9 %collective-permute-start = (bf16[128,384]{0,1:T(8,128)(2,1)S(1)}, bf16[128,384]{0,1:T(8,128)(2,1)S(1)}, u32[]{:S(2)}, u32[]{:S(2)}) collective-permute-start(bf16[128,384]{0,1:T(8,128)(2,1)S(1)} %fusion.115), channel_id=1, source_target_pairs={{24,0},{0,8},{8,16},{16,24},{25,1},{1,9},{9,17},{17,25},{26,2},{2,... | collective-permute-start | bytes 294920 | tf_op jit(solution)/shard_map/while/body/eval_jaxpr/ppermute | solution.py:23
  117.8 6.4 %collective-permute-start.1 = (bf16[128,384]{0,1:T(8,128)(2,1)S(1)}, bf16[128,384]{0,1:T(8,128)(2,1)S(1)}, u32[]{:S(2)}, u32[]{:S(2)}) collective-permute-start(bf16[128,384]{0,1:T(8,128)(2,1)S(1)} %fusion.117), channel_id=1, source_target_pairs={{24,0},{0,8},{8,16},{16,24},{25,1},{1,9},{9,17},{17,25},{26,2},{2,... | collective-permute-start | bytes 294920 | tf_op jit(solution)/shard_map/while/body/eval_jaxpr/ppermute | solution.py:23
  125.0 5.6 %collective-permute-start = (bf16[128,384]{0,1:T(8,128)(2,1)S(1)}, bf16[128,384]{0,1:T(8,128)(2,1)S(1)}, u32[]{:S(2)}, u32[]{:S(2)}) collective-permute-start(bf16[128,384]{0,1:T(8,128)(2,1)S(1)} %fusion.115), channel_id=1, source_target_pairs={{24,0},{0,8},{8,16},{16,24},{25,1},{1,9},{9,17},{17,25},{26,2},{2,... | collective-permute-start | bytes 294920 | tf_op jit(solution)/shard_map/while/body/eval_jaxpr/ppermute | solution.py:23
  125.9 5.7 %collective-permute-start.1 = (bf16[128,384]{0,1:T(8,128)(2,1)S(1)}, bf16[128,384]{0,1:T(8,128)(2,1)S(1)}, u32[]{:S(2)}, u32[]{:S(2)}) collective-permute-start(bf16[128,384]{0,1:T(8,128)(2,1)S(1)} %fusion.117), channel_id=1, source_target_pairs={{24,0},{0,8},{8,16},{16,24},{25,1},{1,9},{9,17},{17,25},{26,2},{2,... | collective-permute-start | bytes 294920 | tf_op jit(solution)/shard_map/while/body/eval_jaxpr/ppermute | solution.py:23
  132.4 5.6 %collective-permute-start = (bf16[128,384]{0,1:T(8,128)(2,1)S(1)}, bf16[128,384]{0,1:T(8,128)(2,1)S(1)}, u32[]{:S(2)}, u32[]{:S(2)}) collective-permute-start(bf16[128,384]{0,1:T(8,128)(2,1)S(1)} %fusion.115), channel_id=1, source_target_pairs={{24,0},{0,8},{8,16},{16,24},{25,1},{1,9},{9,17},{17,25},{26,2},{2,... | collective-permute-start | bytes 294920 | tf_op jit(solution)/shard_map/while/body/eval_jaxpr/ppermute | solution.py:23
  133.6 5.6 %collective-permute-start.1 = (bf16[128,384]{0,1:T(8,128)(2,1)S(1)}, bf16[128,384]{0,1:T(8,128)(2,1)S(1)}, u32[]{:S(2)}, u32[]{:S(2)}) collective-permute-start(bf16[128,384]{0,1:T(8,128)(2,1)S(1)} %fusion.117), channel_id=1, source_target_pairs={{24,0},{0,8},{8,16},{16,24},{25,1},{1,9},{9,17},{17,25},{26,2},{2,... | collective-permute-start | bytes 294920 | tf_op jit(solution)/shard_map/while/body/eval_jaxpr/ppermute | solution.py:23
  167.3 0.7 copy-start.7
where the time goes:
time: 182 us; the launch traced here: 181 us
  blocking collectives  130 us (71%)
  waiting for transfers between devices  15.5 us (9%)
  local copies, waits for them, and re-layouts  12.4 us (7%)
  starting transfers between devices  10.6 us (6%)
  matrix products  6.14 us (3%)
  between operations  3.17 us (2%)
  other arithmetic  3.03 us (2%)
    psum x3, blocking collectives, group_sum(): summed = lax.psum(placed, 'fsdp')  57.7 us
    ppermute x8, waiting for transfers between devices, from_behind(): return lax.ppermute(block, axis, route)  15.5 us
    all_gather x1, blocking collectives, per_device(): lax.all_gather(query_gain, 'fsdp', axis=0, tiled=True)  12.7 us
    all_gather x1, blocking collectives, per_device(): lax.all_gather(key_gain, 'fsdp', axis=0, tiled=True)  12.7 us
    ppermute x8, starting transfers between devices, from_behind(): return lax.ppermute(block, axis, route)  10.6 us
    unnamed x39, local copies, waits for them, and re-layouts  9.83 us
    all_gather x1, blocking collectives, per_device(): lax.all_gather(ktan_flat, 'ctx', axis=0, tiled=True)  9.63 us
    all_gather x1, blocking collectives, per_device(): lax.all_gather(key_flat, 'ctx', axis=0, tiled=True)  9.52 us
  transfers between devices with their start and end apart: 8, of which 8 were waited for; matrix products, arithmetic and copies ran while one was open for 1% of the time, Pallas kernels for 0%

commit v1 on v0

v1 whole, which is shorter than its diff:
```python
import functools
import math

import jax
import jax.numpy as jnp
import numpy as np
from jax import lax
from jax.experimental import pallas as pl
from jax.experimental.pallas import tpu as pltpu
from jax.sharding import PartitionSpec as P

HD = 128
STEPS = 1000

eps_norm = 1e-06
loss_scale = 256.0
rope_base = 10000.0
floor_term = 0.1

BOTH = ("ctx", "fsdp")
F32 = jnp.float32
BF16 = jnp.bfloat16
ORDER_ROWS = 16

NT = (((1,), (1,)), ((), ()))
TN = (((0,), (0,)), ((), ()))
NN = (((1,), (0,)), ((), ()))


def mm(lhs, rhs, dims):
    return lax.dot_general(lhs, rhs, dims, preferred_element_type=F32)


def eye_mask(size):
    rows = lax.broadcasted_iota(jnp.int32, (size, size), 0)
    return rows == lax.broadcasted_iota(jnp.int32, (size, size), 1)


def as_row(column):
    return jnp.sum(jnp.where(eye_mask(column.shape[0]), column, 0.0), axis=0, keepdims=True)


def as_column(row):
    return jnp.sum(jnp.where(eye_mask(row.shape[1]), row, 0.0), axis=1, keepdims=True)


def hosted_head(ctx_id, fsdp_id, n_ctx):
    return (ctx_id + n_ctx - fsdp_id % n_ctx) % n_ctx


def turn(field, cos_t, sin_t):
    return field * cos_t + pltpu.roll(field, HD // 2, 1) * sin_t


def sample_sum(ref, ctx_id, n_fsdp, head_split):
    start = ctx_id * n_fsdp + (lax.axis_index("fsdp") // head_split) * head_split
    return jnp.sum(ref[pl.ds(start, head_split)], axis=0)


def norm_scales(stats, channels):
    mean = stats * (1.0 / channels)
    inv = lax.rsqrt(mean[0:2] + eps_norm)
    inv_q, inv_k = as_column(inv[0:1]), as_column(inv[1:2])
    tilt = inv * inv * inv * mean[2:4]
    return inv_q, inv_k, as_column(tilt[0:1]), as_column(tilt[1:2])


def pack_kernel(n_ctx, heads, order_ref, q_ref, k_ref, v_ref, qt_ref, kt_ref, vt_ref, *outs):
    stats_ref, block_refs = outs[0], outs[1:]
    ctx_id, fsdp_id = lax.axis_index("ctx"), lax.axis_index("fsdp")
    rows = q_ref.shape[0]
    order = jnp.full((ORDER_ROWS, HD), order_ref[0].astype(F32), F32).astype(BF16)
    for dist, block in enumerate(block_refs):
        head = jnp.minimum(hosted_head(ctx_id ^ dist, fsdp_id, n_ctx), heads - 1)
        lanes = pl.ds(pl.multiple_of(head * HD, HD), HD)
        for at, ref in enumerate((q_ref, k_ref, v_ref, qt_ref, kt_ref, vt_ref)):
            block[at * rows : (at + 1) * rows, :] = ref[:, lanes]
        block[6 * rows :, :] = order
    q, k = q_ref[...].astype(F32), k_ref[...].astype(F32)
    qt, kt = qt_ref[...].astype(F32), kt_ref[...].astype(F32)
    sums = jnp.concatenate(
        [as_row(jnp.sum(p, axis=1, keepdims=True)) for p in (q * q, k * k, q * qt, k * kt)], axis=0
    )
    stats_ref[...] = jnp.broadcast_to(sums[None], stats_ref.shape)


def forward_kernel(n_ctx, n_fsdp, heads, channels, *refs):
    stats_ref, gains_ref, table_ref, coef_ref = refs[:4]
    block_refs = refs[4 : 4 + n_ctx]
    energy_ref, qcat_ref, kcat_ref, vcat_ref, out_ref, goal_ref, lse_ref, turn_ref = refs[4 + n_ctx :]
    ctx_id, fsdp_id = lax.axis_index("ctx"), lax.axis_index("fsdp")
    head = hosted_head(ctx_id, fsdp_id, n_ctx)
    active = head < heads
    gain_q, gain_k = gains_ref[0:1], gains_ref[1:2]
    rows = (block_refs[0].shape[0] - ORDER_ROWS) // 6
    inv_root = HD ** (-0.5)
    for dist, block in enumerate(block_refs):
        here = slice(dist * rows, (dist + 1) * rows)
        stats = sample_sum(stats_ref, ctx_id ^ dist, n_fsdp, channels // (heads * HD))
        inv_q, inv_k, tilt_q, tilt_k = norm_scales(stats, channels)
        order = block[6 * rows : 6 * rows + 1, :].astype(F32)
        both = table_ref[0:rows, :]
        for other in range(1, n_ctx):
            both = jnp.where(order == float(other), table_ref[other * rows : (other + 1) * rows, :], both)
        swapped = pltpu.roll(both, HD // 2, 1)
        low = lax.broadcasted_iota(jnp.int32, (rows, HD), 1) < HD // 2
        cos_t = jnp.where(low, both, swapped)
        sin_t = jnp.where(low, -swapped, both)
        turn_ref[here, 0:HD] = cos_t
        turn_ref[here, HD:] = sin_t

        def part(at):
            return block[at * rows : (at + 1) * rows, :]

        q, k = part(0).astype(F32), part(1).astype(F32)
        qt, kt = part(3).astype(F32), part(4).astype(F32)
        qcat_ref[here, HD:] = turn(q * inv_q * gain_q, cos_t, sin_t).astype(BF16)
        qcat_ref[here, 0:HD] = turn((qt * inv_q - q * tilt_q) * gain_q, cos_t, sin_t).astype(BF16)
        kcat_ref[here, 0:HD] = turn(k * inv_k * gain_k, cos_t, sin_t).astype(BF16)
        kcat_ref[here, HD:] = turn((kt * inv_k - k * tilt_k) * gain_k, cos_t, sin_t).astype(BF16)
        vcat_ref[here, 0:HD] = part(2)
        vcat_ref[here, HD:] = part(5)
    for dist in range(n_ctx):
        here = slice(dist * rows, (dist + 1) * rows)
        scores = mm(qcat_ref[here, HD:], kcat_ref[:, 0:HD], NT) * inv_root
        slopes = mm(qcat_ref[here, :], kcat_ref[...], NT) * inv_root
        peak = jnp.max(scores, axis=1, keepdims=True)
        weights = jnp.exp(scores - peak)
        totals = jnp.sum(weights, axis=1, keepdims=True)
        tilted = weights * slopes
        numer = mm(weights.astype(BF16), vcat_ref[...], NN)
        numer_tan = numer[:, HD:] + mm(tilted.astype(BF16), vcat_ref[:, 0:HD], NN)
        tilt = jnp.sum(tilted, axis=1, keepdims=True)
        output = numer[:, 0:HD] / totals
        output_tan = numer_tan / totals - (tilt / totals) * output
        goal = coef_ref[0:1] * output + coef_ref[1:2] * output_tan
        out_ref[here, :] = output
        goal_ref[here, :] = goal
        lse_ref[here, :] = jnp.broadcast_to(peak + jnp.log(totals), (rows, HD))
        row = as_row(jnp.sum(goal * goal, axis=1, keepdims=True))
        energy_ref[0, pl.ds(ctx_id ^ dist, 1), :] = jnp.where(active, row, 0.0)
    first = energy_ref[0]
    for at in range(1, energy_ref.shape[0]):
        energy_ref[at] = first


def backward_kernel(n_ctx, n_fsdp, heads, channels, *refs):
    stats_ref, energy_ref, gains_ref, qcat_ref, kcat_ref, vcat_ref = refs[:6]
    out_ref, goal_ref, lse_ref, turn_ref = refs[6:10]
    block_refs = refs[10 : 10 + n_ctx]
    cross_ref = refs[10 + n_ctx]
    back_refs = refs[11 + n_ctx : 11 + 2 * n_ctx]
    probs_ref, dscore_ref, cot_ref = refs[11 + 2 * n_ctx :]
    ctx_id, fsdp_id = lax.axis_index("ctx"), lax.axis_index("fsdp")
    active = hosted_head(ctx_id, fsdp_id, n_ctx) < heads
    head_split = channels // (heads * HD)
    sample = fsdp_id // head_split
    gain_q, gain_k = gains_ref[0:1], gains_ref[1:2]
    rows = (block_refs[0].shape[0] - ORDER_ROWS) // 6
    inv_root = HD ** (-0.5)
    energy = jnp.zeros((n_ctx, rows), F32)
    for ctx_at in range(n_ctx):
        energy = energy + jnp.sum(energy_ref[pl.ds(ctx_at * n_fsdp + sample * head_split, head_split)], axis=0)
    level = loss_scale / (jnp.sqrt(energy * (1.0 / channels)) + floor_term)
    block_ids = lax.broadcasted_iota(jnp.int32, (n_ctx, rows), 0)
    gain_q_sum = jnp.zeros((1, HD), F32)
    gain_k_sum = jnp.zeros((1, HD), F32)
    crosses = []
    for dist in range(n_ctx):
        here = slice(dist * rows, (dist + 1) * rows)
        owner = ctx_id ^ dist
        scale = as_column(jnp.sum(jnp.where(block_ids == owner, level, 0.0), axis=0, keepdims=True))
        output = out_ref[here, :]
        cot = (scale * goal_ref[here, :]).astype(BF16)
        drift = jnp.sum(cot.astype(F32) * output, axis=1, keepdims=True)
        scores = mm(qcat_ref[here, HD:], kcat_ref[:, 0:HD], NT) * inv_root
        probs = jnp.exp(scores - lse_ref[here, 0:1])
        dprobs = mm(cot, vcat_ref[:, 0:HD], NT)
        dscore = (probs * (dprobs - drift) * inv_root).astype(BF16)
        probs_ref[here, :] = probs.astype(BF16)
        dscore_ref[here, :] = dscore
        cot_ref[here, :] = cot
        dquery = mm(dscore, kcat_ref[:, 0:HD], NN)
        inv_q = norm_scales(sample_sum(stats_ref, owner, n_fsdp, head_split), channels)[0]
        x = block_refs[dist][0:rows, :].astype(F32)
        dy = turn(dquery, turn_ref[here, 0:HD], -turn_ref[here, HD:])
        grown = gain_q * dy
        back_refs[dist][0:rows, :] = grown.astype(BF16)
        crosses.append(as_row(jnp.sum(x * grown, axis=1, keepdims=True)))
        gain_q_sum = gain_q_sum + jnp.sum(dy * x * inv_q, axis=0, keepdims=True)
    for dist in range(n_ctx):
        here = slice(dist * rows, (dist + 1) * rows)
        owner = ctx_id ^ dist
        back_refs[dist][2 * rows : 3 * rows, :] = mm(probs_ref[:, here], cot_ref[...], TN).astype(BF16)
        dkey = mm(dscore_ref[:, here], qcat_ref[:, HD:], TN)
        inv_k = norm_scales(sample_sum(stats_ref, owner, n_fsdp, head_split), channels)[1]
        x = block_refs[dist][rows : 2 * rows, :].astype(F32)
        dy = turn(dkey, turn_ref[here, 0:HD], -turn_ref[here, HD:])
        grown = gain_k * dy
        back_refs[dist][rows : 2 * rows, :] = grown.astype(BF16)
        cross_k = as_row(jnp.sum(x * grown, axis=1, keepdims=True))
        gain_k_sum = gain_k_sum + jnp.sum(dy * x * inv_k, axis=0, keepdims=True)
        crosses[dist] = jnp.concatenate([crosses[dist], cross_k], axis=0)
    for dist in range(n_ctx):
        sums = jnp.concatenate([crosses[dist], gain_q_sum, gain_k_sum], axis=0)
        sums = jnp.where(active, sums, 0.0)
        start = (ctx_id ^ dist) * n_fsdp
        for at in range(n_fsdp):
            cross_ref[start + at] = sums


def finish_kernel(n_ctx, n_fsdp, heads, channels, *refs):
    stats_ref, cross_ref, q_ref, k_ref = refs[:4]
    back_refs = refs[4 : 4 + n_ctx]
    dq_ref, dk_ref, dv_ref, dgain_ref = refs[4 + n_ctx :]
    ctx_id, fsdp_id = lax.axis_index("ctx"), lax.axis_index("fsdp")
    head_split = channels // (heads * HD)
    sample = fsdp_id // head_split
    rows = q_ref.shape[0]
    inv_q, inv_k, _, _ = norm_scales(sample_sum(stats_ref, ctx_id, n_fsdp, head_split), channels)
    total = jnp.zeros((4, rows), F32)
    for ctx_at in range(n_ctx):
        total = total + jnp.sum(cross_ref[pl.ds(ctx_at * n_fsdp + sample * head_split, head_split)], axis=0)
    mean = total[0:2] * (1.0 / channels)
    tilt_q = inv_q * inv_q * inv_q * as_column(mean[0:1])
    tilt_k = inv_k * inv_k * inv_k * as_column(mean[1:2])
    for dist in range(n_ctx):
        host = ctx_id ^ dist
        head = hosted_head(host, fsdp_id, n_ctx)

        @pl.when(head < heads)
        def _(dist=dist, host=host, head=head):
            back = back_refs[dist]
            lanes = pl.ds(pl.multiple_of(head * HD, HD), HD)
            h_q, h_k = back[0:rows, :].astype(F32), back[rows : 2 * rows, :].astype(F32)
            dq_ref[:, lanes] = (inv_q * h_q - q_ref[:, lanes].astype(F32) * tilt_q).astype(BF16)
            dk_ref[:, lanes] = (inv_k * h_k - k_ref[:, lanes].astype(F32) * tilt_k).astype(BF16)
            dv_ref[:, lanes] = back[2 * rows : 3 * rows, :]
            dgain_ref[:, lanes] = cross_ref[host * n_fsdp + fsdp_id, 2:4, :]


def per_device(
    queries,
    keys,
    values,
    query_tangent,
    key_tangent,
    value_tangent,
    query_gain,
    key_gain,
    time_index,
    shard_order,
):
    n_ctx, n_fsdp = lax.axis_size("ctx"), lax.axis_size("fsdp")
    n_all = n_ctx * n_fsdp
    ctx_id, fsdp_id = lax.axis_index("ctx"), lax.axis_index("fsdp")
    rows, ch_dev = queries.shape
    heads = ch_dev // HD
    channels = query_gain.shape[0] * n_fsdp
    head_split = channels // ch_dev
    seq = rows * n_ctx
    sizes = (n_ctx, n_fsdp, heads, channels)
    head = hosted_head(ctx_id, fsdp_id, n_ctx)

    vmem = pl.BlockSpec(memory_space=pltpu.VMEM)
    smem = pl.BlockSpec(memory_space=pltpu.SMEM)

    def kernel(body, ins, outs, scratch=(), flops=10**8, in_specs=None):
        return pl.pallas_call(
            body,
            out_shape=[jax.ShapeDtypeStruct(*o) for o in outs],
            in_specs=in_specs or [vmem] * len(ins),
            out_specs=[vmem] * len(outs),
            scratch_shapes=list(scratch),
            cost_estimate=pl.CostEstimate(flops=flops, bytes_accessed=2**20, transcendentals=0),
        )(*ins)

    def exchange(chunks):
        return lax.all_to_all(chunks, BOTH, 0, 0)

    def to_peers(blocks, sends):
        out = [blocks[0]]
        for dist in range(1, n_ctx):
            route = [
                (c * n_fsdp + f, (c ^ dist) * n_fsdp + f)
                for c in range(n_ctx)
                for f in range(n_fsdp)
                if sends(c, c ^ dist, f)
            ]
            out.append(lax.ppermute(blocks[dist], BOTH, route))
        return out

    places = np.arange(seq, dtype=np.float32)
    freqs = (rope_base ** (-np.arange(HD // 2) / (HD // 2))).astype(np.float32)
    angles = (places[:, None] * freqs[None, :]).astype(np.float64)
    table = jnp.asarray(np.concatenate([np.cos(angles), np.sin(angles)], axis=1).astype(np.float32))

    if channels == query_gain.shape[0] * head_split:
        gains = (query_gain, key_gain)
    else:
        gains = tuple(
            lax.dynamic_slice_in_dim(
                lax.all_gather(g, "fsdp", axis=0, tiled=True), (fsdp_id % head_split) * ch_dev, ch_dev, 0
            )
            for g in (query_gain, key_gain)
        )
    head_at = jnp.minimum(head, heads - 1) * HD
    head_gains = jnp.stack([lax.dynamic_slice_in_dim(g, head_at, HD, 0) for g in gains])

    slot_count = time_index.shape[0]
    picked = jnp.sum(
        jnp.where(jnp.arange(slot_count, dtype=jnp.int32) == fsdp_id // head_split, time_index, 0)
    )
    angle_t = 0.5 * math.pi * (picked.astype(F32) + 0.5) / STEPS
    coefs = jnp.stack([jnp.sin(angle_t) * jnp.cos(angle_t), jnp.cos(angle_t) ** 2])
    coefs = jnp.broadcast_to(coefs[:, None], (2, HD))

    block_shape = ((6 * rows + ORDER_ROWS, HD), BF16)
    stats_out, *blocks = kernel(
        functools.partial(pack_kernel, n_ctx, heads),
        (shard_order, queries, keys, values, query_tangent, key_tangent, value_tangent),
        [((n_all, 4, rows), F32)] + [block_shape] * n_ctx,
        in_specs=[smem] + [vmem] * 6,
    )
    blocks = to_peers(blocks, lambda c, peer, f: hosted_head(peer, f, n_ctx) < heads)
    stats = exchange(stats_out)

    energy_out, qcat, kcat, vcat, output, goal, lse, turns = kernel(
        functools.partial(forward_kernel, *sizes),
        (stats, head_gains, table, coefs, *blocks),
        [((n_all, n_ctx, rows), F32)]
        + [((seq, 2 * HD), BF16)] * 3
        + [((seq, HD), F32)] * 3
        + [((seq, 2 * HD), F32)],
    )
    energy = exchange(energy_out)

    cross_out, *back = kernel(
        functools.partial(backward_kernel, *sizes),
        (stats, energy, head_gains, qcat, kcat, vcat, output, goal, lse, turns, *blocks),
        [((n_all, 4, rows), F32)] + [((3 * rows, HD), BF16)] * n_ctx,
        scratch=[
            pltpu.VMEM((seq, seq), BF16),
            pltpu.VMEM((seq, seq), BF16),
            pltpu.VMEM((seq, HD), BF16),
        ],
    )
    back = to_peers(back, lambda c, peer, f: hosted_head(c, f, n_ctx) < heads)
    crosses = exchange(cross_out)

    query_grad, key_grad, value_grad, gain_grads = kernel(
        functools.partial(finish_kernel, *sizes),
        (stats, crosses, queries, keys, *back),
        [((rows, ch_dev), BF16)] * 3 + [((2, ch_dev), F32)],
    )
    if query_gain.shape[0] == ch_dev:
        query_gain_grad, key_gain_grad = gain_grads[0], gain_grads[1]
    else:
        start = (fsdp_id % head_split) * ch_dev
        placed = lax.dynamic_update_slice(jnp.zeros((2, channels), F32), gain_grads, (0, start))
        query_gain_grad, key_gain_grad = lax.psum_scatter(placed, "fsdp", scatter_dimension=1, tiled=True)
    return (query_grad, key_grad, value_grad, query_gain_grad, key_gain_grad)


def solution(mesh):
    placed = (P("ctx", "fsdp"),) * 6 + (P("fsdp"), P("fsdp"), P(), P("ctx"))
    return jax.shard_map(
        per_device,
        mesh=mesh,
        in_specs=placed,
        out_specs=(P("ctx", "fsdp"), P("ctx", "fsdp"), P("ctx", "fsdp"), P("fsdp"), P("fsdp")),
        check_vma=False,
    )
```

time: 182 us -> 70.4 us (0.39)
  the two profiles are of different devices: /device:TPU:0 before, /device:TPU:8 now
where the time goes in v1:
time: 70.4 us; the launch traced here: 69.7 us
  starting transfers between devices  27.4 us (39%)
  Pallas kernels  14.7 us (21%)
  waiting for transfers between devices  11 us (16%)
  blocking collectives  10.2 us (14%)
  local copies, waits for them, and re-layouts  3.53 us (5%)
  between operations  2.26 us (3%)
    ppermute x6, starting transfers between devices, to_peers(): out.append(lax.ppermute(blocks[dist], BOTH, route))  17.4 us
    pallas_call x4, Pallas kernels, kernel(): pl.pallas_call(body, out_shape=[jax.ShapeDtypeStruct(*o) for o in outs],...  14.7 us
    ppermute x6, waiting for transfers between devices, to_peers(): out.append(lax.ppermute(blocks[dist], BOTH, route))  11 us
    all_to_all x1, blocking collectives, exchange(): return lax.all_to_all(chunks, BOTH, 0, 0)  10.2 us
    all_to_all x2, starting transfers between devices, exchange(): return lax.all_to_all(chunks, BOTH, 0, 0)  9.99 us
  transfers between devices with their start and end apart: 8, of which 3 were waited for; matrix products, arithmetic and copies ran while one was open for 2% of the time, Pallas kernels for 0%

profile of v1, /device:TPU:8, one launch (start us, length us, event | category | flops | bytes accessed | tf_op | source)
XLA Modules:
  0.0 69.7 jit_solution(14715382834968715438)
XLA Ops:
  1.3 2.1 %shard_map.146 = (f32[32,4,128]{2,1,0:T(4,128)}, bf16[784,128]{1,0:T(8,128)(2,1)}, bf16[784,128]{1,0:T(8,128)(2,1)}, bf16[784,128]{1,0:T(8,128)(2,1)}, bf16[784,128]{1,0:T(8,128)(2,1)}) custom-call(s32[1]{0:T(128)S(6)} %copy.17.order_ref, bf16[128,384]{1,0:T(8,128)(2,1)} %refs_2_.2, bf16[128,384]{1,0:T(8,128)(2,1)} %refs_3_.1, bf16[128,384]{1,0:T(8,128)(2,1)} %v_ref.1, ...), custom_call_target="tpu_custom_call" | custom-call | flops 100000000 | bytes 1048576 | tf_op jit(solution)/shard_map/pallas_call | solution.py:269
  3.4 6.0 %all-to-all-start = ((f32[32,4,128]{2,1,0:T(4,128)}), f32[32,4,128]{2,1,0:T(4,128)S(1)}, u32[]{:S(2)}, u32[]{:S(2)}) async-start(f32[32,4,128]{2,1,0:T(4,128)} %get-tuple-element.27), calls=%async_computation | async-start | bytes 131072 | tf_op jit(solution)/shard_map/all_to_all | solution.py:279
  9.5 1.3 %collective-permute-start = (bf16[784,128]{1,0:T(8,128)(2,1)}, bf16[784,128]{1,0:T(8,128)(2,1)S(1)}, u32[]{:S(2)}, u32[]{:S(2)}) collective-permute-start(bf16[784,128]{1,0:T(8,128)(2,1)} %get-tuple-element.29), channel_id=1, source_target_pairs={{0,8},{1,9},{3,11},{4,12},{5,13},{7,15},{8,0},{10,2},{11,3},{12,4}... | collective-permute-start | bytes 602120 | tf_op jit(solution)/shard_map/ppermute | solution.py:290
  10.8 5.5 %collective-permute-start.1 = (bf16[784,128]{1,0:T(8,128)(2,1)}, bf16[784,128]{1,0:T(8,128)(2,1)S(1)}, u32[]{:S(2)}, u32[]{:S(2)}) collective-permute-start(bf16[784,128]{1,0:T(8,128)(2,1)} %get-tuple-element.30), channel_id=1, source_target_pairs={{0,16},{1,17},{2,18},{4,20},{5,21},{6,22},{9,25},{10,26},{11,27},{... | collective-permute-start | bytes 602120 | tf_op jit(solution)/shard_map/ppermute | solution.py:290
  16.2 1.9 %collective-permute-start.2 = (bf16[784,128]{1,0:T(8,128)(2,1)}, bf16[784,128]{1,0:T(8,128)(2,1)S(1)}, u32[]{:S(2)}, u32[]{:S(2)}) collective-permute-start(bf16[784,128]{1,0:T(8,128)(2,1)} %get-tuple-element.31), channel_id=1, source_target_pairs={{1,25},{2,26},{3,27},{5,29},{6,30},{7,31},{8,16},{9,17},{10,18},{1... | collective-permute-start | bytes 602120 | tf_op jit(solution)/shard_map/ppermute | solution.py:290
  19.0 0.8 %dynamic-slice_bitcast_fusion = (f32[1,128]{1,0:T(1,128)S(1)}, f32[1,128]{1,0:T(1,128)S(1)}) fusion(f32[384]{0:T(512)} %param.18, s32[]{:T(128)S(6)} %select_n.25, f32[384]{0:T(512)} %param.17), kind=kLoop, calls=%fused_computation.4 | loop fusion | bytes 2052 | tf_op jit(solution)/shard_map/stack | solution.py:308
  19.8 0.1 pad_maximum_fusion.1
  19.9 0.6 pad_maximum_fusion.refs_1_.refs_2_
  20.4 5.5 %collective-permute-done.1.refs_6_.refs_12_ = bf16[784,128]{1,0:T(8,128)(2,1)S(1)} collective-permute-done((bf16[784,128]{1,0:T(8,128)(2,1)}, bf16[784,128]{1,0:T(8,128)(2,1)S(1)}, u32[]{:S(2)}, u32[]{:S(2)}) %collective-permute-start.1) | collective-permute-done | bytes 200736 | tf_op jit(solution)/shard_map/ppermute | solution.py:290
  26.0 0.7 broadcast_in_dim.4.refs_3_
  26.7 0.1 copy-done.3
  26.7 5.2 %shard_map.147 = (f32[32,4,128]{2,1,0:T(4,128)}, bf16[512,256]{1,0:T(8,128)(2,1)}, bf16[512,256]{1,0:T(8,128)(2,1)}, bf16[512,256]{1,0:T(8,128)(2,1)}, f32[512,1...) custom-call(f32[32,4,128]{2,1,0:T(4,128)} %copy-done, ...), custom_call_target="tpu_custom_call" | custom-call | flops 100000000 | bytes 1048576 | tf_op jit(solution)/shard_map/pallas_call | solution.py:269
  32.0 10.2 %all_to_all.15.refs_1_ = f32[32,4,128]{2,1,0:T(4,128)} all-to-all(f32[32,4,128]{2,1,0:T(4,128)} %get-tuple-element.32), channel_id=1, replica_groups=mesh['ctx'=4,'fsdp'=8] {'ctx','fsdp'}, dimensions={0} | all-to-all | bytes 131072 | tf_op jit(solution)/shard_map/all_to_all | solution.py:279
  42.2 5.2 %shard_map.148 = (f32[32,4,128]{2,1,0:T(4,128)}, bf16[384,128]{1,0:T(8,128)(2,1)}, bf16[384,128]{1,0:T(8,128)(2,1)}, bf16[384,128]{1,0:T(8,128)(2,1)}, bf16[384,128]{1,0:T(8,128)(2,1)}) custom-call(f32[32,4,128]{2,1,0:T(4,128)} %copy-done, f32[32,4,128]{2,1,0:T(4,128)} %all_to_all.15.refs_1_, f32[2,128]{1,0:T(2,128)} %pad_maximum_fusion.refs_1_.refs_2_, ...), custom_call_target="tpu_custom_call" | custom-call | flops 100000000 | bytes 1048576 | tf_op jit(solution)/shard_map/pallas_call | solution.py:269
  47.4 4.0 %all-to-all-start.2 = ((f32[32,4,128]{2,1,0:T(4,128)}), f32[32,4,128]{2,1,0:T(4,128)S(1)}, u32[]{:S(2)}, u32[]{:S(2)}) async-start(f32[32,4,128]{2,1,0:T(4,128)} %get-tuple-element.40), calls=%async_computation.2 | async-start | bytes 131072 | tf_op jit(solution)/shard_map/all_to_all | solution.py:279
  51.3 3.4 %collective-permute-start.3 = (bf16[384,128]{1,0:T(8,128)(2,1)}, bf16[384,128]{1,0:T(8,128)(2,1)S(1)}, u32[]{:S(2)}, u32[]{:S(2)}) collective-permute-start(bf16[384,128]{1,0:T(8,128)(2,1)} %get-tuple-element.42), channel_id=1, source_target_pairs={{0,8},{2,10},{3,11},{4,12},{6,14},{7,15},{8,0},{9,1},{11,3},{12,4}... | collective-permute-start | bytes 294920 | tf_op jit(solution)/shard_map/ppermute | solution.py:290
  54.7 3.4 %collective-permute-start.4 = (bf16[384,128]{1,0:T(8,128)(2,1)}, bf16[384,128]{1,0:T(8,128)(2,1)S(1)}, u32[]{:S(2)}, u32[]{:S(2)}) collective-permute-start(bf16[384,128]{1,0:T(8,128)(2,1)} %get-tuple-element.43), channel_id=1, source_target_pairs={{0,16},{2,18},{3,19},{4,20},{6,22},{7,23},{8,24},{9,25},{11,27},{1... | collective-permute-start | bytes 294920 | tf_op jit(solution)/shard_map/ppermute | solution.py:290
  58.2 1.9 %collective-permute-start.5 = (bf16[384,128]{1,0:T(8,128)(2,1)S(1)}, bf16[384,128]{1,0:T(8,128)(2,1)S(1)}, u32[]{:S(2)}, u32[]{:S(2)}) collective-permute-start(bf16[384,128]{1,0:T(8,128)(2,1)S(1)} %copy-done.8), channel_id=1, source_target_pairs={{0,24},{2,26},{3,27},{4,28},{6,30},{7,31},{8,16},{9,17},{11,19},{1... | collective-permute-start | bytes 294920 | tf_op jit(solution)/shard_map/ppermute | solution.py:290
  60.1 2.4 %collective-permute-done.4.refs_6_ = bf16[384,128]{1,0:T(8,128)(2,1)S(1)} collective-permute-done((bf16[384,128]{1,0:T(8,128)(2,1)}, bf16[384,128]{1,0:T(8,128)(2,1)S(1)}, u32[]{:S(2)}, u32[]{:S(2)}) %collective-permute-start.4) | collective-permute-done | bytes 98336 | tf_op jit(solution)/shard_map/ppermute | solution.py:290
  62.5 3.1 %collective-permute-done.5.refs_7_ = bf16[384,128]{1,0:T(8,128)(2,1)S(1)} collective-permute-done((bf16[384,128]{1,0:T(8,128)(2,1)S(1)}, bf16[384,128]{1,0:T(8,128)(2,1)S(1)}, u32[]{:S(2)}, u32[]{:S(2)}) %collective-permute-start.5) | collective-permute-done | bytes 98336 | tf_op jit(solution)/shard_map/ppermute | solution.py:290
  65.6 0.6 copy-done.7
  66.2 0.0 copy-done.4
  66.2 2.2 %shard_map.149 = (bf16[128,384]{1,0:T(8,128)(2,1)}, bf16[128,384]{1,0:T(8,128)(2,1)}, bf16[128,384]{1,0:T(8,128)(2,1)}, f32[2,384]{1,0:T(2,128)}) custom-call(f32[32,4,128]{2,1,0:T(4,128)} %copy-done, f32[32,4,128]{2,1,0:T(4,128)} %copy-done.4, bf16[128,384]{1,0:T(8,128)(2,1)} %refs_2_.2, bf16[128,384]{1,0:T(8,128)(2,1)} %refs_3_.1, ...), custom_call_target="tpu_custom_call" | custom-call | flops 100000000 | bytes 1048576 | tf_op jit(solution)/shard_map/pallas_call | solution.py:269
  68.4 1.3 %slice_reduce_fusion = (f32[384]{0:T(512)}, f32[384]{0:T(512)}) fusion(f32[2,384]{1,0:T(2,128)} %get-tuple-element.48), kind=kLoop, calls=%fused_computation | loop fusion | bytes 6144 | tf_op jit(solution)/shard_map/slice | solution.py:357
  (20 shorter events, 0.0 us)
Async XLA Ops:
  3.4 17.0 %all-to-all-start = ((f32[32,4,128]{2,1,0:T(4,128)}), f32[32,4,128]{2,1,0:T(4,128)S(1)}, u32[]{:S(2)}, u32[]{:S(2)}) async-start(f32[32,4,128]{2,1,0:T(4,128)} %get-tuple-element.27), calls=%async_computation | async-start | bytes 131072 | tf_op jit(solution)/shard_map/all_to_all | solution.py:279
  9.5 11.0 %collective-permute-start = (bf16[784,128]{1,0:T(8,128)(2,1)}, bf16[784,128]{1,0:T(8,128)(2,1)S(1)}, u32[]{:S(2)}, u32[]{:S(2)}) collective-permute-start(bf16[784,128]{1,0:T(8,128)(2,1)} %get-tuple-element.29), channel_id=1, source_target_pairs={{0,8},{1,9},{3,11},{4,12},{5,13},{7,15},{8,0},{10,2},{11,3},{12,4}... | collective-permute-start | bytes 602120 | tf_op jit(solution)/shard_map/ppermute | solution.py:290
  10.8 15.2 %collective-permute-start.1 = (bf16[784,128]{1,0:T(8,128)(2,1)}, bf16[784,128]{1,0:T(8,128)(2,1)S(1)}, u32[]{:S(2)}, u32[]{:S(2)}) collective-permute-start(bf16[784,128]{1,0:T(8,128)(2,1)} %get-tuple-element.30), channel_id=1, source_target_pairs={{0,16},{1,17},{2,18},{4,20},{5,21},{6,22},{9,25},{10,26},{11,27},{... | collective-permute-start | bytes 602120 | tf_op jit(solution)/shard_map/ppermute | solution.py:290
  16.2 9.8 %collective-permute-start.2 = (bf16[784,128]{1,0:T(8,128)(2,1)}, bf16[784,128]{1,0:T(8,128)(2,1)S(1)}, u32[]{:S(2)}, u32[]{:S(2)}) collective-permute-start(bf16[784,128]{1,0:T(8,128)(2,1)} %get-tuple-element.31), channel_id=1, source_target_pairs={{1,25},{2,26},{3,27},{5,29},{6,30},{7,31},{8,16},{9,17},{10,18},{1... | collective-permute-start | bytes 602120 | tf_op jit(solution)/shard_map/ppermute | solution.py:290
  20.4 6.2 %copy-start = (f32[32,4,128]{2,1,0:T(4,128)}, f32[32,4,128]{2,1,0:T(4,128)S(1)}, u32[]{:S(2)}) copy-start(f32[32,4,128]{2,1,0:T(4,128)S(1)} %all-to-all-done.refs_0_) | copy-start | bytes 196612
  20.4 6.2 %copy-start.1 = (bf16[784,128]{1,0:T(8,128)(2,1)}, bf16[784,128]{1,0:T(8,128)(2,1)S(1)}, u32[]{:S(2)}) copy-start(bf16[784,128]{1,0:T(8,128)(2,1)S(1)} %collective-permute-done.refs_5_.refs_11_) | copy-start | bytes 602116
  26.0 0.7 %copy-start.2 = (bf16[784,128]{1,0:T(8,128)(2,1)}, bf16[784,128]{1,0:T(8,128)(2,1)S(1)}, u32[]{:S(2)}) copy-start(bf16[784,128]{1,0:T(8,128)(2,1)S(1)} %collective-permute-done.1.refs_6_.refs_12_) | copy-start | bytes 602116
  26.0 0.8 %copy-start.3 = (bf16[784,128]{1,0:T(8,128)(2,1)}, bf16[784,128]{1,0:T(8,128)(2,1)S(1)}, u32[]{:S(2)}) copy-start(bf16[784,128]{1,0:T(8,128)(2,1)S(1)} %collective-permute-done.2.refs_7_.refs_13_) | copy-start | bytes 602116
  47.4 10.8 %copy-start.8 = (bf16[384,128]{1,0:T(8,128)(2,1)S(1)}, bf16[384,128]{1,0:T(8,128)(2,1)}, u32[]{:S(2)}) copy-start(bf16[384,128]{1,0:T(8,128)(2,1)} %get-tuple-element.44) | copy-start | bytes 294916
  47.4 18.2 %all-to-all-start.2 = ((f32[32,4,128]{2,1,0:T(4,128)}), f32[32,4,128]{2,1,0:T(4,128)S(1)}, u32[]{:S(2)}, u32[]{:S(2)}) async-start(f32[32,4,128]{2,1,0:T(4,128)} %get-tuple-element.40), calls=%async_computation.2 | async-start | bytes 131072 | tf_op jit(solution)/shard_map/all_to_all | solution.py:279
  51.3 8.7 %collective-permute-start.3 = (bf16[384,128]{1,0:T(8,128)(2,1)}, bf16[384,128]{1,0:T(8,128)(2,1)S(1)}, u32[]{:S(2)}, u32[]{:S(2)}) collective-permute-start(bf16[384,128]{1,0:T(8,128)(2,1)} %get-tuple-element.42), channel_id=1, source_target_pairs={{0,8},{2,10},{3,11},{4,12},{6,14},{7,15},{8,0},{9,1},{11,3},{12,4}... | collective-permute-start | bytes 294920 | tf_op jit(solution)/shard_map/ppermute | solution.py:290
  54.7 7.8 %collective-permute-start.4 = (bf16[384,128]{1,0:T(8,128)(2,1)}, bf16[384,128]{1,0:T(8,128)(2,1)S(1)}, u32[]{:S(2)}, u32[]{:S(2)}) collective-permute-start(bf16[384,128]{1,0:T(8,128)(2,1)} %get-tuple-element.43), channel_id=1, source_target_pairs={{0,16},{2,18},{3,19},{4,20},{6,22},{7,23},{8,24},{9,25},{11,27},{1... | collective-permute-start | bytes 294920 | tf_op jit(solution)/shard_map/ppermute | solution.py:290
  58.2 7.4 %collective-permute-start.5 = (bf16[384,128]{1,0:T(8,128)(2,1)S(1)}, bf16[384,128]{1,0:T(8,128)(2,1)S(1)}, u32[]{:S(2)}, u32[]{:S(2)}) collective-permute-start(bf16[384,128]{1,0:T(8,128)(2,1)S(1)} %copy-done.8), channel_id=1, source_target_pairs={{0,24},{2,26},{3,27},{4,28},{6,30},{7,31},{8,16},{9,17},{11,19},{1... | collective-permute-start | bytes 294920 | tf_op jit(solution)/shard_map/ppermute | solution.py:290
  60.1 5.5 %copy-start.5 = (bf16[384,128]{1,0:T(8,128)(2,1)}, bf16[384,128]{1,0:T(8,128)(2,1)S(1)}, u32[]{:S(2)}) copy-start(bf16[384,128]{1,0:T(8,128)(2,1)S(1)} %collective-permute-done.3.refs_5_) | copy-start | bytes 294916
  62.5 3.1 %copy-start.6 = (bf16[384,128]{1,0:T(8,128)(2,1)}, bf16[384,128]{1,0:T(8,128)(2,1)S(1)}, u32[]{:S(2)}) copy-start(bf16[384,128]{1,0:T(8,128)(2,1)S(1)} %collective-permute-done.4.refs_6_) | copy-start | bytes 294916
  65.6 0.6 copy-start.7
  65.6 0.7 copy-start.4

commit v2 on v1

v2 whole, which is shorter than its diff:
```python
import functools
import math

import jax
import jax.numpy as jnp
import numpy as np
from jax import lax
from jax.experimental import pallas as pl
from jax.experimental.pallas import tpu as pltpu
from jax.sharding import PartitionSpec as P


HD = 128
STEPS = 1000

eps_norm = 1e-06
loss_scale = 256.0
rope_base = 10000.0
floor_term = 0.1

BOTH = ("ctx", "fsdp")
F32 = jnp.float32
BF16 = jnp.bfloat16
ORDER_ROWS = 16

NT = (((1,), (1,)), ((), ()))
TN = (((0,), (0,)), ((), ()))
NN = (((1,), (0,)), ((), ()))


def mm(lhs, rhs, dims):
    return lax.dot_general(lhs, rhs, dims, preferred_element_type=F32)


def eye_mask(size):
    rows = lax.broadcasted_iota(jnp.int32, (size, size), 0)
    return rows == lax.broadcasted_iota(jnp.int32, (size, size), 1)


def as_row(column):
    return jnp.sum(jnp.where(eye_mask(column.shape[0]), column, 0.0), axis=0, keepdims=True)


def as_column(row):
    return jnp.sum(jnp.where(eye_mask(row.shape[1]), row, 0.0), axis=1, keepdims=True)


def hosted_head(ctx_id, fsdp_id, n_ctx):
    return (ctx_id + n_ctx - fsdp_id % n_ctx) % n_ctx


def turn(field, cos_t, sin_t):
    return field * cos_t + pltpu.roll(field, HD // 2, 1) * sin_t


def head_lanes(head, heads):
    return pl.ds(pl.multiple_of(jnp.minimum(head, heads - 1) * HD, HD), HD)


def norm_scales(stats, channels):
    mean = stats * (1.0 / channels)
    inv = lax.rsqrt(mean[0:2] + eps_norm)
    inv_q, inv_k = as_column(inv[0:1]), as_column(inv[1:2])
    tilt = inv * inv * inv * mean[2:4]
    return inv_q, inv_k, as_column(tilt[0:1]), as_column(tilt[1:2])


def pack_kernel(n_ctx, heads, *refs):
    order_hbm, gain_hbms, field_hbms = refs[0], refs[1:3], refs[3:9]
    stats_ref, gain_refs, block_refs = refs[9], refs[10:12], refs[12 : 12 + n_ctx]
    order_ref, line_refs, field_refs, sems = refs[12 + n_ctx], refs[13 + n_ctx : 15 + n_ctx], refs[15 + n_ctx : -1], refs[-1]
    sources = (*field_hbms, order_hbm, *gain_hbms)
    targets = (*field_refs, order_ref, *line_refs)
    copies = [pltpu.make_async_copy(a, b, sems.at[at]) for at, (a, b) in enumerate(zip(sources, targets))]
    for copy in copies:
        copy.start()
    ctx_id, fsdp_id = lax.axis_index("ctx"), lax.axis_index("fsdp")
    rows = field_refs[0].shape[0]
    for copy in copies:
        copy.wait()
    order = jnp.full((ORDER_ROWS, HD), order_ref[0].astype(F32), F32).astype(BF16)
    for dist, block in enumerate(block_refs):
        lanes = head_lanes(hosted_head(ctx_id ^ dist, fsdp_id, n_ctx), heads)
        for at, ref in enumerate(field_refs):
            block[at * rows : (at + 1) * rows, :] = ref[:, lanes]
        block[6 * rows :, :] = order
    q, k, qt, kt = (field_refs[at][...].astype(F32) for at in (0, 1, 3, 4))
    for at, product in enumerate((q * q, k * k, q * qt, k * kt)):
        stats_ref[at : at + 1, :] = as_row(jnp.sum(product, axis=1, keepdims=True))
    for gain_ref, line_ref in zip(gain_refs, line_refs):
        gain_ref[...] = line_ref[...].reshape(gain_ref.shape)


def forward_kernel(n_ctx, n_fsdp, heads, channels, *refs):
    time_ref, gain_q_ref, gain_k_ref, table_ref = refs[:4]
    block_refs = refs[4 : 4 + n_ctx]
    stats_refs = refs[4 + n_ctx : 4 + 2 * n_ctx]
    energy_ref, qcat_ref, kcat_ref, vcat_ref, out_ref, goal_ref, lse_ref, turn_ref = refs[4 + 2 * n_ctx : -2]
    slots_ref, sem = refs[-2:]
    copy = pltpu.make_async_copy(time_ref, slots_ref, sem)
    copy.start()
    ctx_id, fsdp_id = lax.axis_index("ctx"), lax.axis_index("fsdp")
    head = hosted_head(ctx_id, fsdp_id, n_ctx)
    active = head < heads
    lanes = head_lanes(head, heads)
    gain_q, gain_k = gain_q_ref[:, lanes], gain_k_ref[:, lanes]
    rows = (block_refs[0].shape[0] - ORDER_ROWS) // 6
    inv_root = HD ** (-0.5)
    for dist, block in enumerate(block_refs):
        here = slice(dist * rows, (dist + 1) * rows)
        inv_q, inv_k, tilt_q, tilt_k = norm_scales(stats_refs[dist][...], channels)
        order = block[6 * rows : 6 * rows + 1, :].astype(F32)
        both = table_ref[0:rows, :]
        for other in range(1, n_ctx):
            both = jnp.where(order == float(other), table_ref[other * rows : (other + 1) * rows, :], both)
        swapped = pltpu.roll(both, HD // 2, 1)
        low = lax.broadcasted_iota(jnp.int32, (rows, HD), 1) < HD // 2
        cos_t = jnp.where(low, both, swapped)
        sin_t = jnp.where(low, -swapped, both)
        turn_ref[here, 0:HD] = cos_t
        turn_ref[here, HD:] = sin_t

        def part(at):
            return block[at * rows : (at + 1) * rows, :]

        q, k = part(0).astype(F32), part(1).astype(F32)
        qt, kt = part(3).astype(F32), part(4).astype(F32)
        qcat_ref[here, HD:] = turn(q * inv_q * gain_q, cos_t, sin_t).astype(BF16)
        qcat_ref[here, 0:HD] = turn((qt * inv_q - q * tilt_q) * gain_q, cos_t, sin_t).astype(BF16)
        kcat_ref[here, 0:HD] = turn(k * inv_k * gain_k, cos_t, sin_t).astype(BF16)
        kcat_ref[here, HD:] = turn((kt * inv_k - k * tilt_k) * gain_k, cos_t, sin_t).astype(BF16)
        vcat_ref[here, 0:HD] = part(2)
        vcat_ref[here, HD:] = part(5)
    copy.wait()
    picked = slots_ref[fsdp_id // (channels // (heads * HD))].astype(F32)
    angle_t = jnp.full((8, HD), 0.5 * math.pi * (picked + 0.5) / STEPS)
    coef_out = (jnp.sin(angle_t) * jnp.cos(angle_t))[0:1]
    coef_tan = (jnp.cos(angle_t) ** 2)[0:1]
    for dist in range(n_ctx):
        here = slice(dist * rows, (dist + 1) * rows)
        scores = mm(qcat_ref[here, HD:], kcat_ref[:, 0:HD], NT) * inv_root
        slopes = mm(qcat_ref[here, :], kcat_ref[...], NT) * inv_root
        peak = jnp.max(scores, axis=1, keepdims=True)
        weights = jnp.exp(scores - peak)
        totals = jnp.sum(weights, axis=1, keepdims=True)
        tilted = weights * slopes
        numer = mm(weights.astype(BF16), vcat_ref[...], NN)
        numer_tan = numer[:, HD:] + mm(tilted.astype(BF16), vcat_ref[:, 0:HD], NN)
        tilt = jnp.sum(tilted, axis=1, keepdims=True)
        output = numer[:, 0:HD] / totals
        output_tan = numer_tan / totals - (tilt / totals) * output
        goal = coef_out * output + coef_tan * output_tan
        out_ref[here, :] = output
        goal_ref[here, :] = goal
        lse_ref[here, :] = jnp.broadcast_to(peak + jnp.log(totals), (rows, HD))
        row = as_row(jnp.sum(goal * goal, axis=1, keepdims=True))
        energy_ref[0, pl.ds(ctx_id ^ dist, 1), :] = jnp.where(active, row, 0.0)
    first = energy_ref[0]
    for at in range(1, energy_ref.shape[0]):
        energy_ref[at] = first


def backward_kernel(n_ctx, n_fsdp, heads, channels, *refs):
    energy_ref, gain_q_ref, gain_k_ref, qcat_ref, kcat_ref, vcat_ref = refs[:6]
    out_ref, goal_ref, lse_ref, turn_ref = refs[6:10]
    block_refs = refs[10 : 10 + n_ctx]
    stats_refs = refs[10 + n_ctx : 10 + 2 * n_ctx]
    cross_ref = refs[10 + 2 * n_ctx]
    back_refs = refs[11 + 2 * n_ctx : 11 + 3 * n_ctx]
    probs_ref, dscore_ref, cot_ref = refs[11 + 3 * n_ctx :]
    ctx_id, fsdp_id = lax.axis_index("ctx"), lax.axis_index("fsdp")
    head = hosted_head(ctx_id, fsdp_id, n_ctx)
    active = head < heads
    head_split = channels // (heads * HD)
    sample = fsdp_id // head_split
    lanes = head_lanes(head, heads)
    gain_q, gain_k = gain_q_ref[:, lanes], gain_k_ref[:, lanes]
    rows = (block_refs[0].shape[0] - ORDER_ROWS) // 6
    inv_root = HD ** (-0.5)
    energy = jnp.zeros((n_ctx, rows), F32)
    for ctx_at in range(n_ctx):
        energy = energy + jnp.sum(energy_ref[pl.ds(ctx_at * n_fsdp + sample * head_split, head_split)], axis=0)
    level = loss_scale / (jnp.sqrt(energy * (1.0 / channels)) + floor_term)
    block_ids = lax.broadcasted_iota(jnp.int32, (n_ctx, rows), 0)
    gain_q_sum = jnp.zeros((1, HD), F32)
    gain_k_sum = jnp.zeros((1, HD), F32)
    crosses = []
    for dist in range(n_ctx):
        here = slice(dist * rows, (dist + 1) * rows)
        owner = ctx_id ^ dist
        scale = as_column(jnp.sum(jnp.where(block_ids == owner, level, 0.0), axis=0, keepdims=True))
        output = out_ref[here, :]
        cot = (scale * goal_ref[here, :]).astype(BF16)
        drift = jnp.sum(cot.astype(F32) * output, axis=1, keepdims=True)
        scores = mm(qcat_ref[here, HD:], kcat_ref[:, 0:HD], NT) * inv_root
        probs = jnp.exp(scores - lse_ref[here, 0:1])
        dprobs = mm(cot, vcat_ref[:, 0:HD], NT)
        dscore = (probs * (dprobs - drift) * inv_root).astype(BF16)
        probs_ref[here, :] = probs.astype(BF16)
        dscore_ref[here, :] = dscore
        cot_ref[here, :] = cot
        dquery = mm(dscore, kcat_ref[:, 0:HD], NN)
        inv_q = norm_scales(stats_refs[dist][...], channels)[0]
        x = block_refs[dist][0:rows, :].astype(F32)
        dy = turn(dquery, turn_ref[here, 0:HD], -turn_ref[here, HD:])
        grown = gain_q * dy
        back_refs[dist][0:rows, :] = grown.astype(BF16)
        crosses.append(as_row(jnp.sum(x * grown, axis=1, keepdims=True)))
        gain_q_sum = gain_q_sum + jnp.sum(dy * x * inv_q, axis=0, keepdims=True)
    for dist in range(n_ctx):
        here = slice(dist * rows, (dist + 1) * rows)
        back_refs[dist][2 * rows : 3 * rows, :] = mm(probs_ref[:, here], cot_ref[...], TN).astype(BF16)
        dkey = mm(dscore_ref[:, here], qcat_ref[:, HD:], TN)
        inv_k = norm_scales(stats_refs[dist][...], channels)[1]
        x = block_refs[dist][rows : 2 * rows, :].astype(F32)
        dy = turn(dkey, turn_ref[here, 0:HD], -turn_ref[here, HD:])
        grown = gain_k * dy
        back_refs[dist][rows : 2 * rows, :] = grown.astype(BF16)
        cross_k = as_row(jnp.sum(x * grown, axis=1, keepdims=True))
        gain_k_sum = gain_k_sum + jnp.sum(dy * x * inv_k, axis=0, keepdims=True)
        crosses[dist] = jnp.concatenate([crosses[dist], cross_k], axis=0)
    for dist in range(n_ctx):
        sums = jnp.concatenate([crosses[dist], gain_q_sum, gain_k_sum], axis=0)
        sums = jnp.where(active, sums, 0.0)
        start = (ctx_id ^ dist) * n_fsdp
        for at in range(n_fsdp):
            cross_ref[start + at] = sums


def finish_kernel(n_ctx, n_fsdp, heads, channels, *refs):
    stats_ref, cross_ref, q_ref, k_ref = refs[:4]
    back_refs = refs[4 : 4 + n_ctx]
    dq_ref, dk_ref, dv_ref, dgain_q_ref, dgain_k_ref, gain_q_ref, gain_k_ref = refs[4 + n_ctx :]
    ctx_id, fsdp_id = lax.axis_index("ctx"), lax.axis_index("fsdp")
    head_split = channels // (heads * HD)
    sample = fsdp_id // head_split
    rows = q_ref.shape[0]
    inv_q, inv_k, _, _ = norm_scales(stats_ref[...], channels)
    total = jnp.zeros((4, rows), F32)
    for ctx_at in range(n_ctx):
        total = total + jnp.sum(cross_ref[pl.ds(ctx_at * n_fsdp + sample * head_split, head_split)], axis=0)
    mean = total[0:2] * (1.0 / channels)
    tilt_q = inv_q * inv_q * inv_q * as_column(mean[0:1])
    tilt_k = inv_k * inv_k * inv_k * as_column(mean[1:2])
    for dist in range(n_ctx):
        host = ctx_id ^ dist
        head = hosted_head(host, fsdp_id, n_ctx)

        @pl.when(head < heads)
        def _(dist=dist, host=host, head=head):
            back = back_refs[dist]
            lanes = head_lanes(head, heads)
            h_q, h_k = back[0:rows, :].astype(F32), back[rows : 2 * rows, :].astype(F32)
            dq_ref[:, lanes] = (inv_q * h_q - q_ref[:, lanes].astype(F32) * tilt_q).astype(BF16)
            dk_ref[:, lanes] = (inv_k * h_k - k_ref[:, lanes].astype(F32) * tilt_k).astype(BF16)
            dv_ref[:, lanes] = back[2 * rows : 3 * rows, :]
            sums = cross_ref[host * n_fsdp + fsdp_id]
            gain_q_ref[:, lanes] = sums[2:3]
            gain_k_ref[:, lanes] = sums[3:4]

    dgain_q_ref[...] = gain_q_ref[...].reshape(dgain_q_ref.shape)
    dgain_k_ref[...] = gain_k_ref[...].reshape(dgain_k_ref.shape)


def per_device(
    queries,
    keys,
    values,
    query_tangent,
    key_tangent,
    value_tangent,
    query_gain,
    key_gain,
    time_index,
    shard_order,
):
    n_ctx, n_fsdp = lax.axis_size("ctx"), lax.axis_size("fsdp")
    n_all = n_ctx * n_fsdp
    fsdp_id = lax.axis_index("fsdp")
    rows, ch_dev = queries.shape
    heads = ch_dev // HD
    channels = query_gain.shape[0] * n_fsdp
    head_split = channels // ch_dev
    seq = rows * n_ctx
    sizes = (n_ctx, n_fsdp, heads, channels)

    vmem = pl.BlockSpec(memory_space=pltpu.VMEM)

    hbm = pl.BlockSpec(memory_space=pltpu.HBM)

    def kernel(body, ins, outs, scratch=(), flops=10**8, from_hbm=0):
        return pl.pallas_call(
            body,
            out_shape=[jax.ShapeDtypeStruct(*o) for o in outs],
            in_specs=[hbm] * from_hbm + [vmem] * (len(ins) - from_hbm),
            out_specs=[vmem] * len(outs),
            scratch_shapes=list(scratch),
            cost_estimate=pl.CostEstimate(flops=flops, bytes_accessed=2**20, transcendentals=0),
            compiler_params=pltpu.CompilerParams(vmem_limit_bytes=20 * 2**20 + seq * 2**13),
        )(*ins)

    def in_hbm(array):
        return pltpu.with_memory_space_constraint(array, pltpu.HBM)

    def swap(block, axis, dist):
        return lax.ppermute(block, axis, [(i, i ^ dist) for i in range(lax.axis_size(axis))])

    def sum_over_sample(block):
        block = block + swap(block, "fsdp", 1)
        return sum([swap(block, "fsdp", d) for d in range(2, head_split, 2)], block)

    def from_peers(blocks):
        out = [blocks[0]] + [None] * (n_ctx - 1)
        for dist in reversed(range(1, n_ctx)):
            out[dist] = swap(blocks[dist], "ctx", dist)
        return out

    places = np.arange(seq, dtype=np.float32)
    freqs = (rope_base ** (-np.arange(HD // 2) / (HD // 2))).astype(np.float32)
    angles = (places[:, None] * freqs[None, :]).astype(np.float64)
    table = jnp.asarray(np.concatenate([np.cos(angles), np.sin(angles)], axis=1).astype(np.float32))

    gains = (query_gain, key_gain)
    if query_gain.shape[0] != ch_dev:
        start = (fsdp_id % head_split) * ch_dev
        gains = [lax.all_gather(g, "fsdp", axis=0, tiled=True) for g in gains]
        gains = [lax.dynamic_slice_in_dim(g, start, ch_dev, 0) for g in gains]

    fields = (queries, keys, values, query_tangent, key_tangent, value_tangent)
    gains = [in_hbm(a) for a in gains]
    fields = [in_hbm(a) for a in fields]
    part, gain_q, gain_k, *blocks = kernel(
        functools.partial(pack_kernel, n_ctx, heads),
        (shard_order, *gains, *fields),
        [((4, rows), F32)] + [((1, ch_dev), F32)] * 2 + [((6 * rows + ORDER_ROWS, HD), BF16)] * n_ctx,
        scratch=[pltpu.SMEM((1,), jnp.int32)]
        + [pltpu.VMEM((ch_dev,), F32)] * 2
        + [pltpu.VMEM((rows, ch_dev), BF16)] * 6
        + [pltpu.SemaphoreType.DMA((9,))],
        from_hbm=9,
    )
    gains = (gain_q, gain_k)
    blocks = from_peers(blocks)
    stats = from_peers([sum_over_sample(part)] * n_ctx)

    energy_out, qcat, kcat, vcat, output, goal, lse, turns = kernel(
        functools.partial(forward_kernel, *sizes),
        (time_index, *gains, table, *blocks, *stats),
        [((n_all, n_ctx, rows), F32)]
        + [((seq, 2 * HD), BF16)] * 3
        + [((seq, HD), F32)] * 3
        + [((seq, 2 * HD), F32)],
        scratch=[pltpu.SMEM(time_index.shape, jnp.int32), pltpu.SemaphoreType.DMA],
        from_hbm=1,
    )
    energy = lax.all_to_all(energy_out, BOTH, 0, 0)

    cross_out, *back = kernel(
        functools.partial(backward_kernel, *sizes),
        (energy, *gains, qcat, kcat, vcat, output, goal, lse, turns, *blocks, *stats),
        [((n_all, 4, rows), F32)] + [((3 * rows, HD), BF16)] * n_ctx,
        scratch=[
            pltpu.VMEM((seq, seq), BF16),
            pltpu.VMEM((seq, seq), BF16),
            pltpu.VMEM((seq, HD), BF16),
        ],
    )
    back = from_peers(back)
    crosses = lax.all_to_all(cross_out, BOTH, 0, 0)

    query_grad, key_grad, value_grad, *gain_grads = kernel(
        functools.partial(finish_kernel, *sizes),
        (stats[0], crosses, queries, keys, *back),
        [((rows, ch_dev), BF16)] * 3 + [((ch_dev,), F32)] * 2,
        scratch=[pltpu.VMEM((1, ch_dev), F32)] * 2,
    )
    if query_gain.shape[0] != ch_dev:
        placed = [
            lax.dynamic_update_slice_in_dim(jnp.zeros((channels,), F32), g, start, 0) for g in gain_grads
        ]
        gain_grads = [lax.psum_scatter(g, "fsdp", scatter_dimension=0, tiled=True) for g in placed]
    return (query_grad, key_grad, value_grad, *gain_grads)


def solution(mesh):
    placed = (P("ctx", "fsdp"),) * 6 + (P("fsdp"), P("fsdp"), P(), P("ctx"))
    return jax.shard_map(
        per_device,
        mesh=mesh,
        in_specs=placed,
        out_specs=(P("ctx", "fsdp"), P("ctx", "fsdp"), P("ctx", "fsdp"), P("fsdp"), P("fsdp")),
        check_vma=False,
    )
```

time: 70.4 us -> 56.5 us (0.80)
  the two profiles are of different devices: /device:TPU:8 before, /device:TPU:0 now
where the time goes in v2:
time: 56.5 us; the launch traced here: 56.2 us
  starting transfers between devices  20.4 us (36%)
  waiting for transfers between devices  12.9 us (23%)
  blocking collectives  12 us (21%)
  Pallas kernels  8.92 us (16%)
  between operations  2.01 us (4%)
    ppermute x13, starting transfers between devices, swap(): lax.ppermute(block, axis, [(i, i ^ dist) for i in range(lax.axis_size(axi...  17.7 us
    ppermute x13, waiting for transfers between devices, swap(): lax.ppermute(block, axis, [(i, i ^ dist) for i in range(lax.axis_size(axi...  12.9 us
    all_to_all x1, blocking collectives, per_device(): energy = lax.all_to_all(energy_out, BOTH, 0, 0)  12 us
    pallas_call x4, Pallas kernels, kernel(): pl.pallas_call(body, out_shape=[jax.ShapeDtypeStruct(*o) for o in outs],...  8.92 us
    all_to_all x1, starting transfers between devices, per_device(): crosses = lax.all_to_all(cross_out, BOTH, 0, 0)  2.7 us
  transfers between devices with their start and end apart: 14, of which 6 were waited for; matrix products, arithmetic and copies ran while one was open for 0% of the time, Pallas kernels for 0%

profile of v2, /device:TPU:0, one launch (start us, length us, event | category | flops | bytes accessed | tf_op | source)
XLA Modules:
  0.0 56.2 jit_solution(9063485115760827378)
XLA Ops:
  1.3 1.5 %shard_map.146 = (f32[4,128]{1,0:T(4,128)S(1)}, f32[1,384]{1,0:T(1,128)S(1)}, f32[1,384]{1,0:T(1,128)S(1)}, bf16[784,128]{1,0:T(8,128)(2,1)S(1)}, bf16[784,128]{...) custom-call(s32[1]{0:T(128)S(6)} %copy.17.refs_0_, f32[384]{0:T(512)} %refs_1_.1, ...), custom_call_target="tpu_custom_call" | custom-call | flops 100000000 | bytes 1048576 | tf_op jit(solution)/shard_map/pallas_call | solution.py:292
  2.8 0.6 collective-permute-start
  3.3 0.8 %collective-permute-done = f32[4,128]{1,0:T(4,128)S(1)} collective-permute-done((f32[4,128]{1,0:T(4,128)S(1)}, f32[4,128]{1,0:T(4,128)S(1)}, u32[]{:S(2)}, u32[]{:S(2)}) %collective-permute-start) | collective-permute-done | bytes 2080 | tf_op jit(solution)/shard_map/ppermute | solution.py:306
  4.2 4.9 %collective-permute-start.3 = (f32[4,128]{1,0:T(4,128)S(1)}, f32[4,128]{1,0:T(4,128)S(1)}, u32[]{:S(2)}, u32[]{:S(2)}) collective-permute-start(f32[4,128]{1,0:T(4,128)S(1)} %add.12), channel_id=1, source_target_pairs={{0,6},{1,7},{2,4},{3,5},{4,2},{5,3},{6,0},{7,1},{8,14},{9,15},{10,... | collective-permute-start | bytes 6152 | tf_op jit(solution)/shard_map/ppermute | solution.py:306
  9.1 0.6 %collective-permute-start.1 = (f32[4,128]{1,0:T(4,128)S(1)}, f32[4,128]{1,0:T(4,128)S(1)}, u32[]{:S(2)}, u32[]{:S(2)}) collective-permute-start(f32[4,128]{1,0:T(4,128)S(1)} %add.12), channel_id=1, source_target_pairs={{0,2},{1,3},{2,0},{3,1},{4,6},{5,7},{6,4},{7,5},{8,10},{9,11},{10,... | collective-permute-start | bytes 6152 | tf_op jit(solution)/shard_map/ppermute | solution.py:306
  9.7 1.7 %collective-permute-start.4 = (bf16[784,128]{1,0:T(8,128)(2,1)S(1)}, bf16[784,128]{1,0:T(8,128)(2,1)S(1)}, u32[]{:S(2)}, u32[]{:S(2)}) collective-permute-start(bf16[784,128]{1,0:T(8,128)(2,1)S(1)} %get-tuple-element.29), channel_id=1, source_target_pairs={{0,8},{8,0},{16,24},{24,16},{1,9},{9,1},{17,25},{25,17},{2,10},{10... | collective-permute-start | bytes 602120 | tf_op jit(solution)/shard_map/ppermute | solution.py:306
  11.4 1.5 %collective-permute-start.5 = (bf16[784,128]{1,0:T(8,128)(2,1)S(1)}, bf16[784,128]{1,0:T(8,128)(2,1)S(1)}, u32[]{:S(2)}, u32[]{:S(2)}) collective-permute-start(bf16[784,128]{1,0:T(8,128)(2,1)S(1)} %get-tuple-element.30), channel_id=1, source_target_pairs={{0,16},{8,24},{16,0},{24,8},{1,17},{9,25},{17,1},{25,9},{2,18},{10... | collective-permute-start | bytes 602120 | tf_op jit(solution)/shard_map/ppermute | solution.py:306
  12.9 0.4 collective-permute-start.6
  13.3 0.3 collective-permute-done.2
  13.6 2.5 %collective-permute-start.9 = (f32[4,128]{1,0:T(4,128)S(1)}, f32[4,128]{1,0:T(4,128)S(1)}, u32[]{:S(2)}, u32[]{:S(2)}) collective-permute-start(f32[4,128]{1,0:T(4,128)S(1)} %add_add_fusion.refs_8_.refs_14_.refs_0_), channel_id=1, source_target_pairs={{0,24},{8,16},{16,8},{24,0},{1,25},{9,17},{17,9},{25,1},{2,26},{10... | collective-permute-start | bytes 6152 | tf_op jit(solution)/shard_map/ppermute | solution.py:306
  16.1 0.5 collective-permute-start.8
  16.6 5.0 %collective-permute-done.9.refs_11_.refs_17_ = f32[4,128]{1,0:T(4,128)S(1)} collective-permute-done((f32[4,128]{1,0:T(4,128)S(1)}, f32[4,128]{1,0:T(4,128)S(1)}, u32[]{:S(2)}, u32[]{:S(2)}) %collective-permute-start.9) | collective-permute-done | bytes 2080 | tf_op jit(solution)/shard_map/ppermute | solution.py:306
  21.6 1.4 %collective-permute-start.7 = (f32[4,128]{1,0:T(4,128)S(1)}, f32[4,128]{1,0:T(4,128)S(1)}, u32[]{:S(2)}, u32[]{:S(2)}) collective-permute-start(f32[4,128]{1,0:T(4,128)S(1)} %add_add_fusion.refs_8_.refs_14_.refs_0_), channel_id=1, source_target_pairs={{0,8},{8,0},{16,24},{24,16},{1,9},{9,1},{17,25},{25,17},{2,10},{10... | collective-permute-start | bytes 6152 | tf_op jit(solution)/shard_map/ppermute | solution.py:306
  23.6 1.5 %collective-permute-done.7.refs_9_.refs_15_ = f32[4,128]{1,0:T(4,128)S(1)} collective-permute-done((f32[4,128]{1,0:T(4,128)S(1)}, f32[4,128]{1,0:T(4,128)S(1)}, u32[]{:S(2)}, u32[]{:S(2)}) %collective-permute-start.7) | collective-permute-done | bytes 2080 | tf_op jit(solution)/shard_map/ppermute | solution.py:306
  25.2 3.0 %shard_map.147 = (f32[32,4,128]{2,1,0:T(4,128)S(1)}, bf16[512,256]{1,0:T(8,128)(2,1)S(1)}, bf16[512,256]{1,0:T(8,128)(2,1)S(1)}, bf16[512,256]{1,0:T(8,128)(2,1)...) custom-call(s32[1]{0:T(128)S(6)} %copy.16.refs_0_, ...), custom_call_target="tpu_custom_call" | custom-call | flops 100000000 | bytes 1048576 | tf_op jit(solution)/shard_map/pallas_call | solution.py:292
  28.2 12.0 %all_to_all.10.refs_0_ = f32[32,4,128]{2,1,0:T(4,128)S(1)} all-to-all(f32[32,4,128]{2,1,0:T(4,128)S(1)} %get-tuple-element.32), channel_id=1, replica_groups=mesh['ctx'=4,'fsdp'=8] {'ctx','fsdp'}, dimensions={0} | all-to-all | bytes 131072 | tf_op jit(solution)/shard_map/all_to_all | solution.py:356
  40.2 3.4 %shard_map.148 = (f32[32,4,128]{2,1,0:T(4,128)}, bf16[384,128]{1,0:T(8,128)(2,1)S(1)}, bf16[384,128]{1,0:T(8,128)(2,1)S(1)}, bf16[384,128]{1,0:T(8,128)(2,1)S(1)}, bf16[384,128]{1,0:T(8,128)(2,1)S(1)}) custom-call(f32[32,4,128]{2,1,0:T(4,128)S(1)} %all_to_all.10.refs_0_, f32[1,384]{1,0:T(1,128)S(1)} %get-tuple-element.26.refs_1_, ...), custom_call_target="tpu_custom_call" | custom-call | flops 100000000 | bytes 1048576 | tf_op jit(solution)/shard_map/pallas_call | solution.py:292
  43.6 2.7 %all-to-all-start.1 = ((f32[32,4,128]{2,1,0:T(4,128)}), f32[32,4,128]{2,1,0:T(4,128)S(1)}, u32[]{:S(2)}, u32[]{:S(2)}) async-start(f32[32,4,128]{2,1,0:T(4,128)} %get-tuple-element.40), calls=%async_computation.1 | async-start | bytes 131072 | tf_op jit(solution)/shard_map/all_to_all | solution.py:369
  46.3 1.7 %collective-permute-start.10 = (bf16[384,128]{1,0:T(8,128)(2,1)S(1)}, bf16[384,128]{1,0:T(8,128)(2,1)S(1)}, u32[]{:S(2)}, u32[]{:S(2)}) collective-permute-start(bf16[384,128]{1,0:T(8,128)(2,1)S(1)} %get-tuple-element.42), channel_id=1, source_target_pairs={{0,8},{8,0},{16,24},{24,16},{1,9},{9,1},{17,25},{25,17},{2,10},{10... | collective-permute-start | bytes 294920 | tf_op jit(solution)/shard_map/ppermute | solution.py:306
  48.0 1.5 %collective-permute-start.11 = (bf16[384,128]{1,0:T(8,128)(2,1)S(1)}, bf16[384,128]{1,0:T(8,128)(2,1)S(1)}, u32[]{:S(2)}, u32[]{:S(2)}) collective-permute-start(bf16[384,128]{1,0:T(8,128)(2,1)S(1)} %get-tuple-element.43), channel_id=1, source_target_pairs={{0,16},{8,24},{16,0},{24,8},{1,17},{9,25},{17,1},{25,9},{2,18},{10... | collective-permute-start | bytes 294920 | tf_op jit(solution)/shard_map/ppermute | solution.py:306
  49.5 0.4 collective-permute-start.12
  49.9 1.7 %collective-permute-done.10.refs_5_ = bf16[384,128]{1,0:T(8,128)(2,1)S(1)} collective-permute-done((bf16[384,128]{1,0:T(8,128)(2,1)S(1)}, bf16[384,128]{1,0:T(8,128)(2,1)S(1)}, u32[]{:S(2)}, u32[]{:S(2)}) %collective-permute-start.10) | collective-permute-done | bytes 98336 | tf_op jit(solution)/shard_map/ppermute | solution.py:306
  51.6 3.6 %collective-permute-done.11.refs_6_ = bf16[384,128]{1,0:T(8,128)(2,1)S(1)} collective-permute-done((bf16[384,128]{1,0:T(8,128)(2,1)S(1)}, bf16[384,128]{1,0:T(8,128)(2,1)S(1)}, u32[]{:S(2)}, u32[]{:S(2)}) %collective-permute-start.11) | collective-permute-done | bytes 98336 | tf_op jit(solution)/shard_map/ppermute | solution.py:306
  55.2 1.0 %shard_map.149 = (bf16[128,384]{1,0:T(8,128)(2,1)}, bf16[128,384]{1,0:T(8,128)(2,1)}, bf16[128,384]{1,0:T(8,128)(2,1)}, f32[384]{0:T(512)}, f32[384]{0:T(512)}) custom-call(f32[4,128]{1,0:T(4,128)S(1)} %add_add_fusion.refs_8_.refs_14_.refs_0_, f32[32,4,128]{2,1,0:T(4,128)S(1)} %all-to-all-done.1.refs_1_, bf16[128,384]{1,0:T(8,128)(2,1)S(1)} %copy-done, ...), custom_call_target="tpu_custom_call" | custom-call | flops 100000000 | bytes 1048576 | tf_op jit(solution)/shard_map/pallas_call | solution.py:292
  (17 shorter events, 0.0 us)
Async XLA Ops:
  1.3 23.9 %copy-start.2 = (f32[512,128]{1,0:T(8,128)S(1)}, f32[512,128]{1,0:T(8,128)}, u32[]{:S(2)}) copy-start(f32[512,128]{1,0:T(8,128)} %constant.2.clone.refs_3_) | copy-start | bytes 786436
  2.8 1.4 %collective-permute-start = (f32[4,128]{1,0:T(4,128)S(1)}, f32[4,128]{1,0:T(4,128)S(1)}, u32[]{:S(2)}, u32[]{:S(2)}) collective-permute-start(f32[4,128]{1,0:T(4,128)S(1)} %get-tuple-element.25), channel_id=1, source_target_pairs={{0,1},{1,0},{2,3},{3,2},{4,5},{5,4},{6,7},{7,6},{8,9},{9,8},{10,11... | collective-permute-start | bytes 6152 | tf_op jit(solution)/shard_map/ppermute | solution.py:306
  4.2 8.7 %collective-permute-start.3 = (f32[4,128]{1,0:T(4,128)S(1)}, f32[4,128]{1,0:T(4,128)S(1)}, u32[]{:S(2)}, u32[]{:S(2)}) collective-permute-start(f32[4,128]{1,0:T(4,128)S(1)} %add.12), channel_id=1, source_target_pairs={{0,6},{1,7},{2,4},{3,5},{4,2},{5,3},{6,0},{7,1},{8,14},{9,15},{10,... | collective-permute-start | bytes 6152 | tf_op jit(solution)/shard_map/ppermute | solution.py:306
  9.1 4.5 %collective-permute-start.2 = (f32[4,128]{1,0:T(4,128)S(1)}, f32[4,128]{1,0:T(4,128)S(1)}, u32[]{:S(2)}, u32[]{:S(2)}) collective-permute-start(f32[4,128]{1,0:T(4,128)S(1)} %add.12), channel_id=1, source_target_pairs={{0,4},{1,5},{2,6},{3,7},{4,0},{5,1},{6,2},{7,3},{8,12},{9,13},{10,... | collective-permute-start | bytes 6152 | tf_op jit(solution)/shard_map/ppermute | solution.py:306
  9.1 4.5 %collective-permute-start.1 = (f32[4,128]{1,0:T(4,128)S(1)}, f32[4,128]{1,0:T(4,128)S(1)}, u32[]{:S(2)}, u32[]{:S(2)}) collective-permute-start(f32[4,128]{1,0:T(4,128)S(1)} %add.12), channel_id=1, source_target_pairs={{0,2},{1,3},{2,0},{3,1},{4,6},{5,7},{6,4},{7,5},{8,10},{9,11},{10,... | collective-permute-start | bytes 6152 | tf_op jit(solution)/shard_map/ppermute | solution.py:306
  9.7 15.5 %collective-permute-start.4 = (bf16[784,128]{1,0:T(8,128)(2,1)S(1)}, bf16[784,128]{1,0:T(8,128)(2,1)S(1)}, u32[]{:S(2)}, u32[]{:S(2)}) collective-permute-start(bf16[784,128]{1,0:T(8,128)(2,1)S(1)} %get-tuple-element.29), channel_id=1, source_target_pairs={{0,8},{8,0},{16,24},{24,16},{1,9},{9,1},{17,25},{25,17},{2,10},{10... | collective-permute-start | bytes 602120 | tf_op jit(solution)/shard_map/ppermute | solution.py:306
  11.4 13.8 %collective-permute-start.5 = (bf16[784,128]{1,0:T(8,128)(2,1)S(1)}, bf16[784,128]{1,0:T(8,128)(2,1)S(1)}, u32[]{:S(2)}, u32[]{:S(2)}) collective-permute-start(bf16[784,128]{1,0:T(8,128)(2,1)S(1)} %get-tuple-element.30), channel_id=1, source_target_pairs={{0,16},{8,24},{16,0},{24,8},{1,17},{9,25},{17,1},{25,9},{2,18},{10... | collective-permute-start | bytes 602120 | tf_op jit(solution)/shard_map/ppermute | solution.py:306
  12.9 12.3 %collective-permute-start.6 = (bf16[784,128]{1,0:T(8,128)(2,1)S(1)}, bf16[784,128]{1,0:T(8,128)(2,1)S(1)}, u32[]{:S(2)}, u32[]{:S(2)}) collective-permute-start(bf16[784,128]{1,0:T(8,128)(2,1)S(1)} %get-tuple-element.31), channel_id=1, source_target_pairs={{0,24},{8,16},{16,8},{24,0},{1,25},{9,17},{17,9},{25,1},{2,26},{10... | collective-permute-start | bytes 602120 | tf_op jit(solution)/shard_map/ppermute | solution.py:306
  13.6 8.0 %collective-permute-start.9 = (f32[4,128]{1,0:T(4,128)S(1)}, f32[4,128]{1,0:T(4,128)S(1)}, u32[]{:S(2)}, u32[]{:S(2)}) collective-permute-start(f32[4,128]{1,0:T(4,128)S(1)} %add_add_fusion.refs_8_.refs_14_.refs_0_), channel_id=1, source_target_pairs={{0,24},{8,16},{16,8},{24,0},{1,25},{9,17},{17,9},{25,1},{2,26},{10... | collective-permute-start | bytes 6152 | tf_op jit(solution)/shard_map/ppermute | solution.py:306
  16.1 7.5 %collective-permute-start.8 = (f32[4,128]{1,0:T(4,128)S(1)}, f32[4,128]{1,0:T(4,128)S(1)}, u32[]{:S(2)}, u32[]{:S(2)}) collective-permute-start(f32[4,128]{1,0:T(4,128)S(1)} %add_add_fusion.refs_8_.refs_14_.refs_0_), channel_id=1, source_target_pairs={{0,16},{8,24},{16,0},{24,8},{1,17},{9,25},{17,1},{25,9},{2,18},{10... | collective-permute-start | bytes 6152 | tf_op jit(solution)/shard_map/ppermute | solution.py:306
  21.6 3.6 %collective-permute-start.7 = (f32[4,128]{1,0:T(4,128)S(1)}, f32[4,128]{1,0:T(4,128)S(1)}, u32[]{:S(2)}, u32[]{:S(2)}) collective-permute-start(f32[4,128]{1,0:T(4,128)S(1)} %add_add_fusion.refs_8_.refs_14_.refs_0_), channel_id=1, source_target_pairs={{0,8},{8,0},{16,24},{24,16},{1,9},{9,1},{17,25},{25,17},{2,10},{10... | collective-permute-start | bytes 6152 | tf_op jit(solution)/shard_map/ppermute | solution.py:306
  40.2 15.0 %copy-start.1 = (bf16[128,384]{1,0:T(8,128)(2,1)S(1)}, bf16[128,384]{1,0:T(8,128)(2,1)}, u32[]{:S(2)}) copy-start(bf16[128,384]{1,0:T(8,128)(2,1)} %refs_3_.4) | copy-start | bytes 294916
  43.6 11.6 %copy-start = (bf16[128,384]{1,0:T(8,128)(2,1)S(1)}, bf16[128,384]{1,0:T(8,128)(2,1)}, u32[]{:S(2)}) copy-start(bf16[128,384]{1,0:T(8,128)(2,1)} %refs_2_.3) | copy-start | bytes 294916
  43.6 11.6 %all-to-all-start.1 = ((f32[32,4,128]{2,1,0:T(4,128)}), f32[32,4,128]{2,1,0:T(4,128)S(1)}, u32[]{:S(2)}, u32[]{:S(2)}) async-start(f32[32,4,128]{2,1,0:T(4,128)} %get-tuple-element.40), calls=%async_computation.1 | async-start | bytes 131072 | tf_op jit(solution)/shard_map/all_to_all | solution.py:369
  46.3 5.3 %collective-permute-start.10 = (bf16[384,128]{1,0:T(8,128)(2,1)S(1)}, bf16[384,128]{1,0:T(8,128)(2,1)S(1)}, u32[]{:S(2)}, u32[]{:S(2)}) collective-permute-start(bf16[384,128]{1,0:T(8,128)(2,1)S(1)} %get-tuple-element.42), channel_id=1, source_target_pairs={{0,8},{8,0},{16,24},{24,16},{1,9},{9,1},{17,25},{25,17},{2,10},{10... | collective-permute-start | bytes 294920 | tf_op jit(solution)/shard_map/ppermute | solution.py:306
  48.0 7.2 %collective-permute-start.11 = (bf16[384,128]{1,0:T(8,128)(2,1)S(1)}, bf16[384,128]{1,0:T(8,128)(2,1)S(1)}, u32[]{:S(2)}, u32[]{:S(2)}) collective-permute-start(bf16[384,128]{1,0:T(8,128)(2,1)S(1)} %get-tuple-element.43), channel_id=1, source_target_pairs={{0,16},{8,24},{16,0},{24,8},{1,17},{9,25},{17,1},{25,9},{2,18},{10... | collective-permute-start | bytes 294920 | tf_op jit(solution)/shard_map/ppermute | solution.py:306
  49.5 5.7 %collective-permute-start.12 = (bf16[384,128]{1,0:T(8,128)(2,1)S(1)}, bf16[384,128]{1,0:T(8,128)(2,1)S(1)}, u32[]{:S(2)}, u32[]{:S(2)}) collective-permute-start(bf16[384,128]{1,0:T(8,128)(2,1)S(1)} %get-tuple-element.44), channel_id=1, source_target_pairs={{0,24},{8,16},{16,8},{24,0},{1,25},{9,17},{17,9},{25,1},{2,26},{10... | collective-permute-start | bytes 294920 | tf_op jit(solution)/shard_map/ppermute | solution.py:306

commit v3 on v2

--- a/solution.py
+++ b/solution.py
@@ -51,6 +51,17 @@
 
 def turn(field, cos_t, sin_t):
     return field * cos_t + pltpu.roll(field, HD // 2, 1) * sin_t
+
+
+def turn_back(field, angles):
+    cos_t, sin_t = spread(angles)
+    return turn(field, cos_t, -sin_t)
+
+
+def spread(angles):
+    swapped = pltpu.roll(angles, HD // 2, 1)
+    low = lax.broadcasted_iota(jnp.int32, angles.shape, 1) < HD // 2
+    return jnp.where(low, angles, swapped), jnp.where(low, -swapped, angles)
 
 
 def head_lanes(head, heads):
@@ -94,9 +105,9 @@
 def forward_kernel(n_ctx, n_fsdp, heads, channels, *refs):
     time_ref, gain_q_ref, gain_k_ref, table_ref = refs[:4]
     block_refs = refs[4 : 4 + n_ctx]
-    stats_refs = refs[4 + n_ctx : 4 + 2 * n_ctx]
-    energy_ref, qcat_ref, kcat_ref, vcat_ref, out_ref, goal_ref, lse_ref, turn_ref = refs[4 + 2 * n_ctx : -2]
-    slots_ref, sem = refs[-2:]
+    stats_ref = refs[4 + n_ctx]
+    energy_ref, qn_ref, kn_ref, vn_ref, x_ref, goal_ref, lse_ref, drift_ref, turn_ref = refs[5 + n_ctx : -5]
+    qcat_ref, kcat_ref, vcat_ref, slots_ref, sem = refs[-5:]
     copy = pltpu.make_async_copy(time_ref, slots_ref, sem)
     copy.start()
     ctx_id, fsdp_id = lax.axis_index("ctx"), lax.axis_index("fsdp")
@@ -108,17 +119,13 @@
     inv_root = HD ** (-0.5)
     for dist, block in enumerate(block_refs):
         here = slice(dist * rows, (dist + 1) * rows)
-        inv_q, inv_k, tilt_q, tilt_k = norm_scales(stats_refs[dist][...], channels)
+        inv_q, inv_k, tilt_q, tilt_k = norm_scales(stats_ref[4 * dist : 4 * dist + 4, :], channels)
         order = block[6 * rows : 6 * rows + 1, :].astype(F32)
         both = table_ref[0:rows, :]
         for other in range(1, n_ctx):
             both = jnp.where(order == float(other), table_ref[other * rows : (other + 1) * rows, :], both)
-        swapped = pltpu.roll(both, HD // 2, 1)
-        low = lax.broadcasted_iota(jnp.int32, (rows, HD), 1) < HD // 2
-        cos_t = jnp.where(low, both, swapped)
-        sin_t = jnp.where(low, -swapped, both)
-        turn_ref[here, 0:HD] = cos_t
-        turn_ref[here, HD:] = sin_t
+        turn_ref[here, :] = both
+        cos_t, sin_t = spread(both)
 
         def part(at):
             return block[at * rows : (at + 1) * rows, :]
@@ -131,6 +138,11 @@
         kcat_ref[here, HD:] = turn((kt * inv_k - k * tilt_k) * gain_k, cos_t, sin_t).astype(BF16)
         vcat_ref[here, 0:HD] = part(2)
         vcat_ref[here, HD:] = part(5)
+        vn_ref[here, :] = part(2)
+        x_ref[here, 0:HD] = part(0)
+        x_ref[here, HD:] = part(1)
+    qn_ref[...] = qcat_ref[:, HD:]
+    kn_ref[...] = kcat_ref[:, 0:HD]
     copy.wait()
     picked = slots_ref[fsdp_id // (channels // (heads * HD))].astype(F32)
     angle_t = jnp.full((8, HD), 0.5 * math.pi * (picked + 0.5) / STEPS)
@@ -150,9 +162,11 @@
         output = numer[:, 0:HD] / totals
         output_tan = numer_tan / totals - (tilt / totals) * output
         goal = coef_out * output + coef_tan * output_tan
-        out_ref[here, :] = output
         goal_ref[here, :] = goal
-        lse_ref[here, :] = jnp.broadcast_to(peak + jnp.log(totals), (rows, HD))
+        drift_ref[:, here] = as_row(
+            jnp.sum(goal.astype(BF16).astype(F32) * output, axis=1, keepdims=True)
+        )
+        lse_ref[:, here] = as_row(peak + jnp.log(totals))
         row = as_row(jnp.sum(goal * goal, axis=1, keepdims=True))
         energy_ref[0, pl.ds(ctx_id ^ dist, 1), :] = jnp.where(active, row, 0.0)
     first = energy_ref[0]
@@ -160,67 +174,84 @@
         energy_ref[at] = first
 
 
-def backward_kernel(n_ctx, n_fsdp, heads, channels, *refs):
-    energy_ref, gain_q_ref, gain_k_ref, qcat_ref, kcat_ref, vcat_ref = refs[:6]
-    out_ref, goal_ref, lse_ref, turn_ref = refs[6:10]
-    block_refs = refs[10 : 10 + n_ctx]
-    stats_refs = refs[10 + n_ctx : 10 + 2 * n_ctx]
-    cross_ref = refs[10 + 2 * n_ctx]
-    back_refs = refs[11 + 2 * n_ctx : 11 + 3 * n_ctx]
-    probs_ref, dscore_ref, cot_ref = refs[11 + 3 * n_ctx :]
+def token_levels(energy_ref, n_ctx, n_fsdp, head_split, channels):
+    sample = lax.axis_index("fsdp") // head_split
+    energy = sum(
+        jnp.sum(energy_ref[pl.ds(at * n_fsdp + sample * head_split, head_split)], axis=0)
+        for at in range(n_ctx)
+    )
+    return loss_scale / (jnp.sqrt(energy * (1.0 / channels)) + floor_term)
+
+
+def pick_row(table, at):
+    ids = lax.broadcasted_iota(jnp.int32, table.shape, 0)
+    return jnp.sum(jnp.where(ids == at, table, 0.0), axis=0, keepdims=True)
+
+
+def query_kernel(n_ctx, heads, channels, *refs):
+    gain_ref, qn_ref, kn_ref, vn_ref, x_ref, goal_ref, lse_ref, drift_ref, turn_ref, stats_ref = refs[:10]
+    probs_ref, dscore_ref, cross_ref, lift_ref, grown_ref, goal_b_ref, dscore_b_ref = refs[10:]
+    head = hosted_head(lax.axis_index("ctx"), lax.axis_index("fsdp"), n_ctx)
+    gain = gain_ref[:, head_lanes(head, heads)]
+    rows = cross_ref.shape[1]
+    inv_root = HD ** (-0.5)
+    goal_b_ref[...] = goal_ref[...].astype(BF16)
+    blocks = [slice(dist * rows, (dist + 1) * rows) for dist in range(n_ctx)]
+    for here in blocks:
+        scores = mm(kn_ref[here, :], qn_ref[...], NT) * inv_root
+        probs = jnp.exp(scores - lse_ref[...])
+        dprobs = mm(vn_ref[here, :], goal_b_ref[...], NT)
+        dscore = probs * (dprobs - drift_ref[...]) * inv_root
+        probs_ref[here, :] = probs.astype(BF16)
+        dscore_ref[here, :] = dscore
+        dscore_b_ref[here, :] = dscore.astype(BF16)
+    for dist, here in enumerate(blocks):
+        dquery = mm(dscore_b_ref[:, here], kn_ref[...], TN)
+        inv_q = norm_scales(stats_ref[4 * dist : 4 * dist + 4, :], channels)[0]
+        x = x_ref[here, 0:HD].astype(F32)
+        dy = turn_back(dquery, turn_ref[here, :])
+        grown = gain * dy
+        grown_ref[here, :] = grown
+        cross_ref[dist : dist + 1, :] = as_row(jnp.sum(x * grown, axis=1, keepdims=True))
+        lift_ref[here, :] = dy * x * inv_q
+
+
+def key_kernel(n_ctx, n_fsdp, heads, channels, *refs):
+    energy_ref, gain_ref, qn_ref, x_ref, goal_ref, turn_ref, stats_ref = refs[:7]
+    probs_ref, dscore_ref, cross_q_ref, lift_ref, grown_ref, cross_ref = refs[7:13]
+    back_refs = refs[13 : 13 + n_ctx]
+    cot_ref = refs[13 + n_ctx]
     ctx_id, fsdp_id = lax.axis_index("ctx"), lax.axis_index("fsdp")
     head = hosted_head(ctx_id, fsdp_id, n_ctx)
     active = head < heads
-    head_split = channels // (heads * HD)
-    sample = fsdp_id // head_split
-    lanes = head_lanes(head, heads)
-    gain_q, gain_k = gain_q_ref[:, lanes], gain_k_ref[:, lanes]
-    rows = (block_refs[0].shape[0] - ORDER_ROWS) // 6
-    inv_root = HD ** (-0.5)
-    energy = jnp.zeros((n_ctx, rows), F32)
-    for ctx_at in range(n_ctx):
-        energy = energy + jnp.sum(energy_ref[pl.ds(ctx_at * n_fsdp + sample * head_split, head_split)], axis=0)
-    level = loss_scale / (jnp.sqrt(energy * (1.0 / channels)) + floor_term)
-    block_ids = lax.broadcasted_iota(jnp.int32, (n_ctx, rows), 0)
+    gain = gain_ref[:, head_lanes(head, heads)]
+    rows = cross_q_ref.shape[1]
+    level = token_levels(energy_ref, n_ctx, n_fsdp, channels // (heads * HD), channels)
+    levels = [pick_row(level, ctx_id ^ dist) for dist in range(n_ctx)]
+    blocks = [slice(dist * rows, (dist + 1) * rows) for dist in range(n_ctx)]
     gain_q_sum = jnp.zeros((1, HD), F32)
+    for here, row, back in zip(blocks, levels, back_refs):
+        scale = as_column(row)
+        back[0:rows, :] = (scale * grown_ref[here, :]).astype(BF16)
+        cot_ref[here, :] = (scale * goal_ref[here, :]).astype(BF16)
+        gain_q_sum = gain_q_sum + jnp.sum(scale * lift_ref[here, :], axis=0, keepdims=True)
+    level_row = jnp.concatenate(levels, axis=1)
     gain_k_sum = jnp.zeros((1, HD), F32)
-    crosses = []
+    cross_k = []
+    for dist, here in enumerate(blocks):
+        back_refs[dist][2 * rows :, :] = mm(probs_ref[here, :], cot_ref[...], NN).astype(BF16)
+        dscore = (dscore_ref[here, :] * level_row).astype(BF16)
+        dkey = mm(dscore, qn_ref[...], NN)
+        inv_k = norm_scales(stats_ref[4 * dist : 4 * dist + 4, :], channels)[1]
+        x = x_ref[here, HD:].astype(F32)
+        dy = turn_back(dkey, turn_ref[here, :])
+        grown = gain * dy
+        back_refs[dist][rows : 2 * rows, :] = grown.astype(BF16)
+        cross_k.append(as_row(jnp.sum(x * grown, axis=1, keepdims=True)))
+        gain_k_sum = gain_k_sum + jnp.sum(dy * x * inv_k, axis=0, keepdims=True)
     for dist in range(n_ctx):
-        here = slice(dist * rows, (dist + 1) * rows)
-        owner = ctx_id ^ dist
-        scale = as_column(jnp.sum(jnp.where(block_ids == owner, level, 0.0), axis=0, keepdims=True))
-        output = out_ref[here, :]
-        cot = (scale * goal_ref[here, :]).astype(BF16)
-        drift = jnp.sum(cot.astype(F32) * output, axis=1, keepdims=True)
-        scores = mm(qcat_ref[here, HD:], kcat_ref[:, 0:HD], NT) * inv_root
-        probs = jnp.exp(scores - lse_ref[here, 0:1])
-        dprobs = mm(cot, vcat_ref[:, 0:HD], NT)
-        dscore = (probs * (dprobs - drift) * inv_root).astype(BF16)
-        probs_ref[here, :] = probs.astype(BF16)
-        dscore_ref[here, :] = dscore
-        cot_ref[here, :] = cot
-        dquery = mm(dscore, kcat_ref[:, 0:HD], NN)
-        inv_q = norm_scales(stats_refs[dist][...], channels)[0]
-        x = block_refs[dist][0:rows, :].astype(F32)
-        dy = turn(dquery, turn_ref[here, 0:HD], -turn_ref[here, HD:])
-        grown = gain_q * dy
-        back_refs[dist][0:rows, :] = grown.astype(BF16)
-        crosses.append(as_row(jnp.sum(x * grown, axis=1, keepdims=True)))
-        gain_q_sum = gain_q_sum + jnp.sum(dy * x * inv_q, axis=0, keepdims=True)
-    for dist in range(n_ctx):
-        here = slice(dist * rows, (dist + 1) * rows)
-        back_refs[dist][2 * rows : 3 * rows, :] = mm(probs_ref[:, here], cot_ref[...], TN).astype(BF16)
-        dkey = mm(dscore_ref[:, here], qcat_ref[:, HD:], TN)
-        inv_k = norm_scales(stats_refs[dist][...], channels)[1]
-        x = block_refs[dist][rows : 2 * rows, :].astype(F32)
-        dy = turn(dkey, turn_ref[here, 0:HD], -turn_ref[here, HD:])
-        grown = gain_k * dy
-        back_refs[dist][rows : 2 * rows, :] = grown.astype(BF16)
-        cross_k = as_row(jnp.sum(x * grown, axis=1, keepdims=True))
-        gain_k_sum = gain_k_sum + jnp.sum(dy * x * inv_k, axis=0, keepdims=True)
-        crosses[dist] = jnp.concatenate([crosses[dist], cross_k], axis=0)
-    for dist in range(n_ctx):
-        sums = jnp.concatenate([crosses[dist], gain_q_sum, gain_k_sum], axis=0)
+        cross_q = cross_q_ref[dist : dist + 1, :] * levels[dist]
+        sums = jnp.concatenate([cross_q, cross_k[dist], gain_q_sum, gain_k_sum], axis=0)
         sums = jnp.where(active, sums, 0.0)
         start = (ctx_id ^ dist) * n_fsdp
         for at in range(n_fsdp):
@@ -235,7 +266,7 @@
     head_split = channels // (heads * HD)
     sample = fsdp_id // head_split
     rows = q_ref.shape[0]
-    inv_q, inv_k, _, _ = norm_scales(stats_ref[...], channels)
+    inv_q, inv_k, _, _ = norm_scales(stats_ref[0:4, :], channels)
     total = jnp.zeros((4, rows), F32)
     for ctx_at in range(n_ctx):
         total = total + jnp.sum(cross_ref[pl.ds(ctx_at * n_fsdp + sample * head_split, head_split)], axis=0)
@@ -253,7 +284,7 @@
             h_q, h_k = back[0:rows, :].astype(F32), back[rows : 2 * rows, :].astype(F32)
             dq_ref[:, lanes] = (inv_q * h_q - q_ref[:, lanes].astype(F32) * tilt_q).astype(BF16)
             dk_ref[:, lanes] = (inv_k * h_k - k_ref[:, lanes].astype(F32) * tilt_k).astype(BF16)
-            dv_ref[:, lanes] = back[2 * rows : 3 * rows, :]
+            dv_ref[:, lanes] = back[2 * rows :, :]
             sums = cross_ref[host * n_fsdp + fsdp_id]
             gain_q_ref[:, lanes] = sums[2:3]
             gain_k_ref[:, lanes] = sums[3:4]
@@ -296,7 +327,7 @@
             out_specs=[vmem] * len(outs),
             scratch_shapes=list(scratch),
             cost_estimate=pl.CostEstimate(flops=flops, bytes_accessed=2**20, transcendentals=0),
-            compiler_params=pltpu.CompilerParams(vmem_limit_bytes=20 * 2**20 + seq * 2**13),
+            compiler_params=pltpu.CompilerParams(vmem_limit_bytes=16 * 2**20 + seq * 2**14),
         )(*ins)
 
     def in_hbm(array):
@@ -309,10 +340,16 @@
         block = block + swap(block, "fsdp", 1)
         return sum([swap(block, "fsdp", d) for d in range(2, head_split, 2)], block)
 
-    def from_peers(blocks):
+    def from_peers(blocks, idle=None):
         out = [blocks[0]] + [None] * (n_ctx - 1)
         for dist in reversed(range(1, n_ctx)):
-            out[dist] = swap(blocks[dist], "ctx", dist)
+            route = []
+            for c in range(n_ctx):
+                for f in range(n_fsdp):
+                    near = idle and idle(c, c ^ dist, f) and idle(c ^ dist, c, f ^ 1)
+                    target = (c, f ^ 1) if near else (c ^ dist, f)
+                    route.append((c * n_fsdp + f, target[0] * n_fsdp + target[1]))
+            out[dist] = lax.ppermute(blocks[dist], BOTH, route)
         return out
 
     places = np.arange(seq, dtype=np.float32)
@@ -340,37 +377,42 @@
         from_hbm=9,
     )
     gains = (gain_q, gain_k)
-    blocks = from_peers(blocks)
-    stats = from_peers([sum_over_sample(part)] * n_ctx)
-
-    energy_out, qcat, kcat, vcat, output, goal, lse, turns = kernel(
+    parts = from_peers([part] * n_ctx)
+    blocks = from_peers(blocks, lambda c, peer, f: hosted_head(peer, f, n_ctx) >= heads)
+    stats = sum_over_sample(jnp.concatenate(parts, axis=0))
+
+    energy_out, qn, kn, vn, x, goal, lse, drift, turns = kernel(
         functools.partial(forward_kernel, *sizes),
-        (time_index, *gains, table, *blocks, *stats),
+        (time_index, *gains, table, *blocks, stats),
         [((n_all, n_ctx, rows), F32)]
-        + [((seq, 2 * HD), BF16)] * 3
-        + [((seq, HD), F32)] * 3
-        + [((seq, 2 * HD), F32)],
-        scratch=[pltpu.SMEM(time_index.shape, jnp.int32), pltpu.SemaphoreType.DMA],
+        + [((seq, HD), BF16)] * 3
+        + [((seq, 2 * HD), BF16), ((seq, HD), F32)]
+        + [((1, seq), F32)] * 2
+        + [((seq, HD), F32)],
+        scratch=[pltpu.VMEM((seq, 2 * HD), BF16)] * 3
+        + [pltpu.SMEM(time_index.shape, jnp.int32), pltpu.SemaphoreType.DMA],
         from_hbm=1,
     )
     energy = lax.all_to_all(energy_out, BOTH, 0, 0)
+    probs, dscore, cross_q, lift, grown = kernel(
+        functools.partial(query_kernel, n_ctx, heads, channels),
+        (gain_q, qn, kn, vn, x, goal, lse, drift, turns, stats),
+        [((seq, seq), BF16), ((seq, seq), F32), ((n_ctx, rows), F32)] + [((seq, HD), F32)] * 2,
+        scratch=[pltpu.VMEM((seq, HD), BF16), pltpu.VMEM((seq, seq), BF16)],
+    )
 
     cross_out, *back = kernel(
-        functools.partial(backward_kernel, *sizes),
-        (energy, *gains, qcat, kcat, vcat, output, goal, lse, turns, *blocks, *stats),
+        functools.partial(key_kernel, *sizes),
+        (energy, gain_k, qn, x, goal, turns, stats, probs, dscore, cross_q, lift, grown),
         [((n_all, 4, rows), F32)] + [((3 * rows, HD), BF16)] * n_ctx,
-        scratch=[
-            pltpu.VMEM((seq, seq), BF16),
-            pltpu.VMEM((seq, seq), BF16),
-            pltpu.VMEM((seq, HD), BF16),
-        ],
-    )
-    back = from_peers(back)
+        scratch=[pltpu.VMEM((seq, HD), BF16)],
+    )
+    back = from_peers(back, lambda c, peer, f: hosted_head(c, f, n_ctx) >= heads)
     crosses = lax.all_to_all(cross_out, BOTH, 0, 0)
 
     query_grad, key_grad, value_grad, *gain_grads = kernel(
         functools.partial(finish_kernel, *sizes),
-        (stats[0], crosses, queries, keys, *back),
+        (stats, crosses, queries, keys, *back),
         [((rows, ch_dev), BF16)] * 3 + [((ch_dev,), F32)] * 2,
         scratch=[pltpu.VMEM((1, ch_dev), F32)] * 2,
     )

time: 56.5 us -> 58.4 us (1.034)
  blocking collectives: 12 us -> 0 us
  waiting for transfers between devices: 12.9 us -> 22 us
  starting transfers between devices: 20.4 us -> 24.2 us
  local copies, waits for them, and re-layouts: 0.01 us -> 0.65 us
    ppermute x0 -> x9, waiting for transfers between devices: none -> 13.8 us  [from_peers(): out[dist] = lax.ppermute(blocks[dist], BOTH, route)]
    ppermute x13 -> x4, starting transfers between devices: 17.7 us -> 4.52 us  [swap(): lax.ppermute(block, axis, [(i, i ^ dist) for i in range(lax.axis_size(axi...]
    all_to_all x1 -> x0, blocking collectives: 12 us -> none  [per_device(): energy = lax.all_to_all(energy_out, BOTH, 0, 0)]
    ppermute x13 -> x4, waiting for transfers between devices: 12.9 us -> 2.14 us  [swap(): lax.ppermute(block, axis, [(i, i ^ dist) for i in range(lax.axis_size(axi...]
    ppermute x0 -> x9, starting transfers between devices: none -> 10.3 us  [from_peers(): out[dist] = lax.ppermute(blocks[dist], BOTH, route)]
    all_to_all x0 -> x1, starting transfers between devices: none -> 6.65 us  [per_device(): energy = lax.all_to_all(energy_out, BOTH, 0, 0)]
    all_to_all x0 -> x1, waiting for transfers between devices: none -> 6.03 us  [per_device(): energy = lax.all_to_all(energy_out, BOTH, 0, 0)]
    unnamed x6 -> x8, local copies, waits for them, and re-layouts: 0.01 us -> 0.65 us
  transfers between devices with their start and end apart: 14 -> 15, of which waited for: 6 -> 10; matrix products, arithmetic and copies ran while one was open for 0% -> 0% of each run, Pallas kernels for 0% -> 2%
where the time goes in v3:
time: 58.4 us; the launch traced here: 58.1 us
  starting transfers between devices  24.2 us (41%)
  waiting for transfers between devices  22 us (38%)
  Pallas kernels  9.22 us (16%)
  between operations  2.03 us (3%)
  local copies, waits for them, and re-layouts  0.65 us (1%)
    ppermute x9, waiting for transfers between devices, from_peers(): out[dist] = lax.ppermute(blocks[dist], BOTH, route)  13.8 us
    ppermute x9, starting transfers between devices, from_peers(): out[dist] = lax.ppermute(blocks[dist], BOTH, route)  10.3 us
    pallas_call x5, Pallas kernels, kernel(): pl.pallas_call(body, out_shape=[jax.ShapeDtypeStruct(*o) for o in outs],...  9.22 us
    all_to_all x1, starting transfers between devices, per_device(): energy = lax.all_to_all(energy_out, BOTH, 0, 0)  6.65 us
    all_to_all x1, waiting for transfers between devices, per_device(): energy = lax.all_to_all(energy_out, BOTH, 0, 0)  6.03 us
    ppermute x4, starting transfers between devices, swap(): lax.ppermute(block, axis, [(i, i ^ dist) for i in range(lax.axis_size(axi...  4.52 us
    all_to_all x1, starting transfers between devices, per_device(): crosses = lax.all_to_all(cross_out, BOTH, 0, 0)  2.7 us
    ppermute x4, waiting for transfers between devices, swap(): lax.ppermute(block, axis, [(i, i ^ dist) for i in range(lax.axis_size(axi...  2.14 us
  transfers between devices with their start and end apart: 15, of which 10 were waited for; matrix products, arithmetic and copies ran while one was open for 0% of the time, Pallas kernels for 2%

profile of v3, /device:TPU:0, one launch (start us, length us, event | category | flops | bytes accessed | tf_op | source)
XLA Modules:
  0.0 58.1 jit_solution(3185553507165752580)
XLA Ops:
  1.3 1.5 %shard_map.146 = (f32[4,128]{1,0:T(4,128)S(1)}, f32[1,384]{1,0:T(1,128)S(1)}, f32[1,384]{1,0:T(1,128)S(1)}, bf16[784,128]{1,0:T(8,128)(2,1)S(1)}, bf16[784,128]{...) custom-call(s32[1]{0:T(128)S(6)} %copy.17.refs_0_, f32[384]{0:T(512)} %refs_1_.1, ...), custom_call_target="tpu_custom_call" | custom-call | flops 100000000 | bytes 1048576 | tf_op jit(solution)/shard_map/pallas_call | solution.py:323
  2.8 4.0 %collective-permute-start.2 = (f32[4,128]{1,0:T(4,128)S(1)}, f32[4,128]{1,0:T(4,128)S(1)}, u32[]{:S(2)}, u32[]{:S(2)}) collective-permute-start(f32[4,128]{1,0:T(4,128)S(1)} %get-tuple-element.31), channel_id=1, source_target_pairs={{0,24},{1,25},{2,26},{3,27},{4,28},{5,29},{6,30},{7,31},{8,16},{9,... | collective-permute-start | bytes 6152 | tf_op jit(solution)/shard_map/ppermute | solution.py:352
  6.8 0.5 collective-permute-start.1
  7.4 0.9 %collective-permute-done.2 = f32[4,128]{1,0:T(4,128)S(1)} collective-permute-done((f32[4,128]{1,0:T(4,128)S(1)}, f32[4,128]{1,0:T(4,128)S(1)}, u32[]{:S(2)}, u32[]{:S(2)}) %collective-permute-start.2) | collective-permute-done | bytes 2080 | tf_op jit(solution)/shard_map/ppermute | solution.py:352
  8.3 2.0 %collective-permute-done.1 = f32[4,128]{1,0:T(4,128)S(1)} collective-permute-done((f32[4,128]{1,0:T(4,128)S(1)}, f32[4,128]{1,0:T(4,128)S(1)}, u32[]{:S(2)}, u32[]{:S(2)}) %collective-permute-start.1) | collective-permute-done | bytes 2080 | tf_op jit(solution)/shard_map/ppermute | solution.py:352
  10.9 1.2 %collective-permute-done.3 = f32[16,128]{1,0:T(8,128)S(1)} collective-permute-done((f32[16,128]{1,0:T(8,128)S(1)}, f32[16,128]{1,0:T(8,128)S(1)}, u32[]{:S(2)}, u32[]{:S(2)}) %collective-permute-start.3) | collective-permute-done | bytes 8224 | tf_op jit(solution)/shard_map/ppermute | solution.py:337
  12.1 3.7 %collective-permute-start.6 = (f32[16,128]{1,0:T(8,128)S(1)}, f32[16,128]{1,0:T(8,128)S(1)}, u32[]{:S(2)}, u32[]{:S(2)}) collective-permute-start(f32[16,128]{1,0:T(8,128)S(1)} %fusion), channel_id=1, source_target_pairs={{0,6},{1,7},{2,4},{3,5},{4,2},{5,3},{6,0},{7,1},{8,14},{9,15},{10,... | collective-permute-start | bytes 24584 | tf_op jit(solution)/shard_map/ppermute | solution.py:337
  15.8 0.8 %collective-permute-start.4 = (f32[16,128]{1,0:T(8,128)S(1)}, f32[16,128]{1,0:T(8,128)S(1)}, u32[]{:S(2)}, u32[]{:S(2)}) collective-permute-start(f32[16,128]{1,0:T(8,128)S(1)} %fusion), channel_id=1, source_target_pairs={{0,2},{1,3},{2,0},{3,1},{4,6},{5,7},{6,4},{7,5},{8,10},{9,11},{10,... | collective-permute-start | bytes 24584 | tf_op jit(solution)/shard_map/ppermute | solution.py:337
  17.0 1.7 %collective-permute-start.8 = (bf16[784,128]{1,0:T(8,128)(2,1)S(1)}, bf16[784,128]{1,0:T(8,128)(2,1)S(1)}, u32[]{:S(2)}, u32[]{:S(2)}) collective-permute-start(bf16[784,128]{1,0:T(8,128)(2,1)S(1)} %get-tuple-element.36), channel_id=1, source_target_pairs={{0,16},{1,17},{2,18},{3,19},{4,20},{5,21},{6,22},{7,23},{8,24},{9,... | collective-permute-start | bytes 602120 | tf_op jit(solution)/shard_map/ppermute | solution.py:352
  19.4 1.0 %collective-permute-done.5 = f32[16,128]{1,0:T(8,128)S(1)} collective-permute-done((f32[16,128]{1,0:T(8,128)S(1)}, f32[16,128]{1,0:T(8,128)S(1)}, u32[]{:S(2)}, u32[]{:S(2)}) %collective-permute-start.5) | collective-permute-done | bytes 8224 | tf_op jit(solution)/shard_map/ppermute | solution.py:337
  20.3 4.1 %collective-permute-done.7.refs_5_ = bf16[784,128]{1,0:T(8,128)(2,1)S(1)} collective-permute-done((bf16[784,128]{1,0:T(8,128)(2,1)S(1)}, bf16[784,128]{1,0:T(8,128)(2,1)S(1)}, u32[]{:S(2)}, u32[]{:S(2)}) %collective-permute-start.7) | collective-permute-done | bytes 200736 | tf_op jit(solution)/shard_map/ppermute | solution.py:352
  24.4 2.1 %collective-permute-done.8.refs_6_ = bf16[784,128]{1,0:T(8,128)(2,1)S(1)} collective-permute-done((bf16[784,128]{1,0:T(8,128)(2,1)S(1)}, bf16[784,128]{1,0:T(8,128)(2,1)S(1)}, u32[]{:S(2)}, u32[]{:S(2)}) %collective-permute-start.8) | collective-permute-done | bytes 200736 | tf_op jit(solution)/shard_map/ppermute | solution.py:352
  26.6 3.6 %shard_map.147 = (f32[32,4,128]{2,1,0:T(4,128)}, bf16[512,128]{1,0:T(8,128)(2,1)S(1)}, bf16[512,128]{1,0:T(8,128)(2,1)S(1)}, bf16[512,128]{1,0:T(8,128)(2,1)S(1)...) custom-call(s32[1]{0:T(128)S(6)} %copy.16.refs_0_, ...), custom_call_target="tpu_custom_call" | custom-call | flops 100000000 | bytes 1048576 | tf_op jit(solution)/shard_map/pallas_call | solution.py:323
  30.2 6.6 %all-to-all-start = ((f32[32,4,128]{2,1,0:T(4,128)}), f32[32,4,128]{2,1,0:T(4,128)S(1)}, u32[]{:S(2)}, u32[]{:S(2)}) async-start(f32[32,4,128]{2,1,0:T(4,128)} %get-tuple-element.38), calls=%async_computation | async-start | bytes 131072 | tf_op jit(solution)/shard_map/all_to_all | solution.py:396
  36.9 1.4 %shard_map.148 = (bf16[512,512]{1,0:T(8,128)(2,1)S(1)}, f32[512,512]{1,0:T(8,128)S(1)}, f32[4,128]{1,0:T(4,128)S(1)}, f32[512,128]{1,0:T(8,128)S(1)}, f32[512,128]{1,0:T(8,128)S(1)}) custom-call(f32[1,384]{1,0:T(1,128)S(1)} %get-tuple-element.32.refs_1_.refs_0_, bf16[512,128]{1,0:T(8,128)(2,1)S(1)} %get-tuple-element.39.refs_1_.refs_2_, ...), custom_call_target="tpu_custom_call" | custom-call | flops 100000000 | bytes 1048576 | tf_op jit(solution)/shard_map/pallas_call | solution.py:323
  38.2 6.0 %all-to-all-done.refs_0_ = f32[32,4,128]{2,1,0:T(4,128)S(1)} async-done(((f32[32,4,128]{2,1,0:T(4,128)}), f32[32,4,128]{2,1,0:T(4,128)S(1)}, u32[]{:S(2)}, u32[]{:S(2)}) %all-to-all-start) | async-done | bytes 65568 | tf_op jit(solution)/shard_map/all_to_all | solution.py:396
  44.2 1.8 %shard_map.149 = (f32[32,4,128]{2,1,0:T(4,128)}, bf16[384,128]{1,0:T(8,128)(2,1)S(1)}, bf16[384,128]{1,0:T(8,128)(2,1)S(1)}, bf16[384,128]{1,0:T(8,128)(2,1)S(1)}, bf16[384,128]{1,0:T(8,128)(2,1)S(1)}) custom-call(f32[32,4,128]{2,1,0:T(4,128)S(1)} %all-to-all-done.refs_0_, f32[1,384]{1,0:T(1,128)S(1)} %get-tuple-element.33.refs_2_.refs_1_, ...), custom_call_target="tpu_custom_call" | custom-call | flops 100000000 | bytes 1048576 | tf_op jit(solution)/shard_map/pallas_call | solution.py:323
  46.0 0.6 %copy-done.3 = bf16[384,128]{1,0:T(8,128)(2,1)} copy-done((bf16[384,128]{1,0:T(8,128)(2,1)}, bf16[384,128]{1,0:T(8,128)(2,1)S(1)}, u32[]{:S(2)}) %copy-start.3) | copy-done | bytes 98328
  46.7 2.7 %all-to-all-start.1 = ((f32[32,4,128]{2,1,0:T(4,128)}), f32[32,4,128]{2,1,0:T(4,128)S(1)}, u32[]{:S(2)}, u32[]{:S(2)}) async-start(f32[32,4,128]{2,1,0:T(4,128)} %get-tuple-element.52), calls=%async_computation.1 | async-start | bytes 131072 | tf_op jit(solution)/shard_map/all_to_all | solution.py:411
  49.4 1.7 %collective-permute-start.10 = (bf16[384,128]{1,0:T(8,128)(2,1)}, bf16[384,128]{1,0:T(8,128)(2,1)S(1)}, u32[]{:S(2)}, u32[]{:S(2)}) collective-permute-start(bf16[384,128]{1,0:T(8,128)(2,1)} %copy-done.3), channel_id=1, source_target_pairs={{0,8},{1,9},{2,10},{3,11},{4,12},{5,13},{6,14},{7,15},{8,0},{9,1},... | collective-permute-start | bytes 294920 | tf_op jit(solution)/shard_map/ppermute | solution.py:352
  51.1 1.5 %collective-permute-start.11 = (bf16[384,128]{1,0:T(8,128)(2,1)S(1)}, bf16[384,128]{1,0:T(8,128)(2,1)S(1)}, u32[]{:S(2)}, u32[]{:S(2)}) collective-permute-start(bf16[384,128]{1,0:T(8,128)(2,1)S(1)} %get-tuple-element.55), channel_id=1, source_target_pairs={{0,16},{1,17},{2,18},{3,19},{4,20},{5,21},{6,22},{7,23},{8,24},{9,... | collective-permute-start | bytes 294920 | tf_op jit(solution)/shard_map/ppermute | solution.py:352
  52.9 2.1 %collective-permute-done.10.refs_5_ = bf16[384,128]{1,0:T(8,128)(2,1)S(1)} collective-permute-done((bf16[384,128]{1,0:T(8,128)(2,1)}, bf16[384,128]{1,0:T(8,128)(2,1)S(1)}, u32[]{:S(2)}, u32[]{:S(2)}) %collective-permute-start.10) | collective-permute-done | bytes 98336 | tf_op jit(solution)/shard_map/ppermute | solution.py:352
  55.0 2.1 %collective-permute-done.11.refs_6_ = bf16[384,128]{1,0:T(8,128)(2,1)S(1)} collective-permute-done((bf16[384,128]{1,0:T(8,128)(2,1)S(1)}, bf16[384,128]{1,0:T(8,128)(2,1)S(1)}, u32[]{:S(2)}, u32[]{:S(2)}) %collective-permute-start.11) | collective-permute-done | bytes 98336 | tf_op jit(solution)/shard_map/ppermute | solution.py:352
  57.1 1.0 %shard_map.150 = (bf16[128,384]{1,0:T(8,128)(2,1)}, bf16[128,384]{1,0:T(8,128)(2,1)}, bf16[128,384]{1,0:T(8,128)(2,1)}, f32[384]{0:T(512)}, f32[384]{0:T(512)}) custom-call(f32[16,128]{1,0:T(8,128)S(1)} %add_add_fusion.refs_8_.refs_9_.refs_6_.refs_0_, f32[32,4,128]{2,1,0:T(4,128)S(1)} %all-to-all-done.1.refs_1_, bf16[128,384]{1,0:T(8,128)(2,1)S(1)} %copy-done, ...), custom_call_target="tpu_custom_call" | custom-call | flops 100000000 | bytes 1048576 | tf_op jit(solution)/shard_map/pallas_call | solution.py:323
  (22 shorter events, 1.6 us)
Async XLA Ops:
  1.3 25.3 %copy-start.2 = (f32[512,128]{1,0:T(8,128)S(1)}, f32[512,128]{1,0:T(8,128)}, u32[]{:S(2)}) copy-start(f32[512,128]{1,0:T(8,128)} %constant.2.clone.refs_3_) | copy-start | bytes 786436
  2.8 5.6 %collective-permute-start.2 = (f32[4,128]{1,0:T(4,128)S(1)}, f32[4,128]{1,0:T(4,128)S(1)}, u32[]{:S(2)}, u32[]{:S(2)}) collective-permute-start(f32[4,128]{1,0:T(4,128)S(1)} %get-tuple-element.31), channel_id=1, source_target_pairs={{0,24},{1,25},{2,26},{3,27},{4,28},{5,29},{6,30},{7,31},{8,16},{9,... | collective-permute-start | bytes 6152 | tf_op jit(solution)/shard_map/ppermute | solution.py:352
  6.8 3.6 %collective-permute-start.1 = (f32[4,128]{1,0:T(4,128)S(1)}, f32[4,128]{1,0:T(4,128)S(1)}, u32[]{:S(2)}, u32[]{:S(2)}) collective-permute-start(f32[4,128]{1,0:T(4,128)S(1)} %get-tuple-element.31), channel_id=1, source_target_pairs={{0,16},{1,17},{2,18},{3,19},{4,20},{5,21},{6,22},{7,23},{8,24},{9,... | collective-permute-start | bytes 6152 | tf_op jit(solution)/shard_map/ppermute | solution.py:352
  7.3 3.6 %collective-permute-start = (f32[4,128]{1,0:T(4,128)S(1)}, f32[4,128]{1,0:T(4,128)S(1)}, u32[]{:S(2)}, u32[]{:S(2)}) collective-permute-start(f32[4,128]{1,0:T(4,128)S(1)} %get-tuple-element.31), channel_id=1, source_target_pairs={{0,8},{1,9},{2,10},{3,11},{4,12},{5,13},{6,14},{7,15},{8,0},{9,1},... | collective-permute-start | bytes 6152 | tf_op jit(solution)/shard_map/ppermute | solution.py:352
  10.9 1.2 %collective-permute-start.3 = (f32[16,128]{1,0:T(8,128)S(1)}, f32[16,128]{1,0:T(8,128)S(1)}, u32[]{:S(2)}, u32[]{:S(2)}) collective-permute-start(f32[16,128]{1,0:T(8,128)S(1)} %pad_maximum_fusion), channel_id=1, source_target_pairs={{0,1},{1,0},{2,3},{3,2},{4,5},{5,4},{6,7},{7,6},{8,9},{9,8},{10,11... | collective-permute-start | bytes 24584 | tf_op jit(solution)/shard_map/ppermute | solution.py:337
  12.1 7.2 %collective-permute-start.6 = (f32[16,128]{1,0:T(8,128)S(1)}, f32[16,128]{1,0:T(8,128)S(1)}, u32[]{:S(2)}, u32[]{:S(2)}) collective-permute-start(f32[16,128]{1,0:T(8,128)S(1)} %fusion), channel_id=1, source_target_pairs={{0,6},{1,7},{2,4},{3,5},{4,2},{5,3},{6,0},{7,1},{8,14},{9,15},{10,... | collective-permute-start | bytes 24584 | tf_op jit(solution)/shard_map/ppermute | solution.py:337
  15.8 4.5 %collective-permute-start.5 = (f32[16,128]{1,0:T(8,128)S(1)}, f32[16,128]{1,0:T(8,128)S(1)}, u32[]{:S(2)}, u32[]{:S(2)}) collective-permute-start(f32[16,128]{1,0:T(8,128)S(1)} %fusion), channel_id=1, source_target_pairs={{0,4},{1,5},{2,6},{3,7},{4,0},{5,1},{6,2},{7,3},{8,12},{9,13},{10,... | collective-permute-start | bytes 24584 | tf_op jit(solution)/shard_map/ppermute | solution.py:337
  15.8 4.5 %collective-permute-start.4 = (f32[16,128]{1,0:T(8,128)S(1)}, f32[16,128]{1,0:T(8,128)S(1)}, u32[]{:S(2)}, u32[]{:S(2)}) collective-permute-start(f32[16,128]{1,0:T(8,128)S(1)} %fusion), channel_id=1, source_target_pairs={{0,2},{1,3},{2,0},{3,1},{4,6},{5,7},{6,4},{7,5},{8,10},{9,11},{10,... | collective-permute-start | bytes 24584 | tf_op jit(solution)/shard_map/ppermute | solution.py:337
  16.6 7.9 %collective-permute-start.7 = (bf16[784,128]{1,0:T(8,128)(2,1)S(1)}, bf16[784,128]{1,0:T(8,128)(2,1)S(1)}, u32[]{:S(2)}, u32[]{:S(2)}) collective-permute-start(bf16[784,128]{1,0:T(8,128)(2,1)S(1)} %get-tuple-element.35), channel_id=1, source_target_pairs={{0,8},{1,9},{2,10},{3,11},{4,12},{5,13},{6,14},{7,15},{8,0},{9,1},... | collective-permute-start | bytes 602120 | tf_op jit(solution)/shard_map/ppermute | solution.py:352
  17.0 9.6 %collective-permute-start.8 = (bf16[784,128]{1,0:T(8,128)(2,1)S(1)}, bf16[784,128]{1,0:T(8,128)(2,1)S(1)}, u32[]{:S(2)}, u32[]{:S(2)}) collective-permute-start(bf16[784,128]{1,0:T(8,128)(2,1)S(1)} %get-tuple-element.36), channel_id=1, source_target_pairs={{0,16},{1,17},{2,18},{3,19},{4,20},{5,21},{6,22},{7,23},{8,24},{9,... | collective-permute-start | bytes 602120 | tf_op jit(solution)/shard_map/ppermute | solution.py:352
  19.3 7.3 %collective-permute-start.9 = (bf16[784,128]{1,0:T(8,128)(2,1)S(1)}, bf16[784,128]{1,0:T(8,128)(2,1)S(1)}, u32[]{:S(2)}, u32[]{:S(2)}) collective-permute-start(bf16[784,128]{1,0:T(8,128)(2,1)S(1)} %get-tuple-element.37), channel_id=1, source_target_pairs={{0,1},{1,25},{2,26},{3,27},{4,5},{5,29},{6,30},{7,31},{8,16},{9,17... | collective-permute-start | bytes 602120 | tf_op jit(solution)/shard_map/ppermute | solution.py:352
  30.2 14.0 %all-to-all-start = ((f32[32,4,128]{2,1,0:T(4,128)}), f32[32,4,128]{2,1,0:T(4,128)S(1)}, u32[]{:S(2)}, u32[]{:S(2)}) async-start(f32[32,4,128]{2,1,0:T(4,128)} %get-tuple-element.38), calls=%async_computation | async-start | bytes 131072 | tf_op jit(solution)/shard_map/all_to_all | solution.py:396
  44.2 12.9 %copy-start.1 = (bf16[128,384]{1,0:T(8,128)(2,1)S(1)}, bf16[128,384]{1,0:T(8,128)(2,1)}, u32[]{:S(2)}) copy-start(bf16[128,384]{1,0:T(8,128)(2,1)} %refs_3_.4) | copy-start | bytes 294916
  46.0 0.6 %copy-start.3 = (bf16[384,128]{1,0:T(8,128)(2,1)}, bf16[384,128]{1,0:T(8,128)(2,1)S(1)}, u32[]{:S(2)}) copy-start(bf16[384,128]{1,0:T(8,128)(2,1)S(1)} %get-tuple-element.54) | copy-start | bytes 294916
  46.7 10.4 %copy-start = (bf16[128,384]{1,0:T(8,128)(2,1)S(1)}, bf16[128,384]{1,0:T(8,128)(2,1)}, u32[]{:S(2)}) copy-start(bf16[128,384]{1,0:T(8,128)(2,1)} %refs_2_.3) | copy-start | bytes 294916
  46.7 10.4 %all-to-all-start.1 = ((f32[32,4,128]{2,1,0:T(4,128)}), f32[32,4,128]{2,1,0:T(4,128)S(1)}, u32[]{:S(2)}, u32[]{:S(2)}) async-start(f32[32,4,128]{2,1,0:T(4,128)} %get-tuple-element.52), calls=%async_computation.1 | async-start | bytes 131072 | tf_op jit(solution)/shard_map/all_to_all | solution.py:411
  49.4 5.7 %collective-permute-start.10 = (bf16[384,128]{1,0:T(8,128)(2,1)}, bf16[384,128]{1,0:T(8,128)(2,1)S(1)}, u32[]{:S(2)}, u32[]{:S(2)}) collective-permute-start(bf16[384,128]{1,0:T(8,128)(2,1)} %copy-done.3), channel_id=1, source_target_pairs={{0,8},{1,9},{2,10},{3,11},{4,12},{5,13},{6,14},{7,15},{8,0},{9,1},... | collective-permute-start | bytes 294920 | tf_op jit(solution)/shard_map/ppermute | solution.py:352
  51.1 6.0 %collective-permute-start.11 = (bf16[384,128]{1,0:T(8,128)(2,1)S(1)}, bf16[384,128]{1,0:T(8,128)(2,1)S(1)}, u32[]{:S(2)}, u32[]{:S(2)}) collective-permute-start(bf16[384,128]{1,0:T(8,128)(2,1)S(1)} %get-tuple-element.55), channel_id=1, source_target_pairs={{0,16},{1,17},{2,18},{3,19},{4,20},{5,21},{6,22},{7,23},{8,24},{9,... | collective-permute-start | bytes 294920 | tf_op jit(solution)/shard_map/ppermute | solution.py:352
  52.6 4.5 %collective-permute-start.12 = (bf16[384,128]{1,0:T(8,128)(2,1)S(1)}, bf16[384,128]{1,0:T(8,128)(2,1)S(1)}, u32[]{:S(2)}, u32[]{:S(2)}) collective-permute-start(bf16[384,128]{1,0:T(8,128)(2,1)S(1)} %get-tuple-element.56), channel_id=1, source_target_pairs={{0,24},{1,0},{2,26},{3,27},{4,28},{5,4},{6,30},{7,31},{8,16},{9,17... | collective-permute-start | bytes 294920 | tf_op jit(solution)/shard_map/ppermute | solution.py:352

commit v4 on v3

--- a/solution.py
+++ b/solution.py
@@ -41,8 +41,12 @@
     return jnp.sum(jnp.where(eye_mask(column.shape[0]), column, 0.0), axis=0, keepdims=True)
 
 
-def as_column(row):
-    return jnp.sum(jnp.where(eye_mask(row.shape[1]), row, 0.0), axis=1, keepdims=True)
+def columns(rows):
+    mask = eye_mask(rows.shape[1])
+    return [
+        jnp.sum(jnp.where(mask, rows[at : at + 1], 0.0), axis=1, keepdims=True)
+        for at in range(rows.shape[0])
+    ]
 
 
 def hosted_head(ctx_id, fsdp_id, n_ctx):
@@ -69,11 +73,13 @@
 
 
 def norm_scales(stats, channels):
-    mean = stats * (1.0 / channels)
-    inv = lax.rsqrt(mean[0:2] + eps_norm)
-    inv_q, inv_k = as_column(inv[0:1]), as_column(inv[1:2])
-    tilt = inv * inv * inv * mean[2:4]
-    return inv_q, inv_k, as_column(tilt[0:1]), as_column(tilt[1:2])
+    return lax.rsqrt(stats[0:2] * (1.0 / channels) + eps_norm)
+
+
+def norm_columns(stats, channels):
+    inv = norm_scales(stats, channels)
+    tilt = inv * inv * inv * (stats[2:4] * (1.0 / channels))
+    return columns(jnp.concatenate([inv, tilt], axis=0))
 
 
 def pack_kernel(n_ctx, heads, *refs):
@@ -119,7 +125,7 @@
     inv_root = HD ** (-0.5)
     for dist, block in enumerate(block_refs):
         here = slice(dist * rows, (dist + 1) * rows)
-        inv_q, inv_k, tilt_q, tilt_k = norm_scales(stats_ref[4 * dist : 4 * dist + 4, :], channels)
+        inv_q, inv_k, tilt_q, tilt_k = norm_columns(stats_ref[4 * dist : 4 * dist + 4, :], channels)
         order = block[6 * rows : 6 * rows + 1, :].astype(F32)
         both = table_ref[0:rows, :]
         for other in range(1, n_ctx):
@@ -150,23 +156,23 @@
     coef_tan = (jnp.cos(angle_t) ** 2)[0:1]
     for dist in range(n_ctx):
         here = slice(dist * rows, (dist + 1) * rows)
-        scores = mm(qcat_ref[here, HD:], kcat_ref[:, 0:HD], NT) * inv_root
-        slopes = mm(qcat_ref[here, :], kcat_ref[...], NT) * inv_root
+        scores = mm(qcat_ref[here, HD:], kcat_ref[:, 0:HD], NT)
+        slopes = mm(qcat_ref[here, :], kcat_ref[...], NT)
         peak = jnp.max(scores, axis=1, keepdims=True)
-        weights = jnp.exp(scores - peak)
+        weights = jnp.exp((scores - peak) * inv_root)
         totals = jnp.sum(weights, axis=1, keepdims=True)
         tilted = weights * slopes
         numer = mm(weights.astype(BF16), vcat_ref[...], NN)
-        numer_tan = numer[:, HD:] + mm(tilted.astype(BF16), vcat_ref[:, 0:HD], NN)
-        tilt = jnp.sum(tilted, axis=1, keepdims=True)
+        numer_tan = numer[:, HD:] + inv_root * mm(tilted.astype(BF16), vcat_ref[:, 0:HD], NN)
+        tilt = jnp.sum(tilted, axis=1, keepdims=True) * inv_root
         output = numer[:, 0:HD] / totals
-        output_tan = numer_tan / totals - (tilt / totals) * output
+        output_tan = (numer_tan - tilt * output) / totals
         goal = coef_out * output + coef_tan * output_tan
         goal_ref[here, :] = goal
         drift_ref[:, here] = as_row(
             jnp.sum(goal.astype(BF16).astype(F32) * output, axis=1, keepdims=True)
         )
-        lse_ref[:, here] = as_row(peak + jnp.log(totals))
+        lse_ref[:, here] = as_row(peak * inv_root + jnp.log(totals))
         row = as_row(jnp.sum(goal * goal, axis=1, keepdims=True))
         energy_ref[0, pl.ds(ctx_id ^ dist, 1), :] = jnp.where(active, row, 0.0)
     first = energy_ref[0]
@@ -198,16 +204,16 @@
     goal_b_ref[...] = goal_ref[...].astype(BF16)
     blocks = [slice(dist * rows, (dist + 1) * rows) for dist in range(n_ctx)]
     for here in blocks:
-        scores = mm(kn_ref[here, :], qn_ref[...], NT) * inv_root
-        probs = jnp.exp(scores - lse_ref[...])
+        scores = mm(kn_ref[here, :], qn_ref[...], NT)
+        probs = jnp.exp(scores * inv_root - lse_ref[...])
         dprobs = mm(vn_ref[here, :], goal_b_ref[...], NT)
-        dscore = probs * (dprobs - drift_ref[...]) * inv_root
+        dscore = probs * (dprobs - drift_ref[...])
         probs_ref[here, :] = probs.astype(BF16)
         dscore_ref[here, :] = dscore
         dscore_b_ref[here, :] = dscore.astype(BF16)
     for dist, here in enumerate(blocks):
-        dquery = mm(dscore_b_ref[:, here], kn_ref[...], TN)
-        inv_q = norm_scales(stats_ref[4 * dist : 4 * dist + 4, :], channels)[0]
+        dquery = mm(dscore_b_ref[:, here], kn_ref[...], TN) * inv_root
+        (inv_q,) = columns(norm_scales(stats_ref[4 * dist : 4 * dist + 4, :], channels)[0:1])
         x = x_ref[here, 0:HD].astype(F32)
         dy = turn_back(dquery, turn_ref[here, :])
         grown = gain * dy
@@ -231,18 +237,18 @@
     blocks = [slice(dist * rows, (dist + 1) * rows) for dist in range(n_ctx)]
     gain_q_sum = jnp.zeros((1, HD), F32)
     for here, row, back in zip(blocks, levels, back_refs):
-        scale = as_column(row)
+        (scale,) = columns(row)
         back[0:rows, :] = (scale * grown_ref[here, :]).astype(BF16)
         cot_ref[here, :] = (scale * goal_ref[here, :]).astype(BF16)
         gain_q_sum = gain_q_sum + jnp.sum(scale * lift_ref[here, :], axis=0, keepdims=True)
-    level_row = jnp.concatenate(levels, axis=1)
+    level_row = jnp.concatenate(levels, axis=1) * HD ** (-0.5)
     gain_k_sum = jnp.zeros((1, HD), F32)
     cross_k = []
     for dist, here in enumerate(blocks):
         back_refs[dist][2 * rows :, :] = mm(probs_ref[here, :], cot_ref[...], NN).astype(BF16)
         dscore = (dscore_ref[here, :] * level_row).astype(BF16)
         dkey = mm(dscore, qn_ref[...], NN)
-        inv_k = norm_scales(stats_ref[4 * dist : 4 * dist + 4, :], channels)[1]
+        (inv_k,) = columns(norm_scales(stats_ref[4 * dist : 4 * dist + 4, :], channels)[1:2])
         x = x_ref[here, HD:].astype(F32)
         dy = turn_back(dkey, turn_ref[here, :])
         grown = gain * dy
@@ -266,13 +272,12 @@
     head_split = channels // (heads * HD)
     sample = fsdp_id // head_split
     rows = q_ref.shape[0]
-    inv_q, inv_k, _, _ = norm_scales(stats_ref[0:4, :], channels)
+    inv = norm_scales(stats_ref[0:4, :], channels)
     total = jnp.zeros((4, rows), F32)
     for ctx_at in range(n_ctx):
         total = total + jnp.sum(cross_ref[pl.ds(ctx_at * n_fsdp + sample * head_split, head_split)], axis=0)
-    mean = total[0:2] * (1.0 / channels)
-    tilt_q = inv_q * inv_q * inv_q * as_column(mean[0:1])
-    tilt_k = inv_k * inv_k * inv_k * as_column(mean[1:2])
+    tilt = inv * inv * inv * (total[0:2] * (1.0 / channels))
+    inv_q, inv_k, tilt_q, tilt_k = columns(jnp.concatenate([inv, tilt], axis=0))
     for dist in range(n_ctx):
         host = ctx_id ^ dist
         head = hosted_head(host, fsdp_id, n_ctx)

time: 58.4 us -> 58 us (level)
  no operation moved by 1% of the time
where the time goes in v4:
time: 58 us; the launch traced here: 57.8 us
  starting transfers between devices  24.2 us (42%)
  waiting for transfers between devices  22 us (38%)
  Pallas kernels  8.89 us (15%)
  between operations  2.03 us (3%)
  local copies, waits for them, and re-layouts  0.65 us (1%)
    ppermute x9, waiting for transfers between devices, from_peers(): out[dist] = lax.ppermute(blocks[dist], BOTH, route)  13.8 us
    ppermute x9, starting transfers between devices, from_peers(): out[dist] = lax.ppermute(blocks[dist], BOTH, route)  10.3 us
    pallas_call x5, Pallas kernels, kernel(): pl.pallas_call(body, out_shape=[jax.ShapeDtypeStruct(*o) for o in outs],...  8.89 us
    all_to_all x1, starting transfers between devices, per_device(): energy = lax.all_to_all(energy_out, BOTH, 0, 0)  6.65 us
    all_to_all x1, waiting for transfers between devices, per_device(): energy = lax.all_to_all(energy_out, BOTH, 0, 0)  6.03 us
    ppermute x4, starting transfers between devices, swap(): lax.ppermute(block, axis, [(i, i ^ dist) for i in range(lax.axis_size(axi...  4.52 us
    all_to_all x1, starting transfers between devices, per_device(): crosses = lax.all_to_all(cross_out, BOTH, 0, 0)  2.7 us
    ppermute x4, waiting for transfers between devices, swap(): lax.ppermute(block, axis, [(i, i ^ dist) for i in range(lax.axis_size(axi...  2.14 us
  transfers between devices with their start and end apart: 15, of which 10 were waited for; matrix products, arithmetic and copies ran while one was open for 0% of the time, Pallas kernels for 2%

profile of v4, /device:TPU:0, one launch (start us, length us, event | category | flops | bytes accessed | tf_op | source)
XLA Modules:
  0.0 57.8 jit_solution(3078949074792356043)
XLA Ops:
  1.3 1.5 %shard_map.146 = (f32[4,128]{1,0:T(4,128)S(1)}, f32[1,384]{1,0:T(1,128)S(1)}, f32[1,384]{1,0:T(1,128)S(1)}, bf16[784,128]{1,0:T(8,128)(2,1)S(1)}, bf16[784,128]{...) custom-call(s32[1]{0:T(128)S(6)} %copy.17.refs_0_, f32[384]{0:T(512)} %refs_1_.1, ...), custom_call_target="tpu_custom_call" | custom-call | flops 100000000 | bytes 1048576 | tf_op jit(solution)/shard_map/pallas_call | solution.py:328
  2.8 4.0 %collective-permute-start.2 = (f32[4,128]{1,0:T(4,128)S(1)}, f32[4,128]{1,0:T(4,128)S(1)}, u32[]{:S(2)}, u32[]{:S(2)}) collective-permute-start(f32[4,128]{1,0:T(4,128)S(1)} %get-tuple-element.31), channel_id=1, source_target_pairs={{0,24},{1,25},{2,26},{3,27},{4,28},{5,29},{6,30},{7,31},{8,16},{9,... | collective-permute-start | bytes 6152 | tf_op jit(solution)/shard_map/ppermute | solution.py:357
  6.8 0.5 collective-permute-start.1
  7.4 0.9 %collective-permute-done.2 = f32[4,128]{1,0:T(4,128)S(1)} collective-permute-done((f32[4,128]{1,0:T(4,128)S(1)}, f32[4,128]{1,0:T(4,128)S(1)}, u32[]{:S(2)}, u32[]{:S(2)}) %collective-permute-start.2) | collective-permute-done | bytes 2080 | tf_op jit(solution)/shard_map/ppermute | solution.py:357
  8.3 2.0 %collective-permute-done.1 = f32[4,128]{1,0:T(4,128)S(1)} collective-permute-done((f32[4,128]{1,0:T(4,128)S(1)}, f32[4,128]{1,0:T(4,128)S(1)}, u32[]{:S(2)}, u32[]{:S(2)}) %collective-permute-start.1) | collective-permute-done | bytes 2080 | tf_op jit(solution)/shard_map/ppermute | solution.py:357
  10.9 1.2 %collective-permute-done.3 = f32[16,128]{1,0:T(8,128)S(1)} collective-permute-done((f32[16,128]{1,0:T(8,128)S(1)}, f32[16,128]{1,0:T(8,128)S(1)}, u32[]{:S(2)}, u32[]{:S(2)}) %collective-permute-start.3) | collective-permute-done | bytes 8224 | tf_op jit(solution)/shard_map/ppermute | solution.py:342
  12.1 3.7 %collective-permute-start.6 = (f32[16,128]{1,0:T(8,128)S(1)}, f32[16,128]{1,0:T(8,128)S(1)}, u32[]{:S(2)}, u32[]{:S(2)}) collective-permute-start(f32[16,128]{1,0:T(8,128)S(1)} %fusion), channel_id=1, source_target_pairs={{0,6},{1,7},{2,4},{3,5},{4,2},{5,3},{6,0},{7,1},{8,14},{9,15},{10,... | collective-permute-start | bytes 24584 | tf_op jit(solution)/shard_map/ppermute | solution.py:342
  15.8 0.8 %collective-permute-start.4 = (f32[16,128]{1,0:T(8,128)S(1)}, f32[16,128]{1,0:T(8,128)S(1)}, u32[]{:S(2)}, u32[]{:S(2)}) collective-permute-start(f32[16,128]{1,0:T(8,128)S(1)} %fusion), channel_id=1, source_target_pairs={{0,2},{1,3},{2,0},{3,1},{4,6},{5,7},{6,4},{7,5},{8,10},{9,11},{10,... | collective-permute-start | bytes 24584 | tf_op jit(solution)/shard_map/ppermute | solution.py:342
  17.0 1.7 %collective-permute-start.8 = (bf16[784,128]{1,0:T(8,128)(2,1)S(1)}, bf16[784,128]{1,0:T(8,128)(2,1)S(1)}, u32[]{:S(2)}, u32[]{:S(2)}) collective-permute-start(bf16[784,128]{1,0:T(8,128)(2,1)S(1)} %get-tuple-element.36), channel_id=1, source_target_pairs={{0,16},{1,17},{2,18},{3,19},{4,20},{5,21},{6,22},{7,23},{8,24},{9,... | collective-permute-start | bytes 602120 | tf_op jit(solution)/shard_map/ppermute | solution.py:357
  19.4 1.0 %collective-permute-done.5 = f32[16,128]{1,0:T(8,128)S(1)} collective-permute-done((f32[16,128]{1,0:T(8,128)S(1)}, f32[16,128]{1,0:T(8,128)S(1)}, u32[]{:S(2)}, u32[]{:S(2)}) %collective-permute-start.5) | collective-permute-done | bytes 8224 | tf_op jit(solution)/shard_map/ppermute | solution.py:342
  20.3 4.1 %collective-permute-done.7.refs_5_ = bf16[784,128]{1,0:T(8,128)(2,1)S(1)} collective-permute-done((bf16[784,128]{1,0:T(8,128)(2,1)S(1)}, bf16[784,128]{1,0:T(8,128)(2,1)S(1)}, u32[]{:S(2)}, u32[]{:S(2)}) %collective-permute-start.7) | collective-permute-done | bytes 200736 | tf_op jit(solution)/shard_map/ppermute | solution.py:357
  24.4 2.1 %collective-permute-done.8.refs_6_ = bf16[784,128]{1,0:T(8,128)(2,1)S(1)} collective-permute-done((bf16[784,128]{1,0:T(8,128)(2,1)S(1)}, bf16[784,128]{1,0:T(8,128)(2,1)S(1)}, u32[]{:S(2)}, u32[]{:S(2)}) %collective-permute-start.8) | collective-permute-done | bytes 200736 | tf_op jit(solution)/shard_map/ppermute | solution.py:357
  26.6 3.3 %shard_map.147 = (f32[32,4,128]{2,1,0:T(4,128)}, bf16[512,128]{1,0:T(8,128)(2,1)S(1)}, bf16[512,128]{1,0:T(8,128)(2,1)S(1)}, bf16[512,128]{1,0:T(8,128)(2,1)S(1)...) custom-call(s32[1]{0:T(128)S(6)} %copy.16.refs_0_, ...), custom_call_target="tpu_custom_call" | custom-call | flops 100000000 | bytes 1048576 | tf_op jit(solution)/shard_map/pallas_call | solution.py:328
  29.8 6.6 %all-to-all-start = ((f32[32,4,128]{2,1,0:T(4,128)}), f32[32,4,128]{2,1,0:T(4,128)S(1)}, u32[]{:S(2)}, u32[]{:S(2)}) async-start(f32[32,4,128]{2,1,0:T(4,128)} %get-tuple-element.38), calls=%async_computation | async-start | bytes 131072 | tf_op jit(solution)/shard_map/all_to_all | solution.py:401
  36.5 1.4 %shard_map.148 = (bf16[512,512]{1,0:T(8,128)(2,1)S(1)}, f32[512,512]{1,0:T(8,128)S(1)}, f32[4,128]{1,0:T(4,128)S(1)}, f32[512,128]{1,0:T(8,128)S(1)}, f32[512,128]{1,0:T(8,128)S(1)}) custom-call(f32[1,384]{1,0:T(1,128)S(1)} %get-tuple-element.32.refs_1_.refs_0_, bf16[512,128]{1,0:T(8,128)(2,1)S(1)} %get-tuple-element.39.refs_1_.refs_2_, ...), custom_call_target="tpu_custom_call" | custom-call | flops 100000000 | bytes 1048576 | tf_op jit(solution)/shard_map/pallas_call | solution.py:328
  37.9 6.0 %all-to-all-done.refs_0_ = f32[32,4,128]{2,1,0:T(4,128)S(1)} async-done(((f32[32,4,128]{2,1,0:T(4,128)}), f32[32,4,128]{2,1,0:T(4,128)S(1)}, u32[]{:S(2)}, u32[]{:S(2)}) %all-to-all-start) | async-done | bytes 65568 | tf_op jit(solution)/shard_map/all_to_all | solution.py:401
  43.9 1.8 %shard_map.149 = (f32[32,4,128]{2,1,0:T(4,128)}, bf16[384,128]{1,0:T(8,128)(2,1)S(1)}, bf16[384,128]{1,0:T(8,128)(2,1)S(1)}, bf16[384,128]{1,0:T(8,128)(2,1)S(1)}, bf16[384,128]{1,0:T(8,128)(2,1)S(1)}) custom-call(f32[32,4,128]{2,1,0:T(4,128)S(1)} %all-to-all-done.refs_0_, f32[1,384]{1,0:T(1,128)S(1)} %get-tuple-element.33.refs_2_.refs_1_, ...), custom_call_target="tpu_custom_call" | custom-call | flops 100000000 | bytes 1048576 | tf_op jit(solution)/shard_map/pallas_call | solution.py:328
  45.7 0.6 %copy-done.3 = bf16[384,128]{1,0:T(8,128)(2,1)} copy-done((bf16[384,128]{1,0:T(8,128)(2,1)}, bf16[384,128]{1,0:T(8,128)(2,1)S(1)}, u32[]{:S(2)}) %copy-start.3) | copy-done | bytes 98328
  46.3 2.7 %all-to-all-start.1 = ((f32[32,4,128]{2,1,0:T(4,128)}), f32[32,4,128]{2,1,0:T(4,128)S(1)}, u32[]{:S(2)}, u32[]{:S(2)}) async-start(f32[32,4,128]{2,1,0:T(4,128)} %get-tuple-element.52), calls=%async_computation.1 | async-start | bytes 131072 | tf_op jit(solution)/shard_map/all_to_all | solution.py:416
  49.0 1.7 %collective-permute-start.10 = (bf16[384,128]{1,0:T(8,128)(2,1)}, bf16[384,128]{1,0:T(8,128)(2,1)S(1)}, u32[]{:S(2)}, u32[]{:S(2)}) collective-permute-start(bf16[384,128]{1,0:T(8,128)(2,1)} %copy-done.3), channel_id=1, source_target_pairs={{0,8},{1,9},{2,10},{3,11},{4,12},{5,13},{6,14},{7,15},{8,0},{9,1},... | collective-permute-start | bytes 294920 | tf_op jit(solution)/shard_map/ppermute | solution.py:357
  50.7 1.5 %collective-permute-start.11 = (bf16[384,128]{1,0:T(8,128)(2,1)S(1)}, bf16[384,128]{1,0:T(8,128)(2,1)S(1)}, u32[]{:S(2)}, u32[]{:S(2)}) collective-permute-start(bf16[384,128]{1,0:T(8,128)(2,1)S(1)} %get-tuple-element.55), channel_id=1, source_target_pairs={{0,16},{1,17},{2,18},{3,19},{4,20},{5,21},{6,22},{7,23},{8,24},{9,... | collective-permute-start | bytes 294920 | tf_op jit(solution)/shard_map/ppermute | solution.py:357
  52.6 2.1 %collective-permute-done.10.refs_5_ = bf16[384,128]{1,0:T(8,128)(2,1)S(1)} collective-permute-done((bf16[384,128]{1,0:T(8,128)(2,1)}, bf16[384,128]{1,0:T(8,128)(2,1)S(1)}, u32[]{:S(2)}, u32[]{:S(2)}) %collective-permute-start.10) | collective-permute-done | bytes 98336 | tf_op jit(solution)/shard_map/ppermute | solution.py:357
  54.7 2.1 %collective-permute-done.11.refs_6_ = bf16[384,128]{1,0:T(8,128)(2,1)S(1)} collective-permute-done((bf16[384,128]{1,0:T(8,128)(2,1)S(1)}, bf16[384,128]{1,0:T(8,128)(2,1)S(1)}, u32[]{:S(2)}, u32[]{:S(2)}) %collective-permute-start.11) | collective-permute-done | bytes 98336 | tf_op jit(solution)/shard_map/ppermute | solution.py:357
  56.8 1.0 %shard_map.150 = (bf16[128,384]{1,0:T(8,128)(2,1)}, bf16[128,384]{1,0:T(8,128)(2,1)}, bf16[128,384]{1,0:T(8,128)(2,1)}, f32[384]{0:T(512)}, f32[384]{0:T(512)}) custom-call(f32[16,128]{1,0:T(8,128)S(1)} %add_add_fusion.refs_8_.refs_9_.refs_6_.refs_0_, f32[32,4,128]{2,1,0:T(4,128)S(1)} %all-to-all-done.1.refs_1_, bf16[128,384]{1,0:T(8,128)(2,1)S(1)} %copy-done, ...), custom_call_target="tpu_custom_call" | custom-call | flops 100000000 | bytes 1048576 | tf_op jit(solution)/shard_map/pallas_call | solution.py:328
  (22 shorter events, 1.6 us)
Async XLA Ops:
  1.3 25.3 %copy-start.2 = (f32[512,128]{1,0:T(8,128)S(1)}, f32[512,128]{1,0:T(8,128)}, u32[]{:S(2)}) copy-start(f32[512,128]{1,0:T(8,128)} %constant.2.clone.refs_3_) | copy-start | bytes 786436
  2.8 5.6 %collective-permute-start.2 = (f32[4,128]{1,0:T(4,128)S(1)}, f32[4,128]{1,0:T(4,128)S(1)}, u32[]{:S(2)}, u32[]{:S(2)}) collective-permute-start(f32[4,128]{1,0:T(4,128)S(1)} %get-tuple-element.31), channel_id=1, source_target_pairs={{0,24},{1,25},{2,26},{3,27},{4,28},{5,29},{6,30},{7,31},{8,16},{9,... | collective-permute-start | bytes 6152 | tf_op jit(solution)/shard_map/ppermute | solution.py:357
  6.8 3.6 %collective-permute-start.1 = (f32[4,128]{1,0:T(4,128)S(1)}, f32[4,128]{1,0:T(4,128)S(1)}, u32[]{:S(2)}, u32[]{:S(2)}) collective-permute-start(f32[4,128]{1,0:T(4,128)S(1)} %get-tuple-element.31), channel_id=1, source_target_pairs={{0,16},{1,17},{2,18},{3,19},{4,20},{5,21},{6,22},{7,23},{8,24},{9,... | collective-permute-start | bytes 6152 | tf_op jit(solution)/shard_map/ppermute | solution.py:357
  7.3 3.6 %collective-permute-start = (f32[4,128]{1,0:T(4,128)S(1)}, f32[4,128]{1,0:T(4,128)S(1)}, u32[]{:S(2)}, u32[]{:S(2)}) collective-permute-start(f32[4,128]{1,0:T(4,128)S(1)} %get-tuple-element.31), channel_id=1, source_target_pairs={{0,8},{1,9},{2,10},{3,11},{4,12},{5,13},{6,14},{7,15},{8,0},{9,1},... | collective-permute-start | bytes 6152 | tf_op jit(solution)/shard_map/ppermute | solution.py:357
  10.9 1.2 %collective-permute-start.3 = (f32[16,128]{1,0:T(8,128)S(1)}, f32[16,128]{1,0:T(8,128)S(1)}, u32[]{:S(2)}, u32[]{:S(2)}) collective-permute-start(f32[16,128]{1,0:T(8,128)S(1)} %pad_maximum_fusion), channel_id=1, source_target_pairs={{0,1},{1,0},{2,3},{3,2},{4,5},{5,4},{6,7},{7,6},{8,9},{9,8},{10,11... | collective-permute-start | bytes 24584 | tf_op jit(solution)/shard_map/ppermute | solution.py:342
  12.1 7.2 %collective-permute-start.6 = (f32[16,128]{1,0:T(8,128)S(1)}, f32[16,128]{1,0:T(8,128)S(1)}, u32[]{:S(2)}, u32[]{:S(2)}) collective-permute-start(f32[16,128]{1,0:T(8,128)S(1)} %fusion), channel_id=1, source_target_pairs={{0,6},{1,7},{2,4},{3,5},{4,2},{5,3},{6,0},{7,1},{8,14},{9,15},{10,... | collective-permute-start | bytes 24584 | tf_op jit(solution)/shard_map/ppermute | solution.py:342
  15.8 4.5 %collective-permute-start.5 = (f32[16,128]{1,0:T(8,128)S(1)}, f32[16,128]{1,0:T(8,128)S(1)}, u32[]{:S(2)}, u32[]{:S(2)}) collective-permute-start(f32[16,128]{1,0:T(8,128)S(1)} %fusion), channel_id=1, source_target_pairs={{0,4},{1,5},{2,6},{3,7},{4,0},{5,1},{6,2},{7,3},{8,12},{9,13},{10,... | collective-permute-start | bytes 24584 | tf_op jit(solution)/shard_map/ppermute | solution.py:342
  15.8 4.5 %collective-permute-start.4 = (f32[16,128]{1,0:T(8,128)S(1)}, f32[16,128]{1,0:T(8,128)S(1)}, u32[]{:S(2)}, u32[]{:S(2)}) collective-permute-start(f32[16,128]{1,0:T(8,128)S(1)} %fusion), channel_id=1, source_target_pairs={{0,2},{1,3},{2,0},{3,1},{4,6},{5,7},{6,4},{7,5},{8,10},{9,11},{10,... | collective-permute-start | bytes 24584 | tf_op jit(solution)/shard_map/ppermute | solution.py:342
  16.6 7.9 %collective-permute-start.7 = (bf16[784,128]{1,0:T(8,128)(2,1)S(1)}, bf16[784,128]{1,0:T(8,128)(2,1)S(1)}, u32[]{:S(2)}, u32[]{:S(2)}) collective-permute-start(bf16[784,128]{1,0:T(8,128)(2,1)S(1)} %get-tuple-element.35), channel_id=1, source_target_pairs={{0,8},{1,9},{2,10},{3,11},{4,12},{5,13},{6,14},{7,15},{8,0},{9,1},... | collective-permute-start | bytes 602120 | tf_op jit(solution)/shard_map/ppermute | solution.py:357
  17.0 9.6 %collective-permute-start.8 = (bf16[784,128]{1,0:T(8,128)(2,1)S(1)}, bf16[784,128]{1,0:T(8,128)(2,1)S(1)}, u32[]{:S(2)}, u32[]{:S(2)}) collective-permute-start(bf16[784,128]{1,0:T(8,128)(2,1)S(1)} %get-tuple-element.36), channel_id=1, source_target_pairs={{0,16},{1,17},{2,18},{3,19},{4,20},{5,21},{6,22},{7,23},{8,24},{9,... | collective-permute-start | bytes 602120 | tf_op jit(solution)/shard_map/ppermute | solution.py:357
  19.3 7.3 %collective-permute-start.9 = (bf16[784,128]{1,0:T(8,128)(2,1)S(1)}, bf16[784,128]{1,0:T(8,128)(2,1)S(1)}, u32[]{:S(2)}, u32[]{:S(2)}) collective-permute-start(bf16[784,128]{1,0:T(8,128)(2,1)S(1)} %get-tuple-element.37), channel_id=1, source_target_pairs={{0,1},{1,25},{2,26},{3,27},{4,5},{5,29},{6,30},{7,31},{8,16},{9,17... | collective-permute-start | bytes 602120 | tf_op jit(solution)/shard_map/ppermute | solution.py:357
  29.8 14.0 %all-to-all-start = ((f32[32,4,128]{2,1,0:T(4,128)}), f32[32,4,128]{2,1,0:T(4,128)S(1)}, u32[]{:S(2)}, u32[]{:S(2)}) async-start(f32[32,4,128]{2,1,0:T(4,128)} %get-tuple-element.38), calls=%async_computation | async-start | bytes 131072 | tf_op jit(solution)/shard_map/all_to_all | solution.py:401
  43.9 12.9 %copy-start.1 = (bf16[128,384]{1,0:T(8,128)(2,1)S(1)}, bf16[128,384]{1,0:T(8,128)(2,1)}, u32[]{:S(2)}) copy-start(bf16[128,384]{1,0:T(8,128)(2,1)} %refs_3_.4) | copy-start | bytes 294916
  45.7 0.6 %copy-start.3 = (bf16[384,128]{1,0:T(8,128)(2,1)}, bf16[384,128]{1,0:T(8,128)(2,1)S(1)}, u32[]{:S(2)}) copy-start(bf16[384,128]{1,0:T(8,128)(2,1)S(1)} %get-tuple-element.54) | copy-start | bytes 294916
  46.3 10.4 %copy-start = (bf16[128,384]{1,0:T(8,128)(2,1)S(1)}, bf16[128,384]{1,0:T(8,128)(2,1)}, u32[]{:S(2)}) copy-start(bf16[128,384]{1,0:T(8,128)(2,1)} %refs_2_.3) | copy-start | bytes 294916
  46.3 10.4 %all-to-all-start.1 = ((f32[32,4,128]{2,1,0:T(4,128)}), f32[32,4,128]{2,1,0:T(4,128)S(1)}, u32[]{:S(2)}, u32[]{:S(2)}) async-start(f32[32,4,128]{2,1,0:T(4,128)} %get-tuple-element.52), calls=%async_computation.1 | async-start | bytes 131072 | tf_op jit(solution)/shard_map/all_to_all | solution.py:416
  49.0 5.7 %collective-permute-start.10 = (bf16[384,128]{1,0:T(8,128)(2,1)}, bf16[384,128]{1,0:T(8,128)(2,1)S(1)}, u32[]{:S(2)}, u32[]{:S(2)}) collective-permute-start(bf16[384,128]{1,0:T(8,128)(2,1)} %copy-done.3), channel_id=1, source_target_pairs={{0,8},{1,9},{2,10},{3,11},{4,12},{5,13},{6,14},{7,15},{8,0},{9,1},... | collective-permute-start | bytes 294920 | tf_op jit(solution)/shard_map/ppermute | solution.py:357
  50.7 6.0 %collective-permute-start.11 = (bf16[384,128]{1,0:T(8,128)(2,1)S(1)}, bf16[384,128]{1,0:T(8,128)(2,1)S(1)}, u32[]{:S(2)}, u32[]{:S(2)}) collective-permute-start(bf16[384,128]{1,0:T(8,128)(2,1)S(1)} %get-tuple-element.55), channel_id=1, source_target_pairs={{0,16},{1,17},{2,18},{3,19},{4,20},{5,21},{6,22},{7,23},{8,24},{9,... | collective-permute-start | bytes 294920 | tf_op jit(solution)/shard_map/ppermute | solution.py:357
  52.2 4.5 %collective-permute-start.12 = (bf16[384,128]{1,0:T(8,128)(2,1)S(1)}, bf16[384,128]{1,0:T(8,128)(2,1)S(1)}, u32[]{:S(2)}, u32[]{:S(2)}) collective-permute-start(bf16[384,128]{1,0:T(8,128)(2,1)S(1)} %get-tuple-element.56), channel_id=1, source_target_pairs={{0,24},{1,0},{2,26},{3,27},{4,28},{5,4},{6,30},{7,31},{8,16},{9,17... | collective-permute-start | bytes 294920 | tf_op jit(solution)/shard_map/ppermute | solution.py:357

commit v5 on v4

--- a/solution.py
+++ b/solution.py
@@ -154,10 +154,17 @@
     angle_t = jnp.full((8, HD), 0.5 * math.pi * (picked + 0.5) / STEPS)
     coef_out = (jnp.sin(angle_t) * jnp.cos(angle_t))[0:1]
     coef_tan = (jnp.cos(angle_t) ** 2)[0:1]
+
+    def products(dist):
+        here = slice(dist * rows, (dist + 1) * rows)
+        return mm(qcat_ref[here, HD:], kcat_ref[:, 0:HD], NT), mm(qcat_ref[here, :], kcat_ref[...], NT)
+
+    later = products(0)
     for dist in range(n_ctx):
         here = slice(dist * rows, (dist + 1) * rows)
-        scores = mm(qcat_ref[here, HD:], kcat_ref[:, 0:HD], NT)
-        slopes = mm(qcat_ref[here, :], kcat_ref[...], NT)
+        scores, slopes = later
+        if dist + 1 < n_ctx:
+            later = products(dist + 1)
         peak = jnp.max(scores, axis=1, keepdims=True)
         weights = jnp.exp((scores - peak) * inv_root)
         totals = jnp.sum(weights, axis=1, keepdims=True)

time: 58 us -> 57.6 us (level)
  no operation moved by 1% of the time
where the time goes in v5:
time: 57.6 us; the launch traced here: 57.3 us
  starting transfers between devices  24.2 us (42%)
  waiting for transfers between devices  22 us (38%)
  Pallas kernels  8.43 us (15%)
  between operations  2.03 us (4%)
  local copies, waits for them, and re-layouts  0.65 us (1%)
    ppermute x9, waiting for transfers between devices, from_peers(): out[dist] = lax.ppermute(blocks[dist], BOTH, route)  13.8 us
    ppermute x9, starting transfers between devices, from_peers(): out[dist] = lax.ppermute(blocks[dist], BOTH, route)  10.3 us
    pallas_call x5, Pallas kernels, kernel(): pl.pallas_call(body, out_shape=[jax.ShapeDtypeStruct(*o) for o in outs],...  8.43 us
    all_to_all x1, starting transfers between devices, per_device(): energy = lax.all_to_all(energy_out, BOTH, 0, 0)  6.65 us
    all_to_all x1, waiting for transfers between devices, per_device(): energy = lax.all_to_all(energy_out, BOTH, 0, 0)  6.03 us
    ppermute x4, starting transfers between devices, swap(): lax.ppermute(block, axis, [(i, i ^ dist) for i in range(lax.axis_size(axi...  4.52 us
    all_to_all x1, starting transfers between devices, per_device(): crosses = lax.all_to_all(cross_out, BOTH, 0, 0)  2.7 us
    ppermute x4, waiting for transfers between devices, swap(): lax.ppermute(block, axis, [(i, i ^ dist) for i in range(lax.axis_size(axi...  2.14 us
  transfers between devices with their start and end apart: 15, of which 10 were waited for; matrix products, arithmetic and copies ran while one was open for 0% of the time, Pallas kernels for 2%

profile of v5, /device:TPU:0, one launch (start us, length us, event | category | flops | bytes accessed | tf_op | source)
XLA Modules:
  0.0 57.3 jit_solution(650416138879829285)
XLA Ops:
  1.3 1.5 %shard_map.146 = (f32[4,128]{1,0:T(4,128)S(1)}, f32[1,384]{1,0:T(1,128)S(1)}, f32[1,384]{1,0:T(1,128)S(1)}, bf16[784,128]{1,0:T(8,128)(2,1)S(1)}, bf16[784,128]{...) custom-call(s32[1]{0:T(128)S(6)} %copy.17.refs_0_, f32[384]{0:T(512)} %refs_1_.1, ...), custom_call_target="tpu_custom_call" | custom-call | flops 100000000 | bytes 1048576 | tf_op jit(solution)/shard_map/pallas_call | solution.py:335
  2.8 4.0 %collective-permute-start.2 = (f32[4,128]{1,0:T(4,128)S(1)}, f32[4,128]{1,0:T(4,128)S(1)}, u32[]{:S(2)}, u32[]{:S(2)}) collective-permute-start(f32[4,128]{1,0:T(4,128)S(1)} %get-tuple-element.31), channel_id=1, source_target_pairs={{0,24},{1,25},{2,26},{3,27},{4,28},{5,29},{6,30},{7,31},{8,16},{9,... | collective-permute-start | bytes 6152 | tf_op jit(solution)/shard_map/ppermute | solution.py:364
  6.8 0.5 collective-permute-start.1
  7.4 0.9 %collective-permute-done.2 = f32[4,128]{1,0:T(4,128)S(1)} collective-permute-done((f32[4,128]{1,0:T(4,128)S(1)}, f32[4,128]{1,0:T(4,128)S(1)}, u32[]{:S(2)}, u32[]{:S(2)}) %collective-permute-start.2) | collective-permute-done | bytes 2080 | tf_op jit(solution)/shard_map/ppermute | solution.py:364
  8.3 2.0 %collective-permute-done.1 = f32[4,128]{1,0:T(4,128)S(1)} collective-permute-done((f32[4,128]{1,0:T(4,128)S(1)}, f32[4,128]{1,0:T(4,128)S(1)}, u32[]{:S(2)}, u32[]{:S(2)}) %collective-permute-start.1) | collective-permute-done | bytes 2080 | tf_op jit(solution)/shard_map/ppermute | solution.py:364
  10.9 1.2 %collective-permute-done.3 = f32[16,128]{1,0:T(8,128)S(1)} collective-permute-done((f32[16,128]{1,0:T(8,128)S(1)}, f32[16,128]{1,0:T(8,128)S(1)}, u32[]{:S(2)}, u32[]{:S(2)}) %collective-permute-start.3) | collective-permute-done | bytes 8224 | tf_op jit(solution)/shard_map/ppermute | solution.py:349
  12.1 3.7 %collective-permute-start.6 = (f32[16,128]{1,0:T(8,128)S(1)}, f32[16,128]{1,0:T(8,128)S(1)}, u32[]{:S(2)}, u32[]{:S(2)}) collective-permute-start(f32[16,128]{1,0:T(8,128)S(1)} %fusion), channel_id=1, source_target_pairs={{0,6},{1,7},{2,4},{3,5},{4,2},{5,3},{6,0},{7,1},{8,14},{9,15},{10,... | collective-permute-start | bytes 24584 | tf_op jit(solution)/shard_map/ppermute | solution.py:349
  15.8 0.8 %collective-permute-start.4 = (f32[16,128]{1,0:T(8,128)S(1)}, f32[16,128]{1,0:T(8,128)S(1)}, u32[]{:S(2)}, u32[]{:S(2)}) collective-permute-start(f32[16,128]{1,0:T(8,128)S(1)} %fusion), channel_id=1, source_target_pairs={{0,2},{1,3},{2,0},{3,1},{4,6},{5,7},{6,4},{7,5},{8,10},{9,11},{10,... | collective-permute-start | bytes 24584 | tf_op jit(solution)/shard_map/ppermute | solution.py:349
  17.0 1.7 %collective-permute-start.8 = (bf16[784,128]{1,0:T(8,128)(2,1)S(1)}, bf16[784,128]{1,0:T(8,128)(2,1)S(1)}, u32[]{:S(2)}, u32[]{:S(2)}) collective-permute-start(bf16[784,128]{1,0:T(8,128)(2,1)S(1)} %get-tuple-element.36), channel_id=1, source_target_pairs={{0,16},{1,17},{2,18},{3,19},{4,20},{5,21},{6,22},{7,23},{8,24},{9,... | collective-permute-start | bytes 602120 | tf_op jit(solution)/shard_map/ppermute | solution.py:364
  19.4 1.0 %collective-permute-done.5 = f32[16,128]{1,0:T(8,128)S(1)} collective-permute-done((f32[16,128]{1,0:T(8,128)S(1)}, f32[16,128]{1,0:T(8,128)S(1)}, u32[]{:S(2)}, u32[]{:S(2)}) %collective-permute-start.5) | collective-permute-done | bytes 8224 | tf_op jit(solution)/shard_map/ppermute | solution.py:349
  20.3 4.1 %collective-permute-done.7.refs_5_ = bf16[784,128]{1,0:T(8,128)(2,1)S(1)} collective-permute-done((bf16[784,128]{1,0:T(8,128)(2,1)S(1)}, bf16[784,128]{1,0:T(8,128)(2,1)S(1)}, u32[]{:S(2)}, u32[]{:S(2)}) %collective-permute-start.7) | collective-permute-done | bytes 200736 | tf_op jit(solution)/shard_map/ppermute | solution.py:364
  24.4 2.1 %collective-permute-done.8.refs_6_ = bf16[784,128]{1,0:T(8,128)(2,1)S(1)} collective-permute-done((bf16[784,128]{1,0:T(8,128)(2,1)S(1)}, bf16[784,128]{1,0:T(8,128)(2,1)S(1)}, u32[]{:S(2)}, u32[]{:S(2)}) %collective-permute-start.8) | collective-permute-done | bytes 200736 | tf_op jit(solution)/shard_map/ppermute | solution.py:364
  26.6 2.8 %shard_map.147 = (f32[32,4,128]{2,1,0:T(4,128)}, bf16[512,128]{1,0:T(8,128)(2,1)S(1)}, bf16[512,128]{1,0:T(8,128)(2,1)S(1)}, bf16[512,128]{1,0:T(8,128)(2,1)S(1)...) custom-call(s32[1]{0:T(128)S(6)} %copy.16.refs_0_, ...), custom_call_target="tpu_custom_call" | custom-call | flops 100000000 | bytes 1048576 | tf_op jit(solution)/shard_map/pallas_call | solution.py:335
  29.4 6.6 %all-to-all-start = ((f32[32,4,128]{2,1,0:T(4,128)}), f32[32,4,128]{2,1,0:T(4,128)S(1)}, u32[]{:S(2)}, u32[]{:S(2)}) async-start(f32[32,4,128]{2,1,0:T(4,128)} %get-tuple-element.38), calls=%async_computation | async-start | bytes 131072 | tf_op jit(solution)/shard_map/all_to_all | solution.py:408
  36.1 1.3 %shard_map.148 = (bf16[512,512]{1,0:T(8,128)(2,1)S(1)}, f32[512,512]{1,0:T(8,128)S(1)}, f32[4,128]{1,0:T(4,128)S(1)}, f32[512,128]{1,0:T(8,128)S(1)}, f32[512,128]{1,0:T(8,128)S(1)}) custom-call(f32[1,384]{1,0:T(1,128)S(1)} %get-tuple-element.32.refs_1_.refs_0_, bf16[512,128]{1,0:T(8,128)(2,1)S(1)} %get-tuple-element.39.refs_1_.refs_2_, ...), custom_call_target="tpu_custom_call" | custom-call | flops 100000000 | bytes 1048576 | tf_op jit(solution)/shard_map/pallas_call | solution.py:335
  37.4 6.0 %all-to-all-done.refs_0_ = f32[32,4,128]{2,1,0:T(4,128)S(1)} async-done(((f32[32,4,128]{2,1,0:T(4,128)}), f32[32,4,128]{2,1,0:T(4,128)S(1)}, u32[]{:S(2)}, u32[]{:S(2)}) %all-to-all-start) | async-done | bytes 65568 | tf_op jit(solution)/shard_map/all_to_all | solution.py:408
  43.4 1.8 %shard_map.149 = (f32[32,4,128]{2,1,0:T(4,128)}, bf16[384,128]{1,0:T(8,128)(2,1)S(1)}, bf16[384,128]{1,0:T(8,128)(2,1)S(1)}, bf16[384,128]{1,0:T(8,128)(2,1)S(1)}, bf16[384,128]{1,0:T(8,128)(2,1)S(1)}) custom-call(f32[32,4,128]{2,1,0:T(4,128)S(1)} %all-to-all-done.refs_0_, f32[1,384]{1,0:T(1,128)S(1)} %get-tuple-element.33.refs_2_.refs_1_, ...), custom_call_target="tpu_custom_call" | custom-call | flops 100000000 | bytes 1048576 | tf_op jit(solution)/shard_map/pallas_call | solution.py:335
  45.2 0.6 %copy-done.3 = bf16[384,128]{1,0:T(8,128)(2,1)} copy-done((bf16[384,128]{1,0:T(8,128)(2,1)}, bf16[384,128]{1,0:T(8,128)(2,1)S(1)}, u32[]{:S(2)}) %copy-start.3) | copy-done | bytes 98328
  45.9 2.7 %all-to-all-start.1 = ((f32[32,4,128]{2,1,0:T(4,128)}), f32[32,4,128]{2,1,0:T(4,128)S(1)}, u32[]{:S(2)}, u32[]{:S(2)}) async-start(f32[32,4,128]{2,1,0:T(4,128)} %get-tuple-element.52), calls=%async_computation.1 | async-start | bytes 131072 | tf_op jit(solution)/shard_map/all_to_all | solution.py:423
  48.6 1.7 %collective-permute-start.10 = (bf16[384,128]{1,0:T(8,128)(2,1)}, bf16[384,128]{1,0:T(8,128)(2,1)S(1)}, u32[]{:S(2)}, u32[]{:S(2)}) collective-permute-start(bf16[384,128]{1,0:T(8,128)(2,1)} %copy-done.3), channel_id=1, source_target_pairs={{0,8},{1,9},{2,10},{3,11},{4,12},{5,13},{6,14},{7,15},{8,0},{9,1},... | collective-permute-start | bytes 294920 | tf_op jit(solution)/shard_map/ppermute | solution.py:364
  50.3 1.5 %collective-permute-start.11 = (bf16[384,128]{1,0:T(8,128)(2,1)S(1)}, bf16[384,128]{1,0:T(8,128)(2,1)S(1)}, u32[]{:S(2)}, u32[]{:S(2)}) collective-permute-start(bf16[384,128]{1,0:T(8,128)(2,1)S(1)} %get-tuple-element.55), channel_id=1, source_target_pairs={{0,16},{1,17},{2,18},{3,19},{4,20},{5,21},{6,22},{7,23},{8,24},{9,... | collective-permute-start | bytes 294920 | tf_op jit(solution)/shard_map/ppermute | solution.py:364
  52.1 2.1 %collective-permute-done.10.refs_5_ = bf16[384,128]{1,0:T(8,128)(2,1)S(1)} collective-permute-done((bf16[384,128]{1,0:T(8,128)(2,1)}, bf16[384,128]{1,0:T(8,128)(2,1)S(1)}, u32[]{:S(2)}, u32[]{:S(2)}) %collective-permute-start.10) | collective-permute-done | bytes 98336 | tf_op jit(solution)/shard_map/ppermute | solution.py:364
  54.2 2.1 %collective-permute-done.11.refs_6_ = bf16[384,128]{1,0:T(8,128)(2,1)S(1)} collective-permute-done((bf16[384,128]{1,0:T(8,128)(2,1)S(1)}, bf16[384,128]{1,0:T(8,128)(2,1)S(1)}, u32[]{:S(2)}, u32[]{:S(2)}) %collective-permute-start.11) | collective-permute-done | bytes 98336 | tf_op jit(solution)/shard_map/ppermute | solution.py:364
  56.3 1.0 %shard_map.150 = (bf16[128,384]{1,0:T(8,128)(2,1)}, bf16[128,384]{1,0:T(8,128)(2,1)}, bf16[128,384]{1,0:T(8,128)(2,1)}, f32[384]{0:T(512)}, f32[384]{0:T(512)}) custom-call(f32[16,128]{1,0:T(8,128)S(1)} %add_add_fusion.refs_8_.refs_9_.refs_6_.refs_0_, f32[32,4,128]{2,1,0:T(4,128)S(1)} %all-to-all-done.1.refs_1_, bf16[128,384]{1,0:T(8,128)(2,1)S(1)} %copy-done, ...), custom_call_target="tpu_custom_call" | custom-call | flops 100000000 | bytes 1048576 | tf_op jit(solution)/shard_map/pallas_call | solution.py:335
  (22 shorter events, 1.6 us)
Async XLA Ops:
  1.3 25.3 %copy-start.2 = (f32[512,128]{1,0:T(8,128)S(1)}, f32[512,128]{1,0:T(8,128)}, u32[]{:S(2)}) copy-start(f32[512,128]{1,0:T(8,128)} %constant.2.clone.refs_3_) | copy-start | bytes 786436
  2.8 5.6 %collective-permute-start.2 = (f32[4,128]{1,0:T(4,128)S(1)}, f32[4,128]{1,0:T(4,128)S(1)}, u32[]{:S(2)}, u32[]{:S(2)}) collective-permute-start(f32[4,128]{1,0:T(4,128)S(1)} %get-tuple-element.31), channel_id=1, source_target_pairs={{0,24},{1,25},{2,26},{3,27},{4,28},{5,29},{6,30},{7,31},{8,16},{9,... | collective-permute-start | bytes 6152 | tf_op jit(solution)/shard_map/ppermute | solution.py:364
  6.8 3.6 %collective-permute-start.1 = (f32[4,128]{1,0:T(4,128)S(1)}, f32[4,128]{1,0:T(4,128)S(1)}, u32[]{:S(2)}, u32[]{:S(2)}) collective-permute-start(f32[4,128]{1,0:T(4,128)S(1)} %get-tuple-element.31), channel_id=1, source_target_pairs={{0,16},{1,17},{2,18},{3,19},{4,20},{5,21},{6,22},{7,23},{8,24},{9,... | collective-permute-start | bytes 6152 | tf_op jit(solution)/shard_map/ppermute | solution.py:364
  7.3 3.6 %collective-permute-start = (f32[4,128]{1,0:T(4,128)S(1)}, f32[4,128]{1,0:T(4,128)S(1)}, u32[]{:S(2)}, u32[]{:S(2)}) collective-permute-start(f32[4,128]{1,0:T(4,128)S(1)} %get-tuple-element.31), channel_id=1, source_target_pairs={{0,8},{1,9},{2,10},{3,11},{4,12},{5,13},{6,14},{7,15},{8,0},{9,1},... | collective-permute-start | bytes 6152 | tf_op jit(solution)/shard_map/ppermute | solution.py:364
  10.9 1.2 %collective-permute-start.3 = (f32[16,128]{1,0:T(8,128)S(1)}, f32[16,128]{1,0:T(8,128)S(1)}, u32[]{:S(2)}, u32[]{:S(2)}) collective-permute-start(f32[16,128]{1,0:T(8,128)S(1)} %pad_maximum_fusion), channel_id=1, source_target_pairs={{0,1},{1,0},{2,3},{3,2},{4,5},{5,4},{6,7},{7,6},{8,9},{9,8},{10,11... | collective-permute-start | bytes 24584 | tf_op jit(solution)/shard_map/ppermute | solution.py:349
  12.1 7.2 %collective-permute-start.6 = (f32[16,128]{1,0:T(8,128)S(1)}, f32[16,128]{1,0:T(8,128)S(1)}, u32[]{:S(2)}, u32[]{:S(2)}) collective-permute-start(f32[16,128]{1,0:T(8,128)S(1)} %fusion), channel_id=1, source_target_pairs={{0,6},{1,7},{2,4},{3,5},{4,2},{5,3},{6,0},{7,1},{8,14},{9,15},{10,... | collective-permute-start | bytes 24584 | tf_op jit(solution)/shard_map/ppermute | solution.py:349
  15.8 4.5 %collective-permute-start.5 = (f32[16,128]{1,0:T(8,128)S(1)}, f32[16,128]{1,0:T(8,128)S(1)}, u32[]{:S(2)}, u32[]{:S(2)}) collective-permute-start(f32[16,128]{1,0:T(8,128)S(1)} %fusion), channel_id=1, source_target_pairs={{0,4},{1,5},{2,6},{3,7},{4,0},{5,1},{6,2},{7,3},{8,12},{9,13},{10,... | collective-permute-start | bytes 24584 | tf_op jit(solution)/shard_map/ppermute | solution.py:349
  15.8 4.5 %collective-permute-start.4 = (f32[16,128]{1,0:T(8,128)S(1)}, f32[16,128]{1,0:T(8,128)S(1)}, u32[]{:S(2)}, u32[]{:S(2)}) collective-permute-start(f32[16,128]{1,0:T(8,128)S(1)} %fusion), channel_id=1, source_target_pairs={{0,2},{1,3},{2,0},{3,1},{4,6},{5,7},{6,4},{7,5},{8,10},{9,11},{10,... | collective-permute-start | bytes 24584 | tf_op jit(solution)/shard_map/ppermute | solution.py:349
  16.6 7.9 %collective-permute-start.7 = (bf16[784,128]{1,0:T(8,128)(2,1)S(1)}, bf16[784,128]{1,0:T(8,128)(2,1)S(1)}, u32[]{:S(2)}, u32[]{:S(2)}) collective-permute-start(bf16[784,128]{1,0:T(8,128)(2,1)S(1)} %get-tuple-element.35), channel_id=1, source_target_pairs={{0,8},{1,9},{2,10},{3,11},{4,12},{5,13},{6,14},{7,15},{8,0},{9,1},... | collective-permute-start | bytes 602120 | tf_op jit(solution)/shard_map/ppermute | solution.py:364
  17.0 9.6 %collective-permute-start.8 = (bf16[784,128]{1,0:T(8,128)(2,1)S(1)}, bf16[784,128]{1,0:T(8,128)(2,1)S(1)}, u32[]{:S(2)}, u32[]{:S(2)}) collective-permute-start(bf16[784,128]{1,0:T(8,128)(2,1)S(1)} %get-tuple-element.36), channel_id=1, source_target_pairs={{0,16},{1,17},{2,18},{3,19},{4,20},{5,21},{6,22},{7,23},{8,24},{9,... | collective-permute-start | bytes 602120 | tf_op jit(solution)/shard_map/ppermute | solution.py:364
  19.3 7.3 %collective-permute-start.9 = (bf16[784,128]{1,0:T(8,128)(2,1)S(1)}, bf16[784,128]{1,0:T(8,128)(2,1)S(1)}, u32[]{:S(2)}, u32[]{:S(2)}) collective-permute-start(bf16[784,128]{1,0:T(8,128)(2,1)S(1)} %get-tuple-element.37), channel_id=1, source_target_pairs={{0,1},{1,25},{2,26},{3,27},{4,5},{5,29},{6,30},{7,31},{8,16},{9,17... | collective-permute-start | bytes 602120 | tf_op jit(solution)/shard_map/ppermute | solution.py:364
  29.4 14.0 %all-to-all-start = ((f32[32,4,128]{2,1,0:T(4,128)}), f32[32,4,128]{2,1,0:T(4,128)S(1)}, u32[]{:S(2)}, u32[]{:S(2)}) async-start(f32[32,4,128]{2,1,0:T(4,128)} %get-tuple-element.38), calls=%async_computation | async-start | bytes 131072 | tf_op jit(solution)/shard_map/all_to_all | solution.py:408
  43.4 12.9 %copy-start.1 = (bf16[128,384]{1,0:T(8,128)(2,1)S(1)}, bf16[128,384]{1,0:T(8,128)(2,1)}, u32[]{:S(2)}) copy-start(bf16[128,384]{1,0:T(8,128)(2,1)} %refs_3_.4) | copy-start | bytes 294916
  45.2 0.6 %copy-start.3 = (bf16[384,128]{1,0:T(8,128)(2,1)}, bf16[384,128]{1,0:T(8,128)(2,1)S(1)}, u32[]{:S(2)}) copy-start(bf16[384,128]{1,0:T(8,128)(2,1)S(1)} %get-tuple-element.54) | copy-start | bytes 294916
  45.9 10.4 %copy-start = (bf16[128,384]{1,0:T(8,128)(2,1)S(1)}, bf16[128,384]{1,0:T(8,128)(2,1)}, u32[]{:S(2)}) copy-start(bf16[128,384]{1,0:T(8,128)(2,1)} %refs_2_.3) | copy-start | bytes 294916
  45.9 10.4 %all-to-all-start.1 = ((f32[32,4,128]{2,1,0:T(4,128)}), f32[32,4,128]{2,1,0:T(4,128)S(1)}, u32[]{:S(2)}, u32[]{:S(2)}) async-start(f32[32,4,128]{2,1,0:T(4,128)} %get-tuple-element.52), calls=%async_computation.1 | async-start | bytes 131072 | tf_op jit(solution)/shard_map/all_to_all | solution.py:423
  48.6 5.7 %collective-permute-start.10 = (bf16[384,128]{1,0:T(8,128)(2,1)}, bf16[384,128]{1,0:T(8,128)(2,1)S(1)}, u32[]{:S(2)}, u32[]{:S(2)}) collective-permute-start(bf16[384,128]{1,0:T(8,128)(2,1)} %copy-done.3), channel_id=1, source_target_pairs={{0,8},{1,9},{2,10},{3,11},{4,12},{5,13},{6,14},{7,15},{8,0},{9,1},... | collective-permute-start | bytes 294920 | tf_op jit(solution)/shard_map/ppermute | solution.py:364
  50.3 6.0 %collective-permute-start.11 = (bf16[384,128]{1,0:T(8,128)(2,1)S(1)}, bf16[384,128]{1,0:T(8,128)(2,1)S(1)}, u32[]{:S(2)}, u32[]{:S(2)}) collective-permute-start(bf16[384,128]{1,0:T(8,128)(2,1)S(1)} %get-tuple-element.55), channel_id=1, source_target_pairs={{0,16},{1,17},{2,18},{3,19},{4,20},{5,21},{6,22},{7,23},{8,24},{9,... | collective-permute-start | bytes 294920 | tf_op jit(solution)/shard_map/ppermute | solution.py:364
  51.8 4.5 %collective-permute-start.12 = (bf16[384,128]{1,0:T(8,128)(2,1)S(1)}, bf16[384,128]{1,0:T(8,128)(2,1)S(1)}, u32[]{:S(2)}, u32[]{:S(2)}) collective-permute-start(bf16[384,128]{1,0:T(8,128)(2,1)S(1)} %get-tuple-element.56), channel_id=1, source_target_pairs={{0,24},{1,0},{2,26},{3,27},{4,28},{5,4},{6,30},{7,31},{8,16},{9,17... | collective-permute-start | bytes 294920 | tf_op jit(solution)/shard_map/ppermute | solution.py:364
